TPU v7x, 32 devices: a whole 2x2x4 slice. The times are simulated.
32 devices in a mesh: depth: 16 (over z, y, x), chan: 2 (over core).
Axes of the slice: x: 2, y: 2, z: 4, core: 2. Of those that a mesh axis runs over, the one named last changes fastest.
Arguments:
- feats: bfloat16 [32, 32, 8, 128], P('chan', 'depth'), may hold values from -6 to 6
- weight_one: bfloat16 [32, 32, 27], replicated, may hold values from -0.21875 to 0.21875
- weight_two: bfloat16 [64, 32, 27], replicated, may hold values from -0.21875 to 0.21875
- cotangent: bfloat16 [64, 16, 4, 64], P('chan', 'depth'), may hold values from -6 to 6
Outputs:
- grad_feats: bfloat16 [32, 32, 8, 128], P('chan', 'depth')
- grad_weight_one: float32 [32, 32, 27], P(None, 'chan')
- grad_weight_two: float32 [64, 32, 27], P(None, 'chan')
All inputs are finite; a program needn't handle non-finite values.
Results may differ from a plain program's by a relative error of at most 0.013.
Values may be sent and summed in bfloat16 or wider, within the bound.
No kernel may reach another device: no remote copies, remote signals or barrier semaphores. Data moves between devices by JAX's collectives and lax.ppermute only.
A program may use at most 128 MiB of HBM per device.

v0:
```python
import jax
import jax.numpy as jnp
from jax import lax
from jax.sharding import PartitionSpec as P

OFFSETS = [
    (first, second, third) for first in range(3) for second in range(3) for third in range(3)
]


def padded_2(block, sides, width):
    for axis, dim in sides:
        count = lax.axis_size(axis)
        forward = [(i, i + 1) for i in range(count - 1)]
        backward = [(target, source) for source, target in forward]
        low = lax.ppermute(
            lax.slice_in_dim(block, block.shape[dim] - width, None, axis=dim), axis, forward
        )
        high = lax.ppermute(lax.slice_in_dim(block, 0, width, axis=dim), axis, backward)
        block = jnp.concatenate([low, block, high], axis=dim)
    return block


def pad_plane(haloed):
    return jnp.pad(haloed, ((0, 0), (0, 0), (1, 1), (1, 1)))


def cut_edges(haloed, lower_keep, upper_keep):
    count = haloed.shape[1]
    position = lax.iota(jnp.int32, count)
    keep = jnp.where(position == 0, lower_keep, jnp.where(position == count - 1, upper_keep, True))
    return jnp.where(keep[None, :, None, None], haloed, jnp.zeros((), haloed.dtype))


def patch_rows(haloed):
    chans = haloed.shape[0]
    planes = haloed.shape[1] - 2
    height = haloed.shape[2]
    across = haloed.shape[3]
    padded = pad_plane(haloed)
    windows = [
        padded[:, first : first + planes, second : second + height, third : third + across]
        for first, second, third in OFFSETS
    ]
    return jnp.stack(windows, 0).reshape(27 * chans, planes * height * across)


def flat_weight(own):
    return jnp.transpose(own, (0, 2, 1)).reshape(own.shape[0], -1)


def flat_transposed(own):
    return jnp.transpose(own, (2, 1, 0)).reshape(-1, own.shape[0])


def weight_layout(weight_sum, chans):
    return jnp.transpose(weight_sum.reshape(weight_sum.shape[0], 27, chans), (0, 2, 1))


def slope(pre):
    sig = jax.nn.sigmoid(pre)
    return sig * (1.0 + pre * (1.0 - sig))


def grad_fold(transposed, patches, piece):
    count = piece.shape[0]
    padded = pad_plane(piece).reshape(count, -1)
    image_sum = jnp.dot(transposed, padded, preferred_element_type=jnp.float32)
    inner = piece[:, 1:-1].reshape(count, -1)
    rows_part = lax.dot_general(
        inner, patches, (((1,), (1,)), ((), ())), preferred_element_type=jnp.float32
    )
    return (image_sum, rows_part)


def shift_sum(image_sum, chans, planes, height, across):
    shaped = image_sum.reshape(27, chans, planes + 2, height + 2, across + 2)
    total = jnp.zeros((chans, planes, height, across), jnp.float32)
    for index, (first, second, third) in enumerate(OFFSETS):
        total = (
            total
            + shaped[
                index,
                :,
                2 - first : 2 - first + planes,
                2 - second : 2 - second + height,
                2 - third : 2 - third + across,
            ]
        )
    return total


def shards(feats, weight_one, weight_two, cotangent):
    groups = lax.axis_size("chan")
    member = lax.axis_index("chan")
    slabs = lax.axis_size("depth")
    place = lax.axis_index("depth")
    lower_keep = place % slabs != 0
    upper_keep = (place + 1) % slabs != 0
    in_chans, planes, height, across = feats.shape
    mid_chans = weight_one.shape[0] // groups
    out_chans = weight_two.shape[0] // groups
    feats_halo = cut_edges(padded_2(feats, (("depth", 1),), 1), lower_keep, upper_keep)
    patches_one = patch_rows(feats_halo)
    own_one = lax.dynamic_slice_in_dim(weight_one, member * in_chans, in_chans, 1)
    partial_one = jnp.dot(flat_weight(own_one), patches_one, preferred_element_type=jnp.float32)
    pre_one = lax.psum_scatter(
        partial_one.astype(jnp.bfloat16), "chan", scatter_dimension=0, tiled=True
    ).astype(jnp.float32)
    act_one = jax.nn.silu(pre_one).astype(jnp.bfloat16).reshape(mid_chans, planes, height, across)
    pooled = (
        act_one.astype(jnp.float32)
        .reshape(mid_chans, planes // 2, 2, height // 2, 2, across // 2, 2)
        .mean(axis=(2, 4, 6))
        .astype(jnp.bfloat16)
    )
    pooled_halo = cut_edges(padded_2(pooled, (("depth", 1),), 1), lower_keep, upper_keep)
    patches_two = patch_rows(pooled_halo)
    own_two = lax.dynamic_slice_in_dim(weight_two, member * mid_chans, mid_chans, 1)
    partial_two = jnp.dot(flat_weight(own_two), patches_two, preferred_element_type=jnp.float32)
    pre_two = lax.psum_scatter(
        partial_two.astype(jnp.bfloat16), "chan", scatter_dimension=0, tiled=True
    ).astype(jnp.float32)
    grad_two = (cotangent.astype(jnp.float32).reshape(out_chans, -1) * slope(pre_two)).astype(
        jnp.bfloat16
    )
    grad_two = grad_two.reshape(out_chans, planes // 2, height // 2, across // 2)
    grad_two_halo = cut_edges(padded_2(grad_two, (("depth", 1),), 1), lower_keep, upper_keep)
    image_two, wsum_two = grad_fold(
        flat_transposed(own_two),
        patches_two,
        lax.all_gather(grad_two_halo, "chan", axis=0, tiled=True),
    )
    grad_weight_two = weight_layout(wsum_two, mid_chans)
    grad_weight_two = lax.psum(grad_weight_two, "depth")
    back_pooled = shift_sum(image_two, mid_chans, planes // 2, height // 2, across // 2)
    spread = (
        jnp.broadcast_to(
            back_pooled[:, :, None, :, None, :, None],
            (mid_chans, planes // 2, 2, height // 2, 2, across // 2, 2),
        ).reshape(mid_chans, -1)
        * 0.125
    )
    grad_one = (
        (spread * slope(pre_one)).astype(jnp.bfloat16).reshape(mid_chans, planes, height, across)
    )
    grad_one_halo = cut_edges(padded_2(grad_one, (("depth", 1),), 1), lower_keep, upper_keep)
    image_one, wsum_one = grad_fold(
        flat_transposed(own_one),
        patches_one,
        lax.all_gather(grad_one_halo, "chan", axis=0, tiled=True),
    )
    grad_weight_one = weight_layout(wsum_one, in_chans)
    grad_weight_one = lax.psum(grad_weight_one, "depth")
    grad_feats = shift_sum(image_one, in_chans, planes, height, across).astype(jnp.bfloat16)
    return (grad_feats, grad_weight_one, grad_weight_two)


def solution(mesh):
    return jax.shard_map(
        shards,
        mesh=mesh,
        in_specs=(P("chan", "depth", None, None), P(), P(), P("chan", "depth", None, None)),
        out_specs=(P("chan", "depth", None, None), P(None, "chan", None), P(None, "chan", None)),
        check_vma=False,
    )
```

profile of v0, /device:TPU:0, one launch (start us, length us, event | category | flops | bytes accessed | tf_op | source)
XLA Modules:
  0.0 237.0 jit_solution(2081670601970649039)
XLA Ops:
  8.2 4.9 %collective-permute-start = (bf16[16,1,8,128]{3,0,2,1:T(8,128)(2,1)S(1)}, bf16[16,1,8,128]{3,0,2,1:T(8,128)(2,1)S(1)}, u32[]{:S(2)}, u32[]{:S(2)}) collective-permute-start(bf16[16,1,8,128]{3,0,2,1:T(8,128)(2,1)S(1)} %get-tuple-element.146), channel_id=1, source_target_pairs={{0,2},{2,4},{4,6},{6,8},{8,10},{10,12},{12,14},{14,16},{16,18},{18... | collective-permute-start | bytes 98312 | tf_op jit(solution)/shard_map/ppermute | solution.py:16
  13.0 1.3 collective-permute-start.1
  14.4 1.1 constant_dynamic-slice_fusion.1
  15.6 3.2 %collective-permute-done.1 = bf16[16,1,8,128]{3,0,2,1:T(8,128)(2,1)S(1)} collective-permute-done((bf16[16,1,8,128]{3,0,2,1:T(8,128)(2,1)S(1)}, bf16[16,1,8,128]{3,0,2,1:T(8,128)(2,1)S(1)}, u32[]{:S(2)}, u32[]{:S(2)}) %collective-permute-start.1) | collective-permute-done | bytes 32800 | tf_op jit(solution)/shard_map/ppermute | solution.py:19
  34.7 10.8 %stack.195 = bf16[27,16,2,8,128]{4,0,3,1,2:T(8,128)(2,1)S(1)} concatenate(bf16[1,16,2,8,128]{4,0,3,1,2:T(2,128)(2,1)S(1)} %copy.2026, bf16[1,16,2,8,128]{4,0,3,1,2:T(2,128)(2,1)} %copy.2027, bf16[1,16,2,8,128]{4,0,3,1,2:T(2,128)(2,1)} %copy.2028, bf16[1,16,2,8,128]{4,0,3,1,2:T(2,128)(2,1)} %copy.2029, bf16[1,16,2,8,128]{4,0,3,1,2:T(2,128)(2,1)S(1)} %copy.2030, ...), dimensions={0} | concatenate | bytes 3538944 | tf_op jit(solution)/shard_map/stack | solution.py:45
  45.5 1.9 copy.2053
  47.4 3.8 %reshape.339 = bf16[432,2048]{1,0:T(8,128)(2,1)} reshape(bf16[27,16,2,8,128]{4,3,2,1,0:T(8,128)(2,1)} %copy.2053) | data formatting | bytes 3538944 | tf_op jit(solution)/shard_map/reshape | solution.py:45
  51.2 2.6 %convolution_convert_fusion = bf16[32,2048]{1,0:T(8,128)(2,1)} fusion(bf16[32,432]{0,1:T(8,128)(2,1)S(1)} %bitcast.368, bf16[432,2048]{1,0:T(8,128)(2,1)} %reshape.339), kind=kOutput, calls=%fused_computation | convolution fusion | flops 56688640 | bytes 1928192 | tf_op jit(solution)/shard_map/dot_general | solution.py:106
  53.9 9.7 %reduce-scatter.3.cloned.1.call-done = bf16[16,2048]{1,0:T(8,128)(2,1)} async-done(((bf16[32,2048]{1,0:T(8,128)(2,1)}), bf16[16,2048]{1,0:T(8,128)(2,1)}) %reduce-scatter.3.cloned.1.call-update) | async-done | bytes 65552 | tf_op jit(solution)/shard_map/reduce_scatter | solution.py:107
  63.6 1.5 fusion.28
  65.2 1.2 copy.2054
  66.4 1.6 reduce_sum.9
  69.0 1.3 collective-permute-start.3
  70.3 4.5 %collective-permute-start.2 = (bf16[16,1,4,64]{3,2,0,1:T(4,128)(2,1)S(1)}, bf16[16,1,4,64]{3,2,0,1:T(4,128)(2,1)S(1)}, u32[]{:S(2)}, u32[]{:S(2)}) collective-permute-start(bf16[16,1,4,64]{3,2,0,1:T(4,128)(2,1)S(1)} %bitcast.399), channel_id=1, source_target_pairs={{0,2},{2,4},{4,6},{6,8},{8,10},{10,12},{12,14},{14,16},{16,18},{18... | collective-permute-start | bytes 24584 | tf_op jit(solution)/shard_map/ppermute | solution.py:16
  74.9 1.4 collective-permute-done.2
  79.7 11.3 %reduce-scatter.5.cloned.1.call-done = bf16[32,256]{1,0:T(8,128)(2,1)} async-done(((bf16[64,256]{1,0:T(8,128)(2,1)}), bf16[32,256]{1,0:T(8,128)(2,1)}) %reduce-scatter.5.cloned.1.call-update) | async-done | bytes 16400 | tf_op jit(solution)/shard_map/reduce_scatter | solution.py:121
  91.8 1.3 collective-permute-start.5
  93.1 4.5 %collective-permute-start.4 = (bf16[32,1,4,64]{3,0,2,1:T(8,128)(2,1)S(1)}, bf16[32,1,4,64]{3,0,2,1:T(8,128)(2,1)S(1)}, u32[]{:S(2)}, u32[]{:S(2)}) collective-permute-start(bf16[32,1,4,64]{3,0,2,1:T(8,128)(2,1)S(1)} %copy.2056), channel_id=1, source_target_pairs={{0,2},{2,4},{4,6},{6,8},{8,10},{10,12},{12,14},{14,16},{16,18},{18... | collective-permute-start | bytes 49160 | tf_op jit(solution)/shard_map/ppermute | solution.py:16
  97.7 1.6 collective-permute-done.4
  99.3 2.1 all_gather.6
  107.2 4.5 %collective-permute-start.6 = (bf16[16,1,8,128]{3,0,2,1:T(8,128)(2,1)S(1)}, bf16[16,1,8,128]{3,0,2,1:T(8,128)(2,1)S(1)}, u32[]{:S(2)}, u32[]{:S(2)}) collective-permute-start(bf16[16,1,8,128]{3,0,2,1:T(8,128)(2,1)S(1)} %get-tuple-element.144), channel_id=1, source_target_pairs={{0,2},{2,4},{4,6},{6,8},{8,10},{10,12},{12,14},{14,16},{16,18},{18... | collective-permute-start | bytes 98312 | tf_op jit(solution)/shard_map/ppermute | solution.py:16
  111.7 1.3 collective-permute-start.7
  113.0 2.1 convolution_bitcast_fusion
  115.2 3.5 %collective-permute-done.7 = bf16[16,1,8,128]{3,0,2,1:T(8,128)(2,1)S(1)} collective-permute-done((bf16[16,1,8,128]{3,0,2,1:T(8,128)(2,1)S(1)}, bf16[16,1,8,128]{3,0,2,1:T(8,128)(2,1)S(1)}, u32[]{:S(2)}, u32[]{:S(2)}) %collective-permute-start.7) | collective-permute-done | bytes 32800 | tf_op jit(solution)/shard_map/ppermute | solution.py:19
  118.8 2.0 all_gather.7
  122.2 1.6 reshape.344
  123.8 2.8 %dot_general.32 = bf16[4,10,130,32]{2,1,0,3:T(8,128)(2,1)S(1)} reshape(bf16[5200,32]{0,1:T(8,128)(2,1)} %bitcast.366) | data formatting | bytes 665600 | tf_op jit(solution)/shard_map/dot_general | solution.py:68
  126.7 2.5 %fusion = f32[27,16,4,10,130]{4,1,3,2,0:T(8,128)S(1)} fusion(bf16[4,10,130,32]{2,1,0,3:T(8,128)(2,1)S(1)} %dot_general.32, bf16[32,16,27]{0,1,2:T(8,128)(2,1)S(1)} %copy-done.6), kind=kOutput, calls=%fused_computation.28 | convolution fusion | flops 143769600 | bytes 9346048 | tf_op jit(solution)/shard_map/dot_general | solution.py:68
  130.1 1.7 convolution_bitcast_fusion.1
  131.8 77.8 %psum.14 = f32[32,16,27]{2,0,1:T(8,128)S(1)} all-reduce(f32[32,16,27]{2,0,1:T(8,128)S(1)} %convolution_bitcast_fusion.1), channel_id=1, replica_groups=mesh['depth'=16,'chan'=2] {'depth'}, use_global_device_ids=true, to_apply=%region_3.4 | all-reduce | flops 13824 | bytes 110592 | tf_op jit(solution)/shard_map/psum | solution.py:154
  211.1 17.6 %all-reduce.6.cloned.1.call-done = f32[64,16,27]{0,2,1:T(8,128)} async-done(((f32[64,16,27]{0,2,1:T(8,128)}), f32[64,16,27]{0,2,1:T(8,128)}) %all-reduce.6.cloned.1.call-update) | async-done | bytes 110608 | tf_op jit(solution)/shard_map/psum | solution.py:135
  228.8 1.8 copy.2097
  (120 shorter events, 31.8 us)
Async XLA Ops:
  7.2 46.7 %copy-start = (bf16[64,32,27]{0,1,2:T(8,128)(2,1)S(1)}, bf16[64,32,27]{0,1,2:T(8,128)(2,1)}, u32[]{:S(2)}) copy-start(bf16[64,32,27]{0,1,2:T(8,128)(2,1)} %param.6) | copy-start | bytes 331780
  7.2 56.4 %reduce-scatter.3.cloned.1.call-start = ((), (), s32[]{:S(2)}) async-start(), calls=%async_computation.2 | async-start | bytes 196608 | tf_op jit(solution)/shard_map/reduce_scatter | solution.py:107
  8.2 7.4 %collective-permute-start = (bf16[16,1,8,128]{3,0,2,1:T(8,128)(2,1)S(1)}, bf16[16,1,8,128]{3,0,2,1:T(8,128)(2,1)S(1)}, u32[]{:S(2)}, u32[]{:S(2)}) collective-permute-start(bf16[16,1,8,128]{3,0,2,1:T(8,128)(2,1)S(1)} %get-tuple-element.146), channel_id=1, source_target_pairs={{0,2},{2,4},{4,6},{6,8},{8,10},{10,12},{12,14},{14,16},{16,18},{18... | collective-permute-start | bytes 98312 | tf_op jit(solution)/shard_map/ppermute | solution.py:16
  13.0 5.8 %collective-permute-start.1 = (bf16[16,1,8,128]{3,0,2,1:T(8,128)(2,1)S(1)}, bf16[16,1,8,128]{3,0,2,1:T(8,128)(2,1)S(1)}, u32[]{:S(2)}, u32[]{:S(2)}) collective-permute-start(bf16[16,1,8,128]{3,0,2,1:T(8,128)(2,1)S(1)} %get-tuple-element.147), channel_id=1, source_target_pairs={{2,0},{4,2},{6,4},{8,6},{10,8},{12,10},{14,12},{16,14},{18,16},{20... | collective-permute-start | bytes 98312 | tf_op jit(solution)/shard_map/ppermute | solution.py:19
  15.6 35.7 %copy-start.5 = (bf16[32,16,27]{0,1,2:T(8,128)(2,1)}, bf16[32,16,27]{0,1,2:T(8,128)(2,1)S(1)}, u32[]{:S(2)}) copy-start(bf16[32,16,27]{0,1,2:T(8,128)(2,1)S(1)} %copy.2157) | copy-start | bytes 82948
  53.9 37.1 %reduce-scatter.5.cloned.1.call-start = ((), (), s32[]{:S(2)}) async-start(), calls=%async_computation.3 | async-start | bytes 49152 | tf_op jit(solution)/shard_map/reduce_scatter | solution.py:121
  66.4 13.2 %copy-start.7 = (bf16[32,1,4,64]{3,2,1,0:T(4,128)(2,1)S(1)}, bf16[32,1,4,64]{3,2,1,0:T(4,128)(2,1)}, u32[]{:S(2)}) copy-start(bf16[32,1,4,64]{3,2,1,0:T(4,128)(2,1)} %param.7) | copy-start | bytes 49156
  69.0 5.9 %collective-permute-start.3 = (bf16[16,1,4,64]{3,2,0,1:T(4,128)(2,1)S(1)}, bf16[16,1,4,64]{3,2,0,1:T(4,128)(2,1)S(1)}, u32[]{:S(2)}, u32[]{:S(2)}) collective-permute-start(bf16[16,1,4,64]{3,2,0,1:T(4,128)(2,1)S(1)} %bitcast.398), channel_id=1, source_target_pairs={{2,0},{4,2},{6,4},{8,6},{10,8},{12,10},{14,12},{16,14},{18,16},{20... | collective-permute-start | bytes 24584 | tf_op jit(solution)/shard_map/ppermute | solution.py:19
  70.3 6.0 %collective-permute-start.2 = (bf16[16,1,4,64]{3,2,0,1:T(4,128)(2,1)S(1)}, bf16[16,1,4,64]{3,2,0,1:T(4,128)(2,1)S(1)}, u32[]{:S(2)}, u32[]{:S(2)}) collective-permute-start(bf16[16,1,4,64]{3,2,0,1:T(4,128)(2,1)S(1)} %bitcast.399), channel_id=1, source_target_pairs={{0,2},{2,4},{4,6},{6,8},{8,10},{10,12},{12,14},{14,16},{16,18},{18... | collective-permute-start | bytes 24584 | tf_op jit(solution)/shard_map/ppermute | solution.py:16
  78.3 25.5 %copy-start.1 = (bf16[27,16,1,4,64]{4,3,1,2,0:T(4,128)(2,1)}, bf16[27,16,1,4,64]{4,3,1,2,0:T(4,128)(2,1)S(1)}, u32[]{:S(2)}) copy-start(bf16[27,16,1,4,64]{4,3,1,2,0:T(4,128)(2,1)S(1)} %constant_dynamic-update-slice_fusion) | copy-start | bytes 663556
  79.5 149.2 %all-reduce.6.cloned.1.call-start = ((), (), s32[]{:S(2)}) async-start(), calls=%async_computation.4 | async-start | bytes 524288 | tf_op jit(solution)/shard_map/psum | solution.py:135
  91.8 5.9 %collective-permute-start.5 = (bf16[32,1,4,64]{3,0,2,1:T(8,128)(2,1)S(1)}, bf16[32,1,4,64]{3,0,2,1:T(8,128)(2,1)S(1)}, u32[]{:S(2)}, u32[]{:S(2)}) collective-permute-start(bf16[32,1,4,64]{3,0,2,1:T(8,128)(2,1)S(1)} %copy.2056), channel_id=1, source_target_pairs={{2,0},{4,2},{6,4},{8,6},{10,8},{12,10},{14,12},{16,14},{18,16},{20... | collective-permute-start | bytes 49160 | tf_op jit(solution)/shard_map/ppermute | solution.py:19
  93.1 6.1 %collective-permute-start.4 = (bf16[32,1,4,64]{3,0,2,1:T(8,128)(2,1)S(1)}, bf16[32,1,4,64]{3,0,2,1:T(8,128)(2,1)S(1)}, u32[]{:S(2)}, u32[]{:S(2)}) collective-permute-start(bf16[32,1,4,64]{3,0,2,1:T(8,128)(2,1)S(1)} %copy.2056), channel_id=1, source_target_pairs={{0,2},{2,4},{4,6},{6,8},{8,10},{10,12},{12,14},{14,16},{16,18},{18... | collective-permute-start | bytes 49160 | tf_op jit(solution)/shard_map/ppermute | solution.py:16
  101.4 0.7 copy-start.4
  107.2 7.9 %collective-permute-start.6 = (bf16[16,1,8,128]{3,0,2,1:T(8,128)(2,1)S(1)}, bf16[16,1,8,128]{3,0,2,1:T(8,128)(2,1)S(1)}, u32[]{:S(2)}, u32[]{:S(2)}) collective-permute-start(bf16[16,1,8,128]{3,0,2,1:T(8,128)(2,1)S(1)} %get-tuple-element.144), channel_id=1, source_target_pairs={{0,2},{2,4},{4,6},{6,8},{8,10},{10,12},{12,14},{14,16},{16,18},{18... | collective-permute-start | bytes 98312 | tf_op jit(solution)/shard_map/ppermute | solution.py:16
  111.7 7.0 %collective-permute-start.7 = (bf16[16,1,8,128]{3,0,2,1:T(8,128)(2,1)S(1)}, bf16[16,1,8,128]{3,0,2,1:T(8,128)(2,1)S(1)}, u32[]{:S(2)}, u32[]{:S(2)}) collective-permute-start(bf16[16,1,8,128]{3,0,2,1:T(8,128)(2,1)S(1)} %get-tuple-element.145), channel_id=1, source_target_pairs={{2,0},{4,2},{6,4},{8,6},{10,8},{12,10},{14,12},{16,14},{18,16},{20... | collective-permute-start | bytes 98312 | tf_op jit(solution)/shard_map/ppermute | solution.py:19
  120.8 0.7 copy-start.2
  121.6 5.1 %copy-start.6 = (bf16[32,16,27]{0,1,2:T(8,128)(2,1)S(1)}, bf16[32,16,27]{0,1,2:T(8,128)(2,1)}, u32[]{:S(2)}) copy-start(bf16[32,16,27]{0,1,2:T(8,128)(2,1)} %copy-done.5) | copy-start | bytes 82948
  129.2 1.0 copy-start.3
Sparse Core Ops, SparseCore 0:
  54.0 9.5 reduce-scatter.2
  79.6 11.2 reduce-scatter.4
  115.3 113.4 all-reduce.5
where the time goes:
time: 239 us; the launch traced here: 237 us
  blocking collectives  81.9 us (34%)
  local copies, waits for them, and re-layouts  51.5 us (22%)
  waiting for transfers between devices  48.4 us (20%)
  starting transfers between devices  23.7 us (10%)
  between operations  14.3 us (6%)
  matrix products  10.5 us (4%)
  other arithmetic  6.83 us (3%)
    psum x1, blocking collectives, shards(): grad_weight_one = lax.psum(grad_weight_one, 'depth')  77.8 us
    another operation x32, local copies, waits for them, and re-layouts, patch_rows(): return jnp.stack(windows, 0).reshape(27 * chans, planes * height * across)  28.5 us
    ppermute x4, starting transfers between devices, padded_2(): lax.ppermute(lax.slice_in_dim(block, block.shape[dim] - width, None, axis...  18.4 us
    psum x1, waiting for transfers between devices, shards(): grad_weight_two = lax.psum(grad_weight_two, 'depth')  17.6 us
    reduce_scatter x1, waiting for transfers between devices, shards(): lax.psum_scatter(partial_two.astype(jnp.bfloat16), 'chan', scatter_dimens...  11.3 us
    reduce_scatter x1, waiting for transfers between devices, shards(): lax.psum_scatter(partial_one.astype(jnp.bfloat16), 'chan', scatter_dimens...  9.68 us
    unnamed x51, local copies, waits for them, and re-layouts  8.2 us
    ppermute x4, waiting for transfers between devices, padded_2(): lax.ppermute(lax.slice_in_dim(block, 0, width, axis=dim), axis, backward)  6.79 us
  transfers between devices with their start and end apart: 11, of which 7 were waited for; matrix products, arithmetic and copies ran while one was open for 6% of the time, Pallas kernels for 0%

commit v1 on v0

v1 whole, which is shorter than its diff:
```python
import functools

import jax
import jax.numpy as jnp
from jax import lax
from jax.experimental import pallas as pl
from jax.experimental.pallas import tpu as pltpu
from jax.sharding import PartitionSpec as P

F32 = jnp.float32
BF16 = jnp.bfloat16
BLOCK = 4
VMEM = pl.BlockSpec(memory_space=pltpu.VMEM)
SMEM = pl.BlockSpec(memory_space=pltpu.SMEM)


def log2(n):
    assert n & (n - 1) == 0
    return n.bit_length() - 1


def digits(index, *sizes):
    out = []
    for size in reversed(sizes):
        out.append(index & (size - 1))
        index = index >> log2(size)
    return out[::-1]


def iotas(rows, cols):
    return (
        lax.broadcasted_iota(jnp.int32, (rows, cols), 0),
        lax.broadcasted_iota(jnp.int32, (rows, cols), 1),
    )


def one_hot(condition, value=1.0):
    return jnp.where(condition, value, 0.0).astype(BF16)


def mm(a, b):
    return jnp.dot(a, b, preferred_element_type=F32)


def mm_t(a, b):
    return lax.dot_general(a, b, (((0,), (0,)), ((), ())), preferred_element_type=F32)


def order_matrix(chans, planes, height):
    size = chans * planes * height
    k, n = iotas(size, size)
    chan, plane, row = digits(k, chans, planes, height)
    return one_hot(n == (plane * height + row) * chans + chan)


def shifted(x):
    rows = x.shape[0]
    at = lax.broadcasted_iota(jnp.int32, x.shape, 0)
    before = jnp.where(at == 0, 0.0, pltpu.roll(x, 1, 0))
    after = jnp.where(at == rows - 1, 0.0, pltpu.roll(x, rows - 1, 0))
    return before, after


def slope_of(pre, sig):
    return sig * (1.0 + pre * (1.0 - sig))


def pack_kernel(d, feats, cot, out):
    planes, width = d.planes, d.width
    lanes = d.height * d.half
    f = mm_t(feats[...], order_matrix(d.half, planes, d.height)).astype(BF16)
    for p in range(planes):
        out[p * width : (p + 1) * width, :] = f[:, p * lanes : (p + 1) * lanes]
    c = mm_t(cot[...], order_matrix(d.half2, 1, d.height2)).astype(BF16)
    out[planes * width :, :] = c


def weight_kernel(d, w1i, w1o, w2i, w2o, f1, b1, f2, b2):
    mid, half, half2 = d.mid, d.half, d.half2
    h1, h2 = d.height, d.height2
    wide1 = h1 * mid
    own1 = h1 * half
    wide2 = h2 * 2 * half2
    k, n = iotas(mid, wide1)
    spread = mm(w1i[...], one_hot(k == (n & (mid - 1)))).astype(BF16)
    row = lax.broadcasted_iota(jnp.int32, (half, wide1), 1) >> log2(mid)
    zero = jnp.zeros((half, wide1), BF16)
    for a in range(3):
        for c in range(3):
            tiles = [spread[(9 * a + 3 * b + c) * mid : (9 * a + 3 * b + c + 1) * mid] for b in range(3)]
            for g in range(2):
                for r in range(h1):
                    strip = zero
                    for b in range(3):
                        strip = jnp.where(row == r - b + 1, tiles[b][g * half : (g + 1) * half], strip)
                    at = (g * 3 + c) * own1 + r * half
                    f1[a, at : at + half, :] = strip
    k, n = iotas(mid, own1)
    spread = mm(w1o[...], one_hot(k == (n & (half - 1)))).astype(BF16)
    row = lax.broadcasted_iota(jnp.int32, (mid, own1), 1) >> log2(half)
    zero = jnp.zeros((mid, own1), BF16)
    for a in range(3):
        for c in range(3):
            tiles = [spread[(9 * a + 3 * b + c) * mid : (9 * a + 3 * b + c + 1) * mid] for b in range(3)]
            for r in range(h1):
                strip = zero
                for b in range(3):
                    strip = jnp.where(row == r + b - 1, tiles[b], strip)
                at = (c * h1 + r) * mid
                b1[a, at : at + mid, :] = strip
    k, n = iotas(2 * half2, wide2)
    g2, r2, o2 = digits(n, 2, h2, half2)
    spread = mm(w2i[...], one_hot(k == g2 * half2 + o2)).astype(BF16)
    row = digits(lax.broadcasted_iota(jnp.int32, (half, wide2), 1), 2, h2, half2)[1]
    zero = jnp.zeros((half, wide2), BF16)
    for a in range(3):
        for c in range(3):
            tiles = [spread[(9 * a + 3 * b + c) * mid : (9 * a + 3 * b + c + 1) * mid] for b in range(3)]
            for g in range(2):
                for r in range(h2):
                    strip = zero
                    for b in range(3):
                        strip = jnp.where(row == r - b + 1, tiles[b][g * half : (g + 1) * half], strip)
                    at = ((c * 2 + g) * h2 + r) * half
                    f2[a, at : at + half, :] = strip
    k, n = iotas(mid, wide1)
    spread = mm(w2o[...], one_hot(k == (n & (mid - 1)), 0.125)).astype(BF16)
    row = lax.broadcasted_iota(jnp.int32, (half2, wide1), 1) >> (log2(mid) + 1)
    zero = jnp.zeros((half2, wide1), BF16)
    for a in range(3):
        for c in range(3):
            tiles = [
                spread[(9 * a + 3 * b + c) * 2 * half2 : (9 * a + 3 * b + c + 1) * 2 * half2] for b in range(3)
            ]
            for g in range(2):
                for r in range(h2):
                    strip = zero
                    for b in range(3):
                        strip = jnp.where(row == r + b - 1, tiles[b][g * half2 : (g + 1) * half2], strip)
                    at = ((c * 2 + g) * h2 + r) * half2
                    b2[a, at : at + half2, :] = strip


def main_kernel(
    d, scalars, lo, mi, hi, lo_x, mi_x, hi_x, f1, b1, f2, b2,
    feats_out, sums_out, xs, cs, sl, pair, zs, gs, up, g1, g1s,
):
    planes, width, wide1 = d.planes, d.width, d.height * d.mid
    width2 = width // 2
    own1 = d.height * d.half
    wide2 = d.height2 * 2 * d.half2
    own2 = d.height2 * d.half2
    zl = d.height2 * d.mid
    place, at_first, at_last = scalars[0], scalars[1], scalars[2]
    per = BLOCK * planes
    first, last = at_first > 0, at_last > 0

    def unpack(k, carry):
        at = place ^ k
        for block, pairs in enumerate(((lo, lo_x), (mi, mi_x), (hi, hi_x))):
            for g, ref in enumerate(pairs):
                for p in range(planes):
                    x = ref[k, p * width : (p + 1) * width, :]
                    before, after = shifted(x.astype(F32))
                    q = block * per + at * planes + p
                    base = g * 3 * own1
                    xs[q, :, base : base + own1] = before.astype(BF16)
                    xs[q, :, base + own1 : base + 2 * own1] = x
                    xs[q, :, base + 2 * own1 : base + 3 * own1] = after.astype(BF16)
                cs[block * BLOCK + at, :, g * own2 : (g + 1) * own2] = ref[k, planes * width :, :]
        return carry

    lax.fori_loop(0, BLOCK, unpack, 0)

    k, n = iotas(wide1, zl)
    r_in, o_in = digits(k, d.height, d.mid)
    g_in, i_in = digits(o_in, 2, d.half)
    pool = one_hot(n == (g_in * d.height2 + (r_in >> 1)) * d.half + i_in, 0.125)

    def forward(step, carry):
        q = 2 + 4 * step
        pre = jnp.zeros((4 * width, wide1), F32)
        for a in range(3):
            pre += mm(xs[pl.ds(q + a - 1, 4)].reshape(4 * width, 6 * own1), f1[a])
        sig = jax.nn.sigmoid(pre)
        sl[pl.ds(4 * step, 4)] = slope_of(pre, sig).reshape(4, width, wide1)
        act = (pre * sig).astype(BF16)
        rows = mm(act, pool).reshape(2, 2, width, zl)
        pair[...] = rows[:, 0] + rows[:, 1]
        for u in range(2):
            cell = pair[u, pl.ds(0, width2, 2), :] + pair[u, pl.ds(1, width2, 2), :]
            coarse = 1 + 2 * step + u
            outside = (first & (coarse < BLOCK)) | (last & (coarse >= 2 * BLOCK))
            cell = jnp.where(outside, 0.0, cell)
            before, after = shifted(cell)
            zs[coarse - 1, :, 0:zl] = before.astype(BF16)
            zs[coarse - 1, :, zl : 2 * zl] = cell.astype(BF16)
            zs[coarse - 1, :, 2 * zl :] = after.astype(BF16)
        return carry

    lax.fori_loop(0, (3 * per - 4) // 4, forward, 0)

    count = BLOCK + 4
    pre = jnp.zeros((count * width2, wide2), F32)
    for a in range(3):
        pre += mm(zs[a : a + count].reshape(count * width2, 3 * zl), f2[a])
    sig = jax.nn.sigmoid(pre)
    grad_two = cs[2 : 2 + count].reshape(count * width2, wide2).astype(F32) * slope_of(pre, sig)
    for u in range(count):
        g = grad_two[u * width2 : (u + 1) * width2]
        before, after = shifted(g)
        gs[u, :, 0:wide2] = after.astype(BF16)
        gs[u, :, wide2 : 2 * wide2] = g.astype(BF16)
        gs[u, :, 2 * wide2 :] = before.astype(BF16)

    inner = count - 2
    back = jnp.zeros((inner * width2, wide1), F32)
    for a in range(3):
        back += mm(gs[2 - a : 2 - a + inner].reshape(inner * width2, 3 * wide2), b2[a])
    for u in range(inner):
        b = back[u * width2 : (u + 1) * width2]
        for half in range(wide1 // 128):
            lanes = slice(half * 128, (half + 1) * 128)
            up[u * (wide1 // 128) + half, pl.ds(0, width2, 2), :] = b[:, lanes]
            up[u * (wide1 // 128) + half, pl.ds(1, width2, 2), :] = b[:, lanes]
    for u in range(2 * inner):
        q = 6 + u
        both = [up[(u // 2) * (wide1 // 128) + half] for half in range(wide1 // 128)]
        g = jnp.concatenate(both, axis=1) * sl[q - 2]
        if q < per:
            g = jnp.where(first, 0.0, g)
        if q >= 2 * per:
            g = jnp.where(last, 0.0, g)
        g1[u] = g.astype(BF16)

    for u in range(planes + 2):
        g = g1[place * planes + 1 + u]
        before, after = shifted(g.astype(F32))
        g1s[u, :, 0:wide1] = after.astype(BF16)
        g1s[u, :, wide1 : 2 * wide1] = g
        g1s[u, :, 2 * wide1 :] = before.astype(BF16)
    grad = jnp.zeros((planes * width, own1), F32)
    for a in range(3):
        grad += mm(g1s[2 - a : 2 - a + planes].reshape(planes * width, 3 * wide1), b1[a])
    grad = grad.astype(BF16)
    grad = jnp.concatenate([grad[p * width : (p + 1) * width] for p in range(planes)], axis=1)
    feats_out[...] = lax.dot_general(
        order_matrix(d.half, planes, d.height), grad, (((1,), (1,)), ((), ())), preferred_element_type=F32
    ).astype(BF16)

    def collect(parts, groups, rows, chans, lanes_used, base):
        lane = lax.broadcasted_iota(jnp.int32, (chans, 128), 1)
        for g in range(groups):
            for m in range(9):
                total = jnp.zeros((chans, 128), F32)
                for r in range(rows):
                    at = (g * rows + r) * chans
                    tile = parts[m // 3][at : at + chans, (m % 3) * 128 : (m % 3 + 1) * 128]
                    tile = pltpu.roll(tile, (64 * (m % 2) - (r - 1) * d.half) % 128, 1)
                    b = (lane & 63) >> log2(d.half)
                    if r == 0:
                        tile = jnp.where(b == 0, 0.0, tile)
                    if r == rows - 1:
                        tile = jnp.where(b == 2, 0.0, tile)
                    total += tile
                if m % 2:
                    total = jnp.where(lane < 64, held, total)
                held = total
                if m % 2 or m == 8:
                    at = base + (g * 5 + m // 2) * chans
                    sums_out[at : at + chans, :] = total.astype(BF16)

    center = g1[2 : 2 + per].reshape(per * width, wide1)
    parts = [
        mm_t(center, xs[per + a - 1 : 2 * per + a - 1, :, 0 : 3 * own1].reshape(per * width, 3 * own1))
        for a in range(3)
    ]
    collect(parts, 1, d.height, d.mid, own1, 0)
    center = gs[2 : 2 + BLOCK, :, wide2 : 2 * wide2].reshape(BLOCK * width2, wide2)
    parts = [mm_t(center, zs[2 + a : 2 + a + BLOCK].reshape(BLOCK * width2, 3 * zl)) for a in range(3)]
    collect(parts, 2, d.height2, d.half2, own2 // 2, 5 * d.mid)


def final_kernel(d, scalars, *refs):
    parts, (out1, out2, rows1, rows2) = refs[:-4], refs[-4:]
    terms = [p[...].astype(F32) for p in parts]
    while len(terms) > 1:
        terms = [terms[i] + terms[i + 1] for i in range(0, len(terms), 2)]
    total = terms[0]
    member = scalars[3]

    def lay_out(base, groups, chans, scratch, out):
        for m2 in range(5):
            tiles = [total[base + (g * 5 + m2) * chans : base + (g * 5 + m2 + 1) * chans] for g in range(groups)]
            tile = jnp.concatenate(tiles, axis=0) if groups > 1 else tiles[0]
            flat = tile.T
            for m in (2 * m2, 2 * m2 + 1):
                if m < 9:
                    for b in range(3):
                        at = 64 * (m % 2) + b * d.half
                        tap = 9 * (m // 3) + 3 * b + m % 3
                        scratch[tap * d.half : (tap + 1) * d.half, :] = flat[at : at + d.half]
        full = groups * chans
        for i in range(d.half):
            tile = scratch[pl.ds(i, 27, d.half), :]
            tile = jnp.concatenate([tile, jnp.zeros((5, full), F32)], axis=0).T
            tile = pltpu.roll(tile, member * (full // 2), 0)
            out[pl.ds(i, full, d.half), :] = tile[:, :27]

    lay_out(0, 1, d.mid, rows1, out1)
    lay_out(5 * d.mid, 2, d.half2, rows2, out2)


class Sizes:
    pass


def shards(feats, weight_one, weight_two, cotangent):
    d = Sizes()
    slabs = lax.axis_size("depth")
    groups = lax.axis_size("chan")
    assert groups == 2 and slabs % BLOCK == 0
    d.half, d.planes, d.height, d.width = feats.shape
    d.half2, coarse, d.height2, width2 = cotangent.shape
    d.mid = weight_one.shape[0]
    assert d.planes == 2 and coarse == 1 and d.half * 8 == 128 and d.height2 * d.half2 == 128
    assert d.width == 128 and d.height == 8 and d.mid == 32
    place = lax.axis_index("depth")
    member = lax.axis_index("chan")
    blocks = slabs // BLOCK
    scalars = jnp.stack(
        [
            place % BLOCK,
            (place < BLOCK).astype(jnp.int32),
            (place >= slabs - BLOCK).astype(jnp.int32),
            member,
        ]
    ).astype(jnp.int32)
    params = pltpu.CompilerParams(vmem_limit_bytes=40 * 1024 * 1024)

    rows = d.planes * d.width + width2
    item = pl.pallas_call(
        functools.partial(pack_kernel, d),
        out_shape=jax.ShapeDtypeStruct((rows, 128), BF16),
        in_specs=[VMEM] * 2,
        out_specs=VMEM,
        compiler_params=params,
        name="pack",
    )(feats.reshape(-1, d.width), cotangent.reshape(-1, width2))

    def xor(x, k):
        return lax.ppermute(x, "depth", [(i, i ^ k) for i in range(slabs)])

    def swap(x):
        return lax.ppermute(x, "chan", [(0, 1), (1, 0)])

    block = jnp.stack([item] + [xor(item, k) for k in range(1, BLOCK)])
    lo = lax.ppermute(block, "depth", [(i, i + BLOCK) for i in range(slabs - BLOCK)])
    hi = lax.ppermute(block, "depth", [(i + BLOCK, i) for i in range(slabs - BLOCK)])
    block_x, lo_x, hi_x = swap(block), swap(lo), swap(hi)

    w1 = jnp.where(member == 0, weight_one, jnp.roll(weight_one, (d.half, d.half), (0, 1)))
    w2 = jnp.where(member == 0, weight_two, jnp.roll(weight_two, (d.half2, d.half), (0, 1)))
    w1i = jnp.transpose(w1, (2, 1, 0)).reshape(27 * d.mid, d.mid)
    w1o = jnp.transpose(w1, (2, 0, 1)).reshape(27 * d.mid, d.mid)
    w2i = jnp.transpose(w2, (2, 1, 0)).reshape(27 * d.mid, 2 * d.half2)
    w2o = jnp.transpose(w2, (2, 0, 1)).reshape(27 * 2 * d.half2, d.mid)
    wide1 = d.height * d.mid
    own1 = d.height * d.half
    wide2 = d.height2 * 2 * d.half2
    zl = d.height2 * d.mid
    f1, b1, f2, b2 = pl.pallas_call(
        functools.partial(weight_kernel, d),
        out_shape=[
            jax.ShapeDtypeStruct((3, 6 * own1, wide1), BF16),
            jax.ShapeDtypeStruct((3, 3 * wide1, own1), BF16),
            jax.ShapeDtypeStruct((3, 3 * zl, wide2), BF16),
            jax.ShapeDtypeStruct((3, 3 * wide2, wide1), BF16),
        ],
        in_specs=[VMEM] * 4,
        out_specs=[VMEM] * 4,
        compiler_params=params,
        cost_estimate=pl.CostEstimate(flops=1 << 30, bytes_accessed=4 << 20, transcendentals=0),
        name="weights",
    )(w1i, w1o, w2i, w2o)

    per = BLOCK * d.planes
    grad, sums = pl.pallas_call(
        functools.partial(main_kernel, d),
        out_shape=[
            jax.ShapeDtypeStruct((d.half * d.planes * d.height, d.width), BF16),
            jax.ShapeDtypeStruct((5 * d.mid + 10 * d.half2, 128), BF16),
        ],
        in_specs=[SMEM] + [VMEM] * 10,
        out_specs=[VMEM] * 2,
        scratch_shapes=[
            pltpu.VMEM((3 * per, d.width, 6 * own1), BF16),
            pltpu.VMEM((3 * BLOCK, width2, wide2), BF16),
            pltpu.VMEM((3 * per - 4, d.width, wide1), F32),
            pltpu.VMEM((2, d.width, zl), F32),
            pltpu.VMEM((3 * BLOCK - 2, width2, 3 * zl), BF16),
            pltpu.VMEM((BLOCK + 4, width2, 3 * wide2), BF16),
            pltpu.VMEM(((BLOCK + 2) * (wide1 // 128), d.width, 128), F32),
            pltpu.VMEM((2 * (BLOCK + 2), d.width, wide1), BF16),
            pltpu.VMEM((d.planes + 2, d.width, 3 * wide1), BF16),
        ],
        compiler_params=params,
        cost_estimate=pl.CostEstimate(flops=1 << 33, bytes_accessed=8 << 20, transcendentals=0),
        name="chain",
    )(scalars, lo, block, hi, lo_x, block_x, hi_x, f1, b1, f2, b2)

    parts = [sums]
    radix = 1
    while radix < blocks:
        fan = min(4, blocks // radix)
        mine = parts[0]
        if len(parts) > 1:
            mine = sum_parts(parts)
        parts = [mine] + [xor(mine, BLOCK * radix * k) for k in range(1, fan)]
        radix *= fan
    out1, out2 = pl.pallas_call(
        functools.partial(final_kernel, d),
        out_shape=[
            jax.ShapeDtypeStruct((d.mid * d.half, 27), F32),
            jax.ShapeDtypeStruct((2 * d.half2 * d.half, 27), F32),
        ],
        in_specs=[SMEM] + [VMEM] * len(parts),
        out_specs=[VMEM] * 2,
        scratch_shapes=[
            pltpu.VMEM((27 * d.half, d.mid), F32),
            pltpu.VMEM((27 * d.half, 2 * d.half2), F32),
        ],
        compiler_params=params,
        name="finish",
    )(scalars, *parts)
    return (
        grad.reshape(feats.shape),
        out1.reshape(d.mid, d.half, 27),
        out2.reshape(2 * d.half2, d.half, 27),
    )


def sum_parts(parts):
    terms = [p.astype(F32) for p in parts]
    while len(terms) > 1:
        terms = [terms[i] + terms[i + 1] for i in range(0, len(terms), 2)]
    return terms[0].astype(BF16)


def solution(mesh):
    return jax.shard_map(
        shards,
        mesh=mesh,
        in_specs=(P("chan", "depth", None, None), P(), P(), P("chan", "depth", None, None)),
        out_specs=(P("chan", "depth", None, None), P(None, "chan", None), P(None, "chan", None)),
        check_vma=False,
    )
```

time: 239 us -> 55.7 us (0.23)
  blocking collectives: 81.9 us -> 0 us
  local copies, waits for them, and re-layouts: 51.5 us -> 5.06 us
  waiting for transfers between devices: 48.4 us -> 22 us
  between operations: 14.3 us -> 0.81 us
  Pallas kernels: 0 us -> 13 us
  matrix products: 10.5 us -> 0 us
  starting transfers between devices: 23.7 us -> 13.9 us
  other arithmetic: 6.83 us -> 0.64 us
    psum x1 -> x0, blocking collectives: 77.8 us -> none  [shards(): grad_weight_one = lax.psum(grad_weight_one, 'depth')]
    another operation x32 -> x0, local copies, waits for them, and re-layouts: 28.5 us -> none  [patch_rows(): return jnp.stack(windows, 0).reshape(27 * chans, planes * height * across)]
    reduce_scatter x2 -> x0, waiting for transfers between devices: 21 us -> none  [the longest x1 11.3 us: shards(): lax.psum_scatter(partial_two.astype(jnp.bfloat16), 'chan', scatter_dimens...]
    psum x1 -> x0, waiting for transfers between devices: 17.6 us -> none  [shards(): grad_weight_two = lax.psum(grad_weight_two, 'depth')]
    pallas_call x0 -> x4, Pallas kernels: none -> 13 us  [the longest x1 10.5 us: shards(): pl.pallas_call(functools.partial(main_kernel, d), out_shape=[jax.ShapeDty...]
    ppermute x8 -> x11, waiting for transfers between devices: 9.76 us -> 22 us  [the longest x6 14.2 us: xor(): return lax.ppermute(x, 'depth', [(i, i ^ k) for i in range(slabs)])]
    dot_general x6 -> x0, matrix products: 10.5 us -> none  [the longest x2 3.84 us: grad_fold(): lax.dot_general(inner, patches, (((1,), (1,)), ((), ())), preferred_eleme...]
    ppermute x8 -> x11, starting transfers between devices: 23.6 us -> 13.9 us  [the longest x6 9.03 us: xor(): return lax.ppermute(x, 'depth', [(i, i ^ k) for i in range(slabs)])]
  transfers between devices with their start and end apart: 11 -> 11, of which waited for: 7 -> 7; matrix products, arithmetic and copies ran while one was open for 6% -> 4% of each run, Pallas kernels for 0% -> 2%
where the time goes in v1:
time: 55.7 us; the launch traced here: 55.4 us
  waiting for transfers between devices  22 us (39%)
  starting transfers between devices  13.9 us (25%)
  Pallas kernels  13 us (23%)
  local copies, waits for them, and re-layouts  5.06 us (9%)
  between operations  0.81 us (1%)
  other arithmetic  0.64 us (1%)
    ppermute x6, waiting for transfers between devices, xor(): return lax.ppermute(x, 'depth', [(i, i ^ k) for i in range(slabs)])  14.2 us
    pallas_call x1, Pallas kernels, shards(): pl.pallas_call(functools.partial(main_kernel, d), out_shape=[jax.ShapeDty...  10.5 us
    ppermute x6, starting transfers between devices, xor(): return lax.ppermute(x, 'depth', [(i, i ^ k) for i in range(slabs)])  9.03 us
    ppermute x1, waiting for transfers between devices, shards(): lax.ppermute(block, 'depth', [(i + BLOCK, i) for i in range(slabs - BLOCK)])  4.13 us
    ppermute x1, waiting for transfers between devices, shards(): lax.ppermute(block, 'depth', [(i, i + BLOCK) for i in range(slabs - BLOCK)])  3.69 us
    ppermute x1, starting transfers between devices, shards(): lax.ppermute(block, 'depth', [(i, i + BLOCK) for i in range(slabs - BLOCK)])  3.5 us
    unnamed x10, local copies, waits for them, and re-layouts  3.46 us
    pallas_call x1, Pallas kernels, shards(): pl.pallas_call(functools.partial(final_kernel, d), out_shape=[jax.ShapeDt...  1.33 us
  transfers between devices with their start and end apart: 11, of which 7 were waited for; matrix products, arithmetic and copies ran while one was open for 4% of the time, Pallas kernels for 2%

profile of v1, /device:TPU:0, one launch (start us, length us, event | category | flops | bytes accessed | tf_op | source)
XLA Modules:
  0.0 55.4 jit_solution(13729751111785894318)
XLA Ops:
  0.6 0.8 %copy-done = bf16[16,2,8,128]{3,2,1,0:T(8,128)(2,1)S(1)} copy-done((bf16[16,2,8,128]{3,2,1,0:T(8,128)(2,1)S(1)}, bf16[16,2,8,128]{3,2,1,0:T(8,128)(2,1)}, u32[]{:S(2)}) %copy-start) | copy-done | bytes 65560
  1.5 0.8 %copy-done.1 = bf16[32,1,4,64]{3,2,1,0:T(4,128)(2,1)S(1)} copy-done((bf16[32,1,4,64]{3,2,1,0:T(4,128)(2,1)S(1)}, bf16[32,1,4,64]{3,2,1,0:T(4,128)(2,1)}, u32[]{:S(2)}) %copy-start.1) | copy-done | bytes 16408
  2.2 0.2 pack.1
  2.4 3.0 %collective-permute-start = (bf16[320,128]{1,0:T(8,128)(2,1)S(1)}, bf16[320,128]{1,0:T(8,128)(2,1)S(1)}, u32[]{:S(2)}, u32[]{:S(2)}) collective-permute-start(bf16[320,128]{1,0:T(8,128)(2,1)S(1)} %pack.1), channel_id=1, source_target_pairs={{0,2},{2,0},{4,6},{6,4},{8,10},{10,8},{12,14},{14,12},{16,18},{18,... | collective-permute-start | bytes 245768 | tf_op jit(solution)/shard_map/ppermute | solution.py:352
  5.5 1.5 %collective-permute-start.1 = (bf16[320,128]{1,0:T(8,128)(2,1)S(1)}, bf16[320,128]{1,0:T(8,128)(2,1)S(1)}, u32[]{:S(2)}, u32[]{:S(2)}) collective-permute-start(bf16[320,128]{1,0:T(8,128)(2,1)S(1)} %pack.1), channel_id=1, source_target_pairs={{0,4},{2,6},{4,0},{6,2},{8,12},{10,14},{12,8},{14,10},{16,20},{18,... | collective-permute-start | bytes 245768 | tf_op jit(solution)/shard_map/ppermute | solution.py:352
  7.0 0.0 collective-permute-start.2
  7.0 1.2 %fusion.5 = (bf16[32,32,27]{0,1,2:T(8,128)(2,1)S(1)}, bf16[32,32,27]{0,1,2:T(8,128)(2,1)S(1)}) fusion(bf16[64,32,27]{0,1,2:T(8,128)(2,1)} %param.6), kind=kLoop, calls=%fused_computation.12 | loop fusion | bytes 221184 | tf_op jit(solution)/shard_map/jit(_roll_static)/slice | solution.py:363
  8.2 0.1 slice_maximum_fusion
  8.4 2.4 %collective-permute-done.1 = bf16[320,128]{1,0:T(8,128)(2,1)S(1)} collective-permute-done((bf16[320,128]{1,0:T(8,128)(2,1)S(1)}, bf16[320,128]{1,0:T(8,128)(2,1)S(1)}, u32[]{:S(2)}, u32[]{:S(2)}) %collective-permute-start.1) | collective-permute-done | bytes 81952 | tf_op jit(solution)/shard_map/ppermute | solution.py:352
  10.8 1.5 %collective-permute-done.2 = bf16[320,128]{1,0:T(8,128)(2,1)S(1)} collective-permute-done((bf16[320,128]{1,0:T(8,128)(2,1)S(1)}, bf16[320,128]{1,0:T(8,128)(2,1)S(1)}, u32[]{:S(2)}, u32[]{:S(2)}) %collective-permute-start.2) | collective-permute-done | bytes 81952 | tf_op jit(solution)/shard_map/ppermute | solution.py:352
  12.4 3.5 %collective-permute-start.3 = (bf16[4,320,128]{2,1,0:T(8,128)(2,1)S(1)}, bf16[4,320,128]{2,1,0:T(8,128)(2,1)S(1)}, u32[]{:S(2)}, u32[]{:S(2)}) collective-permute-start(bf16[4,320,128]{2,1,0:T(8,128)(2,1)S(1)} %pad_maximum_fusion.mi), channel_id=1, source_target_pairs={{0,8},{2,10},{4,12},{6,14},{8,16},{10,18},{12,20},{14,22},{16,24},... | collective-permute-start | bytes 983048 | tf_op jit(solution)/shard_map/ppermute | solution.py:358
  15.9 1.3 %collective-permute-start.4 = (bf16[4,320,128]{2,1,0:T(8,128)(2,1)S(1)}, bf16[4,320,128]{2,1,0:T(8,128)(2,1)S(1)}, u32[]{:S(2)}, u32[]{:S(2)}) collective-permute-start(bf16[4,320,128]{2,1,0:T(8,128)(2,1)S(1)} %pad_maximum_fusion.mi), channel_id=1, source_target_pairs={{8,0},{10,2},{12,4},{14,6},{16,8},{18,10},{20,12},{22,14},{24,16},... | collective-permute-start | bytes 983048 | tf_op jit(solution)/shard_map/ppermute | solution.py:359
  17.2 0.1 fusion.4
  17.3 0.1 fusion.1
  17.4 0.1 collective-permute-start.6
  17.5 3.7 %collective-permute-done.3.lo = bf16[4,320,128]{2,1,0:T(8,128)(2,1)S(1)} collective-permute-done((bf16[4,320,128]{2,1,0:T(8,128)(2,1)S(1)}, bf16[4,320,128]{2,1,0:T(8,128)(2,1)S(1)}, u32[]{:S(2)}, u32[]{:S(2)}) %collective-permute-start.3) | collective-permute-done | bytes 327712 | tf_op jit(solution)/shard_map/ppermute | solution.py:358
  21.2 4.1 %collective-permute-done.4.hi = bf16[4,320,128]{2,1,0:T(8,128)(2,1)S(1)} collective-permute-done((bf16[4,320,128]{2,1,0:T(8,128)(2,1)S(1)}, bf16[4,320,128]{2,1,0:T(8,128)(2,1)S(1)}, u32[]{:S(2)}, u32[]{:S(2)}) %collective-permute-start.4) | collective-permute-done | bytes 327712 | tf_op jit(solution)/shard_map/ppermute | solution.py:359
  25.4 0.2 fusion.3
  25.5 0.3 copy.8
  25.8 0.2 copy.7
  26.0 1.0 %weights.1 = (bf16[3,768,256]{2,1,0:T(8,128)(2,1)S(1)}, bf16[3,768,128]{2,1,0:T(8,128)(2,1)S(1)}, bf16[3,384,256]{2,1,0:T(8,128)(2,1)S(1)}, bf16[3,768,256]{2,1,0:T(8,128)(2,1)S(1)}) custom-call(bf16[864,32]{1,0:T(8,128)(2,1)S(1)} %bitcast.31, bf16[864,32]{1,0:T(8,128)(2,1)S(1)} %bitcast.26, bf16[864,64]{1,0:T(8,128)(2,1)S(1)} %bitcast.24, ...), custom_call_target="tpu_custom_call" | custom-call | flops 1073741824 | bytes 4194304 | tf_op jit(solution)/shard_map/weights/pallas_call | solution.py:372
  27.0 0.1 pad_add_fusion.scalars
  27.0 10.5 %chain.1 = (bf16[256,128]{1,0:T(8,128)(2,1)}, bf16[480,128]{1,0:T(8,128)(2,1)S(1)}) custom-call(s32[4]{0:T(128)S(1)} %pad_add_fusion.scalars, bf16[4,320,128]{2,1,0:T(8,128)(2,1)S(1)} %collective-permute-done.3.lo, bf16[4,320,128]{2,1,0:T(8,128)(2,1)S(1)} %pad_maximum_fusion.mi, bf16[4,320,128]{2,1,0:T(8,128)(2,1)S(1)} %collective-permute-done.4.hi, ...), custom_call_target="tpu_custom_call" | custom-call | flops 8589934592 | bytes 8388608 | tf_op jit(solution)/shard_map/chain/pallas_call | solution.py:388
  37.5 1.6 %collective-permute-start.10 = (bf16[480,128]{1,0:T(8,128)(2,1)S(1)}, bf16[480,128]{1,0:T(8,128)(2,1)S(1)}, u32[]{:S(2)}, u32[]{:S(2)}) collective-permute-start(bf16[480,128]{1,0:T(8,128)(2,1)S(1)} %get-tuple-element.16.refs_0_), channel_id=1, source_target_pairs={{0,24},{2,26},{4,28},{6,30},{8,16},{10,18},{12,20},{14,22},{16,8},... | collective-permute-start | bytes 368648 | tf_op jit(solution)/shard_map/ppermute | solution.py:352
  39.1 1.6 %collective-permute-start.8 = (bf16[480,128]{1,0:T(8,128)(2,1)S(1)}, bf16[480,128]{1,0:T(8,128)(2,1)S(1)}, u32[]{:S(2)}, u32[]{:S(2)}) collective-permute-start(bf16[480,128]{1,0:T(8,128)(2,1)S(1)} %get-tuple-element.16.refs_0_), channel_id=1, source_target_pairs={{0,8},{2,10},{4,12},{6,14},{8,0},{10,2},{12,4},{14,6},{16,24},{18,... | collective-permute-start | bytes 368648 | tf_op jit(solution)/shard_map/ppermute | solution.py:352
  40.7 1.2 %collective-permute-start.9 = (bf16[480,128]{1,0:T(8,128)(2,1)S(1)}, bf16[480,128]{1,0:T(8,128)(2,1)S(1)}, u32[]{:S(2)}, u32[]{:S(2)}) collective-permute-start(bf16[480,128]{1,0:T(8,128)(2,1)S(1)} %get-tuple-element.16.refs_0_), channel_id=1, source_target_pairs={{0,16},{2,18},{4,20},{6,22},{8,24},{10,26},{12,28},{14,30},{16,0},... | collective-permute-start | bytes 368648 | tf_op jit(solution)/shard_map/ppermute | solution.py:352
  42.0 3.7 %collective-permute-done.10.refs_3_ = bf16[480,128]{1,0:T(8,128)(2,1)S(1)} collective-permute-done((bf16[480,128]{1,0:T(8,128)(2,1)S(1)}, bf16[480,128]{1,0:T(8,128)(2,1)S(1)}, u32[]{:S(2)}, u32[]{:S(2)}) %collective-permute-start.10) | collective-permute-done | bytes 122912 | tf_op jit(solution)/shard_map/ppermute | solution.py:352
  45.6 2.3 %collective-permute-done.8.refs_1_ = bf16[480,128]{1,0:T(8,128)(2,1)S(1)} collective-permute-done((bf16[480,128]{1,0:T(8,128)(2,1)S(1)}, bf16[480,128]{1,0:T(8,128)(2,1)S(1)}, u32[]{:S(2)}, u32[]{:S(2)}) %collective-permute-start.8) | collective-permute-done | bytes 122912 | tf_op jit(solution)/shard_map/ppermute | solution.py:352
  47.9 4.3 %collective-permute-done.9.refs_2_ = bf16[480,128]{1,0:T(8,128)(2,1)S(1)} collective-permute-done((bf16[480,128]{1,0:T(8,128)(2,1)S(1)}, bf16[480,128]{1,0:T(8,128)(2,1)S(1)}, u32[]{:S(2)}, u32[]{:S(2)}) %collective-permute-start.9) | collective-permute-done | bytes 122912 | tf_op jit(solution)/shard_map/ppermute | solution.py:352
  52.2 1.3 %finish.1 = (f32[512,27]{1,0:T(8,128)S(1)}, f32[1024,27]{1,0:T(8,128)S(1)}) custom-call(s32[4]{0:T(128)S(1)} %pad_add_fusion.scalars, bf16[480,128]{1,0:T(8,128)(2,1)S(1)} %get-tuple-element.16.refs_0_, bf16[480,128]{1,0:T(8,128)(2,1)S(1)} %collective-permute-done.8.refs_1_, bf16[480,128]{1,0:T(8,128)(2,1)S(1)} %collective-permute-done.9.refs_2_, ...), custom_call_target="tpu_custom_call" | custom-call | tf_op jit(solution)/shard_map/finish/pallas_call | solution.py:421
  53.6 1.0 %copy.10 = f32[64,16,27]{0,1,2:T(8,128)} copy(f32[64,16,27]{2,1,0:T(8,128)S(1)} %bitcast.27) | data formatting | bytes 221184
  54.5 0.9 %copy.9 = f32[32,16,27]{0,1,2:T(8,128)} copy(f32[32,16,27]{2,1,0:T(8,128)S(1)} %bitcast.30) | data formatting | bytes 110592
  (14 shorter events, 0.1 us)
Async XLA Ops:
  0.6 0.8 %copy-start = (bf16[16,2,8,128]{3,2,1,0:T(8,128)(2,1)S(1)}, bf16[16,2,8,128]{3,2,1,0:T(8,128)(2,1)}, u32[]{:S(2)}) copy-start(bf16[16,2,8,128]{3,2,1,0:T(8,128)(2,1)} %param.4) | copy-start | bytes 196612
  1.5 0.8 %copy-start.1 = (bf16[32,1,4,64]{3,2,1,0:T(4,128)(2,1)S(1)}, bf16[32,1,4,64]{3,2,1,0:T(4,128)(2,1)}, u32[]{:S(2)}) copy-start(bf16[32,1,4,64]{3,2,1,0:T(4,128)(2,1)} %param.7) | copy-start | bytes 49156
  2.2 6.0 %copy-start.3 = (bf16[32,32,27]{1,0,2:T(8,128)(2,1)S(1)}, bf16[32,32,27]{1,0,2:T(8,128)(2,1)}, u32[]{:S(2)}) copy-start(bf16[32,32,27]{1,0,2:T(8,128)(2,1)} %param.5) | copy-start | bytes 165892
  2.4 5.9 %collective-permute-start = (bf16[320,128]{1,0:T(8,128)(2,1)S(1)}, bf16[320,128]{1,0:T(8,128)(2,1)S(1)}, u32[]{:S(2)}, u32[]{:S(2)}) collective-permute-start(bf16[320,128]{1,0:T(8,128)(2,1)S(1)} %pack.1), channel_id=1, source_target_pairs={{0,2},{2,0},{4,6},{6,4},{8,10},{10,8},{12,14},{14,12},{16,18},{18,... | collective-permute-start | bytes 245768 | tf_op jit(solution)/shard_map/ppermute | solution.py:352
  5.5 5.3 %collective-permute-start.1 = (bf16[320,128]{1,0:T(8,128)(2,1)S(1)}, bf16[320,128]{1,0:T(8,128)(2,1)S(1)}, u32[]{:S(2)}, u32[]{:S(2)}) collective-permute-start(bf16[320,128]{1,0:T(8,128)(2,1)S(1)} %pack.1), channel_id=1, source_target_pairs={{0,4},{2,6},{4,0},{6,2},{8,12},{10,14},{12,8},{14,10},{16,20},{18,... | collective-permute-start | bytes 245768 | tf_op jit(solution)/shard_map/ppermute | solution.py:352
  7.0 5.3 %collective-permute-start.2 = (bf16[320,128]{1,0:T(8,128)(2,1)S(1)}, bf16[320,128]{1,0:T(8,128)(2,1)S(1)}, u32[]{:S(2)}, u32[]{:S(2)}) collective-permute-start(bf16[320,128]{1,0:T(8,128)(2,1)S(1)} %pack.1), channel_id=1, source_target_pairs={{0,6},{2,4},{4,2},{6,0},{8,14},{10,12},{12,10},{14,8},{16,22},{18,... | collective-permute-start | bytes 245768 | tf_op jit(solution)/shard_map/ppermute | solution.py:352
  8.2 9.1 %copy-start.2 = (bf16[64,32,27]{0,1,2:T(8,128)(2,1)S(1)}, bf16[64,32,27]{0,1,2:T(8,128)(2,1)}, u32[]{:S(2)}) copy-start(bf16[64,32,27]{0,1,2:T(8,128)(2,1)} %param.6) | copy-start | bytes 331780
  12.4 8.8 %collective-permute-start.3 = (bf16[4,320,128]{2,1,0:T(8,128)(2,1)S(1)}, bf16[4,320,128]{2,1,0:T(8,128)(2,1)S(1)}, u32[]{:S(2)}, u32[]{:S(2)}) collective-permute-start(bf16[4,320,128]{2,1,0:T(8,128)(2,1)S(1)} %pad_maximum_fusion.mi), channel_id=1, source_target_pairs={{0,8},{2,10},{4,12},{6,14},{8,16},{10,18},{12,20},{14,22},{16,24},... | collective-permute-start | bytes 983048 | tf_op jit(solution)/shard_map/ppermute | solution.py:358
  15.9 9.5 %collective-permute-start.4 = (bf16[4,320,128]{2,1,0:T(8,128)(2,1)S(1)}, bf16[4,320,128]{2,1,0:T(8,128)(2,1)S(1)}, u32[]{:S(2)}, u32[]{:S(2)}) collective-permute-start(bf16[4,320,128]{2,1,0:T(8,128)(2,1)S(1)} %pad_maximum_fusion.mi), channel_id=1, source_target_pairs={{8,0},{10,2},{12,4},{14,6},{16,8},{18,10},{20,12},{22,14},{24,16},... | collective-permute-start | bytes 983048 | tf_op jit(solution)/shard_map/ppermute | solution.py:359
  17.4 9.6 %collective-permute-start.6 = (bf16[4,320,128]{2,1,0:T(8,128)(2,1)S(1)}, bf16[4,320,128]{2,1,0:T(8,128)(2,1)S(1)}, u32[]{:S(2)}, u32[]{:S(2)}) collective-permute-start(bf16[4,320,128]{2,1,0:T(8,128)(2,1)S(1)} %pad_maximum_fusion.mi), channel_id=1, source_target_pairs={{0,1},{1,0},{2,3},{3,2},{4,5},{5,4},{6,7},{7,6},{8,9},{9,8},{10,11... | collective-permute-start | bytes 983048 | tf_op jit(solution)/shard_map/ppermute | solution.py:355
  21.2 5.8 %collective-permute-start.5 = (bf16[4,320,128]{2,1,0:T(8,128)(2,1)S(1)}, bf16[4,320,128]{2,1,0:T(8,128)(2,1)S(1)}, u32[]{:S(2)}, u32[]{:S(2)}) collective-permute-start(bf16[4,320,128]{2,1,0:T(8,128)(2,1)S(1)} %collective-permute-done.3.lo), channel_id=1, source_target_pairs={{0,1},{1,0},{2,3},{3,2},{4,5},{5,4},{6,7},{7,6},{8,9},{9,8},{10,11... | collective-permute-start | bytes 983048 | tf_op jit(solution)/shard_map/ppermute | solution.py:355
  25.3 1.7 %collective-permute-start.7 = (bf16[4,320,128]{2,1,0:T(8,128)(2,1)S(1)}, bf16[4,320,128]{2,1,0:T(8,128)(2,1)S(1)}, u32[]{:S(2)}, u32[]{:S(2)}) collective-permute-start(bf16[4,320,128]{2,1,0:T(8,128)(2,1)S(1)} %collective-permute-done.4.hi), channel_id=1, source_target_pairs={{0,1},{1,0},{2,3},{3,2},{4,5},{5,4},{6,7},{7,6},{8,9},{9,8},{10,11... | collective-permute-start | bytes 983048 | tf_op jit(solution)/shard_map/ppermute | solution.py:355
  37.5 8.1 %collective-permute-start.10 = (bf16[480,128]{1,0:T(8,128)(2,1)S(1)}, bf16[480,128]{1,0:T(8,128)(2,1)S(1)}, u32[]{:S(2)}, u32[]{:S(2)}) collective-permute-start(bf16[480,128]{1,0:T(8,128)(2,1)S(1)} %get-tuple-element.16.refs_0_), channel_id=1, source_target_pairs={{0,24},{2,26},{4,28},{6,30},{8,16},{10,18},{12,20},{14,22},{16,8},... | collective-permute-start | bytes 368648 | tf_op jit(solution)/shard_map/ppermute | solution.py:352
  39.1 8.8 %collective-permute-start.8 = (bf16[480,128]{1,0:T(8,128)(2,1)S(1)}, bf16[480,128]{1,0:T(8,128)(2,1)S(1)}, u32[]{:S(2)}, u32[]{:S(2)}) collective-permute-start(bf16[480,128]{1,0:T(8,128)(2,1)S(1)} %get-tuple-element.16.refs_0_), channel_id=1, source_target_pairs={{0,8},{2,10},{4,12},{6,14},{8,0},{10,2},{12,4},{14,6},{16,24},{18,... | collective-permute-start | bytes 368648 | tf_op jit(solution)/shard_map/ppermute | solution.py:352
  40.7 11.5 %collective-permute-start.9 = (bf16[480,128]{1,0:T(8,128)(2,1)S(1)}, bf16[480,128]{1,0:T(8,128)(2,1)S(1)}, u32[]{:S(2)}, u32[]{:S(2)}) collective-permute-start(bf16[480,128]{1,0:T(8,128)(2,1)S(1)} %get-tuple-element.16.refs_0_), channel_id=1, source_target_pairs={{0,16},{2,18},{4,20},{6,22},{8,24},{10,26},{12,28},{14,30},{16,0},... | collective-permute-start | bytes 368648 | tf_op jit(solution)/shard_map/ppermute | solution.py:352

commit v2 on v0

v2 whole, which is shorter than its diff:
```python
import functools

import jax
import jax.numpy as jnp
from jax import lax
from jax.experimental import pallas as pl
from jax.experimental.pallas import tpu as pltpu
from jax.sharding import PartitionSpec as P

F32 = jnp.float32
BF16 = jnp.bfloat16
BLOCK = 4
EDGE = 3
VMEM = pl.BlockSpec(memory_space=pltpu.VMEM)


def log2(n):
    assert n & (n - 1) == 0
    return n.bit_length() - 1


def digits(index, *sizes):
    out = []
    for size in reversed(sizes):
        out.append(index & (size - 1))
        index = index >> log2(size)
    return out[::-1]


def iotas(rows, cols):
    return (
        lax.broadcasted_iota(jnp.int32, (rows, cols), 0),
        lax.broadcasted_iota(jnp.int32, (rows, cols), 1),
    )


def one_hot(condition, value=1.0):
    return jnp.where(condition, value, 0.0).astype(BF16)


def mm(a, b):
    return jnp.dot(a, b, preferred_element_type=F32)


def mm_t(a, b):
    return lax.dot_general(a, b, (((0,), (0,)), ((), ())), preferred_element_type=F32)


def order_matrix(chans, planes, height):
    size = chans * planes * height
    k, n = iotas(size, size)
    chan, plane, row = digits(k, chans, planes, height)
    return one_hot(n == (plane * height + row) * chans + chan)


def shifted(x):
    rows = x.shape[0]
    at = lax.broadcasted_iota(jnp.int32, x.shape, 0)
    before = jnp.where(at == 0, 0.0, pltpu.roll(x, 1, 0))
    after = jnp.where(at == rows - 1, 0.0, pltpu.roll(x, rows - 1, 0))
    return before, after


def slope_of(pre, sig):
    return sig * (1.0 + pre * (1.0 - sig))


def pack_kernel(d, feats, cot, out, feats_in, cot_in, sems):
    copies = [
        pltpu.make_async_copy(feats, feats_in, sems.at[0]),
        pltpu.make_async_copy(cot, cot_in, sems.at[1]),
    ]
    for copy in copies:
        copy.start()
    planes, width = d.planes, d.width
    lanes = d.height * d.half
    turn = order_matrix(d.half, planes, d.height)
    turn2 = order_matrix(d.half2, 1, d.height2)
    copies[0].wait()
    f = mm_t(feats_in[...], turn).astype(BF16)
    for p in range(planes):
        out[p * width : (p + 1) * width, :] = f[:, p * lanes : (p + 1) * lanes]
    copies[1].wait()
    out[planes * width :, :] = mm_t(cot_in[...], turn2).astype(BF16)


def parity():
    return (lax.axis_index("depth") >> log2(BLOCK)) & 1 == 0


def sort_kernel(d, i0, i1, i2, i3, mid, to_a, to_b):
    place = lax.axis_index("depth") & (BLOCK - 1)
    odd = (lax.axis_index("depth") >> log2(BLOCK)) & 1
    width, width2 = d.width, d.width // 2
    body = d.planes * width
    per = BLOCK * body
    for k, ref in enumerate((i0, i1, i2, i3)):
        at = place ^ k
        mid[pl.ds(at * body, body), :] = ref[:body, :]
        mid[pl.ds(per + at * width2, width2), :] = ref[body:, :]
    side = EDGE * width
    for out, top in ((to_a, 1 - odd), (to_b, odd)):
        out[:side, :] = mid[pl.ds(pl.multiple_of(top * (per - side), side // EDGE), side), :]
        out[side:, :] = mid[pl.ds(pl.multiple_of(per + top * 2 * width2, width2), 2 * width2), :]


def band(out, a, at, size, groups, row, shift):
    strip = jnp.zeros((size, row.shape[1]), BF16)
    for b in range(3):
        strip = jnp.where(row == shift[b], groups[b], strip)
    out[a, at : at + size, :] = strip


def weight_kernel(d, w1, w2, f1, b1, f2, b2, w1_in, w2_in, t1, t2, t3, t4, sems):
    copies = [pltpu.make_async_copy(w1, w1_in, sems.at[0]), pltpu.make_async_copy(w2, w2_in, sems.at[1])]
    for copy in copies:
        copy.start()
    member = lax.axis_index("chan")
    mid, half, half2 = d.mid, d.half, d.half2
    h1, h2 = d.height, d.height2
    wide1 = h1 * mid
    own1 = h1 * half
    wide2 = h2 * 2 * half2
    k, n = iotas(mid, wide1)
    own_first = (k ^ (member * half)) == (n & (mid - 1))
    for copy in copies:
        copy.wait()
    for t in range(27):
        at = slice(t * mid, (t + 1) * mid)
        t1[at, :] = mm_t(w1_in[at, :], one_hot(own_first)).astype(BF16)
        t4[t * 2 * half2 : (t + 1) * 2 * half2, :] = mm_t(w2_in[at, :], one_hot(own_first, 0.125)).astype(BF16)
    k, n = iotas(mid, own1)
    t2[...] = mm(w1_in[...], one_hot((k ^ (member * half)) == (n & (half - 1)))).astype(BF16)
    k, n = iotas(2 * half2, wide2)
    g2, _, o2 = digits(n, 2, h2, half2)
    t3[...] = mm(w2_in[...], one_hot((k ^ (member * half2)) == g2 * half2 + o2)).astype(BF16)

    def rows_of(ref, a, c, size, total, group):
        at = [(9 * a + 3 * b + c) * total + (group ^ member) * size for b in range(3)]
        return [ref[pl.ds(pl.multiple_of(x, size), size), :] for x in at]

    row1 = lax.broadcasted_iota(jnp.int32, (half, wide1), 1) >> log2(mid)
    row2 = lax.broadcasted_iota(jnp.int32, (half, own1), 1) >> log2(half)
    row3 = digits(lax.broadcasted_iota(jnp.int32, (half, wide2), 1), 2, h2, half2)[1]
    row4 = lax.broadcasted_iota(jnp.int32, (half2, wide1), 1) >> (log2(mid) + 1)
    for a in range(3):
        for c in range(3):
            for g in range(2):
                tiles = rows_of(t1, a, c, half, mid, g)
                for r in range(h1):
                    band(f1, a, (g * 3 + c) * own1 + r * half, half, tiles, row1, (r + 1, r, r - 1))
                tiles = rows_of(t2, a, c, half, mid, g)
                for r in range(h1):
                    at = (c * h1 + r) * mid + g * half
                    band(b1, a, at, half, tiles, row2, (r - 1, r, r + 1))
                tiles = rows_of(t3, a, c, half, mid, g)
                for r in range(h2):
                    at = ((c * 2 + g) * h2 + r) * half
                    band(f2, a, at, half, tiles, row3, (r + 1, r, r - 1))
                tiles = rows_of(t4, a, c, half2, 2 * half2, g)
                for r in range(h2):
                    at = ((c * 2 + g) * h2 + r) * half2
                    band(b2, a, at, half2, tiles, row4, (r - 1, r, r + 1))


def spread_plane(d, x, xs, q):
    lanes = d.height * d.half
    before, after = shifted(x.astype(F32))
    xs[q, :, 0:lanes] = before.astype(BF16)
    xs[q, :, lanes : 2 * lanes] = x
    xs[q, :, 2 * lanes :] = after.astype(BF16)


def pool_matrix(d):
    k, n = iotas(d.height * d.mid, d.height2 * d.mid)
    r, o = digits(k, d.height, d.mid)
    g, i = digits(o, 2, d.half)
    return one_hot(n == (g * d.height2 + (r >> 1)) * d.half + i, 0.125)


def half_sum(d, xs, q, count, f1, g, pre):
    size = 3 * d.height * d.half
    for a in range(3):
        pre = pre + mm(xs[q + a - 1 : q + a - 1 + count].reshape(count * d.width, size), f1[a, g * size : (g + 1) * size])
    return pre


def first_level(d, pre, count, pool, slopes, rows, at):
    sig = jax.nn.sigmoid(pre)
    slopes[at : at + count] = slope_of(pre, sig).reshape(count, d.width, -1)
    rows[at : at + count] = mm((pre * sig).astype(BF16), pool).reshape(count, d.width, -1)


def pool_pair(d, rows, at, pair, k):
    width2 = d.width // 2
    pair[k] = rows[at] + rows[at + 1]
    return pair[k, pl.ds(0, width2, 2), :] + pair[k, pl.ds(1, width2, 2), :]


def pick(lower, even, a, b, outside):
    value = jnp.where(even, b, a) if lower else jnp.where(even, a, b)
    return jnp.where(outside, jnp.zeros_like(value), value)


def ends():
    place = lax.axis_index("depth")
    return place < BLOCK, place >= lax.axis_size("depth") - BLOCK


def middle_kernel(d, mi, mi_x, f1, xs, xs_x, slopes, rows, pooled, pair):
    per = BLOCK * d.planes
    for p in range(per):
        at = slice(p * d.width, (p + 1) * d.width)
        spread_plane(d, mi[at, :], xs, EDGE + p)
        spread_plane(d, mi_x[at, :], xs_x, EDGE + p)
    pool = pool_matrix(d)
    for q in range(1, per - 1, 3):
        pre = jnp.zeros((3 * d.width, d.height * d.mid), F32)
        for g, ref in enumerate((xs, xs_x)):
            pre = half_sum(d, ref, EDGE + q, 3, f1, g, pre)
        first_level(d, pre, 3, pool, slopes, rows, q - 1)
    for u in range(BLOCK - 2):
        pooled[u] = pool_pair(d, rows, 2 * u + 1, pair, u).astype(BF16)


def outer_kernel(d, a, b, a_x, b_x, xs_in, xs_x_in, f1, xs, xs_x, slopes, rows):
    del xs_in, xs_x_in
    per = BLOCK * d.planes
    even = parity()
    first, last = ends()
    for pair, ref in (((a, b), xs), ((a_x, b_x), xs_x)):
        for p in range(EDGE):
            x, y = (r[p * d.width : (p + 1) * d.width, :] for r in pair)
            spread_plane(d, pick(True, even, x, y, first), ref, p)
            spread_plane(d, pick(False, even, x, y, last), ref, EDGE + per + p)
    pool = pool_matrix(d)
    for k, q in enumerate((1, per + EDGE - 1)):
        pre = jnp.zeros((3 * d.width, d.height * d.mid), F32)
        for g, ref in enumerate((xs, xs_x)):
            pre = half_sum(d, ref, q, 3, f1, g, pre)
        first_level(d, pre, 3, pool, slopes, rows, 3 * k)


def main_kernel(
    d, a, mi, b, a_x, mi_x, b_x, xs, slopes_mid, rows_mid, slopes_out, rows_out, pooled_a, pooled, pooled_b,
    f2, b2, grads_out, sums_out, cs, sl, rows, pair, zs, gs, up, g1,
):
    place = lax.axis_index("depth")
    first, last = ends()
    even = parity()
    planes, width, wide1 = d.planes, d.width, d.height * d.mid
    width2 = width // 2
    own1 = d.height * d.half
    wide2 = d.height2 * 2 * d.half2
    own2 = d.height2 * d.half2
    zl = d.height2 * d.mid
    per = BLOCK * planes

    side = EDGE * width
    for g, (x, m, y) in enumerate(((a, mi, b), (a_x, mi_x, b_x))):
        lanes = slice(g * own2, (g + 1) * own2)
        x, y = x[side:, :], y[side:, :]
        cs[0:2, :, lanes] = pick(True, even, x, y, first).reshape(2, width2, own2)
        cs[2 : 2 + BLOCK, :, lanes] = m[per * width :, :].reshape(BLOCK, width2, own2)
        cs[2 + BLOCK :, :, lanes] = pick(False, even, x, y, last).reshape(2, width2, own2)
    inner = per - 2
    for ref, outer, middle in ((sl, slopes_out, slopes_mid), (rows, rows_out, rows_mid)):
        ref[0:3] = outer[0:3]
        ref[3 : 3 + inner] = middle[...]
        ref[3 + inner :] = outer[3:6]
    for u in range(3 * BLOCK - 2):
        coarse = 1 + u
        if coarse < BLOCK - 1:
            k = coarse - 1
            cell = pick(True, even, pooled_a[k], pooled_b[k], first).astype(F32)
        elif coarse > 2 * BLOCK:
            k = coarse - 2 * BLOCK - 1
            cell = pick(False, even, pooled_a[k], pooled_b[k], last).astype(F32)
        elif BLOCK < coarse < 2 * BLOCK - 1:
            cell = pooled[coarse - BLOCK - 1].astype(F32)
        else:
            cell = pool_pair(d, rows, 2 * coarse - per + 2, pair, u)
        if coarse == BLOCK - 1:
            cell = jnp.where(first, 0.0, cell)
        if coarse == 2 * BLOCK:
            cell = jnp.where(last, 0.0, cell)
        before, after = shifted(cell)
        zs[u, :, 0:zl] = before.astype(BF16)
        zs[u, :, zl : 2 * zl] = cell.astype(BF16)
        zs[u, :, 2 * zl :] = after.astype(BF16)

    count = BLOCK + 4
    pre = jnp.zeros((count * width2, wide2), F32)
    for a in range(3):
        pre += mm(zs[a : a + count].reshape(count * width2, 3 * zl), f2[a])
    sig = jax.nn.sigmoid(pre)
    grad_two = cs[...].reshape(count * width2, wide2).astype(F32) * slope_of(pre, sig)
    for u in range(count):
        g = grad_two[u * width2 : (u + 1) * width2]
        before, after = shifted(g)
        gs[u, :, 0:wide2] = after.astype(BF16)
        gs[u, :, wide2 : 2 * wide2] = g.astype(BF16)
        gs[u, :, 2 * wide2 :] = before.astype(BF16)

    inner = count - 2
    back = jnp.zeros((inner * width2, wide1), F32)
    for a in range(3):
        back += mm(gs[2 - a : 2 - a + inner].reshape(inner * width2, 3 * wide2), b2[a])
    pieces = wide1 // 128
    for u in range(inner):
        b = back[u * width2 : (u + 1) * width2]
        for piece in range(pieces):
            lanes = slice(piece * 128, (piece + 1) * 128)
            up[u * pieces + piece, pl.ds(0, width2, 2), :] = b[:, lanes]
            up[u * pieces + piece, pl.ds(1, width2, 2), :] = b[:, lanes]
    for u in range(per + 2):
        q = per - 1 + u
        both = [up[(q - 6) // 2 * pieces + piece] for piece in range(pieces)]
        g = jnp.concatenate(both, axis=1) * sl[q - per + 2]
        if q < per:
            g = jnp.where(first, 0.0, g)
        if q >= 2 * per:
            g = jnp.where(last, 0.0, g)
        g1[u] = g.astype(BF16)
    grads_out[...] = g1[pl.ds((place & (BLOCK - 1)) * planes, planes + 2)]

    def collect(parts, groups, height, chans, base):
        lane = lax.broadcasted_iota(jnp.int32, (chans, 128), 1)
        tap_row = lane >> log2(d.half)
        for g in range(groups):
            def total(m):
                out = jnp.zeros((chans, 128), F32)
                for r in range(height):
                    at = (g * height + r) * chans
                    tile = parts[m // 3][at : at + chans, (m % 3) * 128 : (m % 3 + 1) * 128]
                    tile = pltpu.roll(tile, (1 - r) * d.half % 128, 1)
                    if r == 0:
                        tile = jnp.where(tap_row == 0, 0.0, tile)
                    if r == height - 1:
                        tile = jnp.where(tap_row == 2, 0.0, tile)
                    out += tile
                return out

            def turned(x, lanes):
                return pltpu.roll(x, lanes % 128, 1) if lanes % 128 else x

            extra = total(8)
            for tile in range(4):
                out = jnp.where(lane < 3 * d.half, total(2 * tile), turned(total(2 * tile + 1), 3 * d.half))
                if tile == 0:
                    out = jnp.where(lane < 6 * d.half, out, turned(extra, 6 * d.half))
                if tile == 1:
                    out = jnp.where(lane < 6 * d.half, out, turned(extra, 4 * d.half))
                at = base + (g * 4 + tile) * chans
                sums_out[at : at + chans, :] = out.astype(BF16)

    center = g1[1 : 1 + per].reshape(per * width, wide1)
    parts = [
        mm_t(center, xs[EDGE + a - 1 : EDGE + a - 1 + per].reshape(per * width, 3 * own1))
        for a in range(3)
    ]
    collect(parts, 1, d.height, d.mid, 0)
    center = gs[2 : 2 + BLOCK, :, wide2 : 2 * wide2].reshape(BLOCK * width2, wide2)
    parts = [mm_t(center, zs[2 + a : 2 + a + BLOCK].reshape(BLOCK * width2, 3 * zl)) for a in range(3)]
    collect(parts, 2, d.height2, d.half2, 4 * d.mid)


def feats_kernel(d, g1, b1, out, wide):
    planes, width, wide1 = d.planes, d.width, d.height * d.mid
    for u in range(planes + 2):
        g = g1[u]
        before, after = shifted(g.astype(F32))
        wide[u, :, 0:wide1] = after.astype(BF16)
        wide[u, :, wide1 : 2 * wide1] = g
        wide[u, :, 2 * wide1 :] = before.astype(BF16)
    grad = jnp.zeros((planes * width, d.height * d.half), F32)
    for a in range(3):
        grad += mm(wide[2 - a : 2 - a + planes].reshape(planes * width, 3 * wide1), b1[a])
    grad = grad.astype(BF16)
    grad = jnp.concatenate([grad[p * width : (p + 1) * width] for p in range(planes)], axis=1)
    turn = order_matrix(d.half, planes, d.height)
    out[...] = lax.dot_general(turn, grad, (((1,), (1,)), ((), ())), preferred_element_type=F32).astype(BF16)


def final_kernel(d, *refs):
    member = lax.axis_index("chan")
    parts, (out1, out2) = refs[:-2], refs[-2:]
    terms = [p[...].astype(F32) for p in parts]
    while len(terms) > 1:
        terms = [terms[i] + terms[i + 1] for i in range(0, len(terms), 2)]
    total = terms[0]
    half = d.half

    def lay_out(base, groups, chans, out):
        full = groups * chans
        for tile in range(4):
            rows = [total[base + (g * 4 + tile) * chans : base + (g * 4 + tile + 1) * chans] for g in range(groups)]
            rows = jnp.concatenate(rows, axis=0) if groups > 1 else rows[0]
            flat = pltpu.roll(rows, member * (full // 2), 0).T
            spots = [(2 * tile, b, b) for b in range(3)] + [(2 * tile + 1, b, 3 + b) for b in range(3)]
            spots += {0: [(8, 0, 6), (8, 1, 7)], 1: [(8, 2, 6)]}.get(tile, [])
            for m, b, spot in spots:
                tap = 9 * (m // 3) + 3 * b + m % 3
                out[tap * half : (tap + 1) * half, :] = flat[spot * half : (spot + 1) * half]

    lay_out(0, 1, d.mid, out1)
    lay_out(4 * d.mid, 2, d.half2, out2)


class Sizes:
    pass


def shards(feats, weight_one, weight_two, cotangent):
    d = Sizes()
    slabs = lax.axis_size("depth")
    assert lax.axis_size("chan") == 2 and slabs % BLOCK == 0
    d.half, d.planes, d.height, d.width = feats.shape
    d.half2, coarse, d.height2, width2 = cotangent.shape
    d.mid = weight_one.shape[0]
    assert d.planes == 2 and coarse == 1 and d.half * 8 == 128 and d.height2 * d.half2 == 128
    assert d.width == 128 and d.height == 8 and d.mid == 32
    blocks = slabs // BLOCK
    per = BLOCK * d.planes
    wide1 = d.height * d.mid
    own1 = d.height * d.half
    wide2 = d.height2 * 2 * d.half2
    zl = d.height2 * d.mid

    def call(kernel, outs, scratch=(), flops=0, ins=None, mib=40, aliases=None):
        def run(*args):
            return pl.pallas_call(
                functools.partial(kernel, d),
                out_shape=[jax.ShapeDtypeStruct(shape, dtype) for shape, dtype in outs],
                in_specs=[pl.BlockSpec(memory_space=ins or pltpu.VMEM)] * len(args),
                out_specs=[VMEM] * len(outs),
                scratch_shapes=list(scratch),
                input_output_aliases=aliases or {},
                compiler_params=pltpu.CompilerParams(vmem_limit_bytes=mib << 20),
                cost_estimate=pl.CostEstimate(flops=flops, bytes_accessed=1 << 20, transcendentals=0),
            )(*args)

        return run

    rows = d.planes * d.width + width2
    feats_shape = (d.half * d.planes * d.height, d.width)
    (item,) = call(
        pack_kernel,
        [((rows, 128), BF16)],
        [
            pltpu.VMEM(feats_shape, BF16),
            pltpu.VMEM((d.half2 * d.height2, width2), BF16),
            pltpu.SemaphoreType.DMA((2,)),
        ],
        ins=pltpu.HBM,
        mib=24,
    )(feats.reshape(feats_shape), cotangent.reshape(-1, width2))

    def xor(x, k):
        return lax.ppermute(x, "depth", [(i, i ^ k) for i in range(slabs)])

    def gather(k):
        return xor(item, k)

    def swap(x):
        return lax.ppermute(x, "chan", [(0, 1), (1, 0)])

    side_rows = EDGE * d.width + 2 * width2
    mid, to_a, to_b = call(
        sort_kernel, [((BLOCK * rows, 128), BF16), ((side_rows, 128), BF16), ((side_rows, 128), BF16)]
    )(item, *[gather(k) for k in range(1, BLOCK)])
    pair_a = [(i, i ^ BLOCK) for i in range(slabs)]
    inside = range(BLOCK, slabs - BLOCK)
    pair_b = [(i, ((i - BLOCK) ^ BLOCK) + BLOCK if i in inside else i) for i in range(slabs)]

    def trade(x_a, x_b):
        a = lax.ppermute(x_a, "depth", pair_a)
        b = lax.ppermute(x_b, "depth", pair_b)
        return a, b

    a, b = trade(to_a, to_b)
    mid_x, a_x, b_x = swap(mid), swap(a), swap(b)

    w1 = jnp.transpose(weight_one, (2, 0, 1)).reshape(27 * d.mid, d.mid)
    w2 = jnp.transpose(weight_two, (2, 1, 0)).reshape(27 * d.mid, 2 * d.half2)
    f1, b1, f2, b2 = call(
        weight_kernel,
        [
            ((3, 6 * own1, wide1), BF16),
            ((3, 3 * wide1, own1), BF16),
            ((3, 3 * zl, wide2), BF16),
            ((3, 3 * wide2, wide1), BF16),
        ],
        [
            pltpu.VMEM(w1.shape, BF16),
            pltpu.VMEM(w2.shape, BF16),
            pltpu.VMEM((27 * d.mid, wide1), BF16),
            pltpu.VMEM((27 * d.mid, own1), BF16),
            pltpu.VMEM((27 * d.mid, wide2), BF16),
            pltpu.VMEM((27 * 2 * d.half2, wide1), BF16),
            pltpu.SemaphoreType.DMA((2,)),
        ],
        flops=1 << 30,
        ins=pltpu.HBM,
        mib=24,
    )(w1, w2)
    xs_mid, xs_mid_x, slopes_mid, rows_mid, pooled = call(
        middle_kernel,
        [
            ((per + 2 * EDGE, d.width, 3 * own1), BF16),
            ((per + 2 * EDGE, d.width, 3 * own1), BF16),
            ((per - 2, d.width, wide1), F32),
            ((per - 2, d.width, zl), F32),
            ((BLOCK - 2, width2, zl), BF16),
        ],
        [pltpu.VMEM((BLOCK - 2, d.width, zl), F32)],
        flops=1 << 30,
    )(mid, mid_x, f1)
    pooled_a, pooled_b = trade(pooled, pooled)
    xs, _, slopes_out, rows_out = call(
        outer_kernel,
        [
            ((per + 2 * EDGE, d.width, 3 * own1), BF16),
            ((per + 2 * EDGE, d.width, 3 * own1), BF16),
            ((6, d.width, wide1), F32),
            ((6, d.width, zl), F32),
        ],
        flops=1 << 30,
        aliases={4: 0, 5: 1},
    )(a, b, a_x, b_x, xs_mid, xs_mid_x, f1)

    grads, sums = call(
        main_kernel,
        [((d.planes + 2, d.width, wide1), BF16), ((4 * d.mid + 8 * d.half2, 128), BF16)],
        [
            pltpu.VMEM((BLOCK + 4, width2, wide2), BF16),
            pltpu.VMEM((per + 4, d.width, wide1), F32),
            pltpu.VMEM((per + 4, d.width, zl), F32),
            pltpu.VMEM((3 * BLOCK - 2, d.width, zl), F32),
            pltpu.VMEM((3 * BLOCK - 2, width2, 3 * zl), BF16),
            pltpu.VMEM((BLOCK + 4, width2, 3 * wide2), BF16),
            pltpu.VMEM(((BLOCK + 2) * (wide1 // 128), d.width, 128), F32),
            pltpu.VMEM((per + 2, d.width, wide1), BF16),
        ],
        flops=1 << 32,
    )(a, mid, b, a_x, mid_x, b_x, xs, slopes_mid, rows_mid, slopes_out, rows_out, pooled_a, pooled, pooled_b, f2, b2)

    parts = [sums]
    radix = 1
    while radix < blocks:
        fan = min(4, blocks // radix)
        mine = parts[0] if len(parts) == 1 else sum_parts(parts)
        parts = [mine] + [xor(mine, BLOCK * radix * k) for k in range(1, fan)]
        radix *= fan
    (grad,) = call(
        feats_kernel, [(feats_shape, BF16)], [pltpu.VMEM((d.planes + 2, d.width, 3 * wide1), BF16)], flops=1 << 30
    )(grads, b1)
    out1, out2 = call(final_kernel, [((27 * d.half, d.mid), F32), ((27 * d.half, 2 * d.half2), F32)])(*parts)
    return (
        grad.reshape(feats.shape),
        out1.reshape(27, d.half, d.mid).transpose(2, 1, 0),
        out2.reshape(27, d.half, 2 * d.half2).transpose(2, 1, 0),
    )


def sum_parts(parts):
    terms = [p.astype(F32) for p in parts]
    while len(terms) > 1:
        terms = [terms[i] + terms[i + 1] for i in range(0, len(terms), 2)]
    return terms[0].astype(BF16)


def solution(mesh):
    return jax.shard_map(
        shards,
        mesh=mesh,
        in_specs=(P("chan", "depth", None, None), P(), P(), P("chan", "depth", None, None)),
        out_specs=(P("chan", "depth", None, None), P(None, "chan", None), P(None, "chan", None)),
        check_vma=False,
    )
```

time: 239 us -> 51.6 us (0.22)
  blocking collectives: 81.9 us -> 0 us
  local copies, waits for them, and re-layouts: 51.5 us -> 3.46 us
  waiting for transfers between devices: 48.4 us -> 13.6 us
  Pallas kernels: 0 us -> 13.7 us
  between operations: 14.3 us -> 0.74 us
  matrix products: 10.5 us -> 0 us
  other arithmetic: 6.83 us -> 0 us
  starting transfers between devices: 23.7 us -> 19.8 us
    psum x1 -> x0, blocking collectives: 77.8 us -> none  [shards(): grad_weight_one = lax.psum(grad_weight_one, 'depth')]
    another operation x32 -> x0, local copies, waits for them, and re-layouts: 28.5 us -> none  [patch_rows(): return jnp.stack(windows, 0).reshape(27 * chans, planes * height * across)]
    reduce_scatter x2 -> x0, waiting for transfers between devices: 21 us -> none  [the longest x1 11.3 us: shards(): lax.psum_scatter(partial_two.astype(jnp.bfloat16), 'chan', scatter_dimens...]
    psum x1 -> x0, waiting for transfers between devices: 17.6 us -> none  [shards(): grad_weight_two = lax.psum(grad_weight_two, 'depth')]
    pallas_call x0 -> x8, Pallas kernels: none -> 13.7 us  [run(): pl.pallas_call(functools.partial(kernel, d), out_shape=[jax.ShapeDtypeStr...]
    dot_general x6 -> x0, matrix products: 10.5 us -> none  [the longest x2 3.84 us: grad_fold(): lax.dot_general(inner, patches, (((1,), (1,)), ((), ())), preferred_eleme...]
    reshape x8 -> x0, local copies, waits for them, and re-layouts: 6.17 us -> none  [the longest x2 4.1 us: patch_rows(): return jnp.stack(windows, 0).reshape(27 * chans, planes * height * across)]
    unnamed x51 -> x8, local copies, waits for them, and re-layouts: 8.2 us -> 3.46 us
  transfers between devices with their start and end apart: 11 -> 13, of which waited for: 7 -> 6; matrix products, arithmetic and copies ran while one was open for 6% -> 0% of each run, Pallas kernels for 0% -> 17%
where the time goes in v2:
time: 51.6 us; the launch traced here: 51.3 us
  starting transfers between devices  19.8 us (38%)
  Pallas kernels  13.7 us (27%)
  waiting for transfers between devices  13.6 us (26%)
  local copies, waits for them, and re-layouts  3.46 us (7%)
  between operations  0.74 us (1%)
    pallas_call x8, Pallas kernels, run(): pl.pallas_call(functools.partial(kernel, d), out_shape=[jax.ShapeDtypeStr...  13.7 us
    ppermute x6, waiting for transfers between devices, xor(): return lax.ppermute(x, 'depth', [(i, i ^ k) for i in range(slabs)])  10 us
    ppermute x6, starting transfers between devices, xor(): return lax.ppermute(x, 'depth', [(i, i ^ k) for i in range(slabs)])  9.08 us
    ppermute x2, starting transfers between devices, trade(): a = lax.ppermute(x_a, 'depth', pair_a)  8.77 us
    ppermute x2, waiting for transfers between devices, trade(): a = lax.ppermute(x_a, 'depth', pair_a)  3.6 us
    unnamed x8, local copies, waits for them, and re-layouts  3.46 us
    ppermute x2, starting transfers between devices, trade(): b = lax.ppermute(x_b, 'depth', pair_b)  1.32 us
  transfers between devices with their start and end apart: 13, of which 6 were waited for; matrix products, arithmetic and copies ran while one was open for 0% of the time, Pallas kernels for 17%

profile of v2, /device:TPU:0, one launch (start us, length us, event | category | flops | bytes accessed | tf_op | source)
XLA Modules:
  0.0 51.3 jit_solution(5598415652640690060)
XLA Ops:
  0.6 0.8 %copy-done = bf16[16,2,8,128]{3,2,1,0:T(8,128)(2,1)S(1)} copy-done((bf16[16,2,8,128]{3,2,1,0:T(8,128)(2,1)S(1)}, bf16[16,2,8,128]{3,2,1,0:T(8,128)(2,1)}, u32[]{:S(2)}) %copy-start) | copy-done | bytes 65560
  1.5 0.8 %copy-done.1 = bf16[32,1,4,64]{3,2,1,0:T(4,128)(2,1)S(1)} copy-done((bf16[32,1,4,64]{3,2,1,0:T(4,128)(2,1)S(1)}, bf16[32,1,4,64]{3,2,1,0:T(4,128)(2,1)}, u32[]{:S(2)}) %copy-start.1) | copy-done | bytes 16408
  2.2 0.6 %shard_map.67.i0 = bf16[320,128]{1,0:T(8,128)(2,1)S(1)} custom-call(bf16[256,128]{1,0:T(8,128)(2,1)S(1)} %bitcast.15, bf16[128,64]{1,0:T(8,128)(2,1)S(1)} %bitcast.16), custom_call_target="tpu_custom_call" | custom-call | bytes 1048576 | tf_op jit(solution)/shard_map/pallas_call | solution.py:432
  2.8 4.0 %collective-permute-start.2 = (bf16[320,128]{1,0:T(8,128)(2,1)S(1)}, bf16[320,128]{1,0:T(8,128)(2,1)S(1)}, u32[]{:S(2)}, u32[]{:S(2)}) collective-permute-start(bf16[320,128]{1,0:T(8,128)(2,1)S(1)} %shard_map.67.i0), channel_id=1, source_target_pairs={{0,6},{2,4},{4,2},{6,0},{8,14},{10,12},{12,10},{14,8},{16,22},{18,... | collective-permute-start | bytes 245768 | tf_op jit(solution)/shard_map/ppermute | solution.py:460
  6.8 0.5 collective-permute-start.1
  7.3 0.1 collective-permute-start
  7.4 1.9 %collective-permute-done.2.i3 = bf16[320,128]{1,0:T(8,128)(2,1)S(1)} collective-permute-done((bf16[320,128]{1,0:T(8,128)(2,1)S(1)}, bf16[320,128]{1,0:T(8,128)(2,1)S(1)}, u32[]{:S(2)}, u32[]{:S(2)}) %collective-permute-start.2) | collective-permute-done | bytes 81952 | tf_op jit(solution)/shard_map/ppermute | solution.py:460
  9.4 1.9 %collective-permute-done.1.i2 = bf16[320,128]{1,0:T(8,128)(2,1)S(1)} collective-permute-done((bf16[320,128]{1,0:T(8,128)(2,1)S(1)}, bf16[320,128]{1,0:T(8,128)(2,1)S(1)}, u32[]{:S(2)}, u32[]{:S(2)}) %collective-permute-start.1) | collective-permute-done | bytes 81952 | tf_op jit(solution)/shard_map/ppermute | solution.py:460
  11.2 0.5 collective-permute-done.i1
  11.7 0.1 shard_map.68
  11.8 0.1 collective-permute-start.6
  11.9 1.6 %collective-permute-start.3 = (bf16[512,128]{1,0:T(8,128)(2,1)S(1)}, bf16[512,128]{1,0:T(8,128)(2,1)S(1)}, u32[]{:S(2)}, u32[]{:S(2)}) collective-permute-start(bf16[512,128]{1,0:T(8,128)(2,1)S(1)} %get-tuple-element.22), channel_id=1, source_target_pairs={{0,8},{2,10},{4,12},{6,14},{8,0},{10,2},{12,4},{14,6},{16,24},{18,... | collective-permute-start | bytes 393224 | tf_op jit(solution)/shard_map/ppermute | solution.py:477
  13.5 0.7 %collective-permute-start.4 = (bf16[512,128]{1,0:T(8,128)(2,1)S(1)}, bf16[512,128]{1,0:T(8,128)(2,1)S(1)}, u32[]{:S(2)}, u32[]{:S(2)}) collective-permute-start(bf16[512,128]{1,0:T(8,128)(2,1)S(1)} %get-tuple-element.24), channel_id=1, source_target_pairs={{0,0},{2,2},{4,4},{6,6},{8,16},{10,18},{12,20},{14,22},{16,8},{18,... | collective-permute-start | bytes 393224 | tf_op jit(solution)/shard_map/ppermute | solution.py:478
  14.2 3.6 %collective-permute-done.3.a = bf16[512,128]{1,0:T(8,128)(2,1)S(1)} collective-permute-done((bf16[512,128]{1,0:T(8,128)(2,1)S(1)}, bf16[512,128]{1,0:T(8,128)(2,1)S(1)}, u32[]{:S(2)}, u32[]{:S(2)}) %collective-permute-start.3) | collective-permute-done | bytes 131104 | tf_op jit(solution)/shard_map/ppermute | solution.py:477
  17.8 0.0 collective-permute-start.5
  17.8 0.0 collective-permute-done.4.b
  17.8 0.5 collective-permute-start.7
  18.3 0.9 %copy-done.2 = bf16[32,32,27]{1,0,2:T(8,128)(2,1)S(1)} copy-done((bf16[32,32,27]{1,0,2:T(8,128)(2,1)S(1)}, bf16[32,32,27]{1,0,2:T(8,128)(2,1)}, u32[]{:S(2)}) %copy-start.2) | copy-done | bytes 55320
  19.2 0.9 %copy-done.3 = bf16[64,32,27]{0,1,2:T(8,128)(2,1)S(1)} copy-done((bf16[64,32,27]{0,1,2:T(8,128)(2,1)S(1)}, bf16[64,32,27]{0,1,2:T(8,128)(2,1)}, u32[]{:S(2)}) %copy-start.3) | copy-done | bytes 110616
  20.2 1.7 %shard_map.69 = (bf16[3,768,256]{2,1,0:T(8,128)(2,1)S(1)}, bf16[3,768,128]{2,1,0:T(8,128)(2,1)S(1)}, bf16[3,384,256]{2,1,0:T(8,128)(2,1)S(1)}, bf16[3,768,256]{2,1,0:T(8,128)(2,1)S(1)}) custom-call(bf16[864,32]{1,0:T(8,128)(2,1)S(1)} %bitcast.17, bf16[864,64]{1,0:T(8,128)(2,1)S(1)} %bitcast.18), custom_call_target="tpu_custom_call" | custom-call | flops 1073741824 | bytes 1048576 | tf_op jit(solution)/shard_map/pallas_call | solution.py:432
  21.8 2.9 %shard_map.70 = (bf16[14,128,384]{2,1,0:T(8,128)(2,1)S(1)}, bf16[14,128,384]{2,1,0:T(8,128)(2,1)S(1)}, f32[6,128,256]{2,1,0:T(8,128)S(1)}, f32[6,128,128]{2,1,0:T(8,128)S(1)}, bf16[2,64,128]{2,1,0:T(8,128)(2,1)S(1)}) custom-call(bf16[1280,128]{1,0:T(8,128)(2,1)S(1)} %get-tuple-element.23.mi, bf16[1280,128]{1,0:T(8,128)(2,1)S(1)} %collective-permute-done.6.mi_x, ...), custom_call_target="tpu_custom_call" | custom-call | flops 1073741824 | bytes 1048576 | tf_op jit(solution)/shard_map/pallas_call | solution.py:432
  24.7 0.7 %collective-permute-start.9 = (bf16[2,64,128]{2,1,0:T(8,128)(2,1)S(1)}, bf16[2,64,128]{2,1,0:T(8,128)(2,1)S(1)}, u32[]{:S(2)}, u32[]{:S(2)}) collective-permute-start(bf16[2,64,128]{2,1,0:T(8,128)(2,1)S(1)} %get-tuple-element.33.pooled), channel_id=1, source_target_pairs={{0,0},{2,2},{4,4},{6,6},{8,16},{10,18},{12,20},{14,22},{16,8},{18,... | collective-permute-start | bytes 98312 | tf_op jit(solution)/shard_map/ppermute | solution.py:478
  25.4 7.1 %collective-permute-start.8 = (bf16[2,64,128]{2,1,0:T(8,128)(2,1)S(1)}, bf16[2,64,128]{2,1,0:T(8,128)(2,1)S(1)}, u32[]{:S(2)}, u32[]{:S(2)}) collective-permute-start(bf16[2,64,128]{2,1,0:T(8,128)(2,1)S(1)} %get-tuple-element.33.pooled), channel_id=1, source_target_pairs={{0,8},{2,10},{4,12},{6,14},{8,0},{10,2},{12,4},{14,6},{16,24},{18,... | collective-permute-start | bytes 98312 | tf_op jit(solution)/shard_map/ppermute | solution.py:477
  32.5 2.8 %shard_map.71 = (bf16[14,128,384]{2,1,0:T(8,128)(2,1)S(1)}, bf16[14,128,384]{2,1,0:T(8,128)(2,1)S(1)}, f32[6,128,256]{2,1,0:T(8,128)S(1)}, f32[6,128,128]{2,1,0:T(8,128)S(1)}) custom-call(bf16[512,128]{1,0:T(8,128)(2,1)S(1)} %collective-permute-done.3.a, ...), custom_call_target="tpu_custom_call", output_to_operand_aliasing={{0}: (4, {}), {1}: (5, {})} | custom-call | flops 1073741824 | bytes 1048576 | tf_op jit(solution)/shard_map/pallas_call | solution.py:432
  35.4 3.5 %shard_map.72 = (bf16[4,128,256]{2,1,0:T(8,128)(2,1)S(1)}, bf16[384,128]{1,0:T(8,128)(2,1)S(1)}) custom-call(bf16[512,128]{1,0:T(8,128)(2,1)S(1)} %collective-permute-done.3.a, bf16[1280,128]{1,0:T(8,128)(2,1)S(1)} %get-tuple-element.23.mi, bf16[512,128]{1,0:T(8,128)(2,1)S(1)} %collective-permute-done.4.b, bf16[512,128]{1,0:T(8,128)(2,1)S(1)} %collective-permute-done.5.a_x, ...), custom_call_target="tpu_custom_call" | custom-call | flops 4294967296 | bytes 1048576 | tf_op jit(solution)/shard_map/pallas_call | solution.py:432
  38.9 1.3 %collective-permute-start.12 = (bf16[384,128]{1,0:T(8,128)(2,1)S(1)}, bf16[384,128]{1,0:T(8,128)(2,1)S(1)}, u32[]{:S(2)}, u32[]{:S(2)}) collective-permute-start(bf16[384,128]{1,0:T(8,128)(2,1)S(1)} %get-tuple-element.38.refs_0_), channel_id=1, source_target_pairs={{0,24},{2,26},{4,28},{6,30},{8,16},{10,18},{12,20},{14,22},{16,8},... | collective-permute-start | bytes 294920 | tf_op jit(solution)/shard_map/ppermute | solution.py:460
  40.1 1.3 %collective-permute-start.11 = (bf16[384,128]{1,0:T(8,128)(2,1)S(1)}, bf16[384,128]{1,0:T(8,128)(2,1)S(1)}, u32[]{:S(2)}, u32[]{:S(2)}) collective-permute-start(bf16[384,128]{1,0:T(8,128)(2,1)S(1)} %get-tuple-element.38.refs_0_), channel_id=1, source_target_pairs={{0,16},{2,18},{4,20},{6,22},{8,24},{10,26},{12,28},{14,30},{16,0},... | collective-permute-start | bytes 294920 | tf_op jit(solution)/shard_map/ppermute | solution.py:460
  41.4 1.9 %collective-permute-start.10 = (bf16[384,128]{1,0:T(8,128)(2,1)S(1)}, bf16[384,128]{1,0:T(8,128)(2,1)S(1)}, u32[]{:S(2)}, u32[]{:S(2)}) collective-permute-start(bf16[384,128]{1,0:T(8,128)(2,1)S(1)} %get-tuple-element.38.refs_0_), channel_id=1, source_target_pairs={{0,8},{2,10},{4,12},{6,14},{8,0},{10,2},{12,4},{14,6},{16,24},{18,... | collective-permute-start | bytes 294920 | tf_op jit(solution)/shard_map/ppermute | solution.py:460
  43.3 1.3 %shard_map.73 = bf16[256,128]{1,0:T(8,128)(2,1)} custom-call(bf16[4,128,256]{2,1,0:T(8,128)(2,1)S(1)} %get-tuple-element.36.g1, bf16[3,768,128]{2,1,0:T(8,128)(2,1)S(1)} %get-tuple-element.37.b1), custom_call_target="tpu_custom_call" | custom-call | flops 1073741824 | bytes 1048576 | tf_op jit(solution)/shard_map/pallas_call | solution.py:432
  44.6 1.8 %collective-permute-done.12.refs_3_ = bf16[384,128]{1,0:T(8,128)(2,1)S(1)} collective-permute-done((bf16[384,128]{1,0:T(8,128)(2,1)S(1)}, bf16[384,128]{1,0:T(8,128)(2,1)S(1)}, u32[]{:S(2)}, u32[]{:S(2)}) %collective-permute-start.12) | collective-permute-done | bytes 98336 | tf_op jit(solution)/shard_map/ppermute | solution.py:460
  46.5 3.9 %collective-permute-done.11.refs_2_ = bf16[384,128]{1,0:T(8,128)(2,1)S(1)} collective-permute-done((bf16[384,128]{1,0:T(8,128)(2,1)S(1)}, bf16[384,128]{1,0:T(8,128)(2,1)S(1)}, u32[]{:S(2)}, u32[]{:S(2)}) %collective-permute-start.11) | collective-permute-done | bytes 98336 | tf_op jit(solution)/shard_map/ppermute | solution.py:460
  50.3 0.9 %shard_map.74 = (f32[432,32]{1,0:T(8,128)}, f32[432,64]{1,0:T(8,128)}) custom-call(bf16[384,128]{1,0:T(8,128)(2,1)S(1)} %get-tuple-element.38.refs_0_, bf16[384,128]{1,0:T(8,128)(2,1)S(1)} %collective-permute-done.10.refs_1_, bf16[384,128]{1,0:T(8,128)(2,1)S(1)} %collective-permute-done.11.refs_2_, bf16[384,128]{1,0:T(8,128)(2,1)S(1)} %collective-permute-done.12.refs_3_), custom_call_target="tpu_custom_call" | custom-call | bytes 1048576 | tf_op jit(solution)/shard_map/pallas_call | solution.py:432
  (10 shorter events, 0.0 us)
Async XLA Ops:
  0.6 0.8 %copy-start = (bf16[16,2,8,128]{3,2,1,0:T(8,128)(2,1)S(1)}, bf16[16,2,8,128]{3,2,1,0:T(8,128)(2,1)}, u32[]{:S(2)}) copy-start(bf16[16,2,8,128]{3,2,1,0:T(8,128)(2,1)} %param.4) | copy-start | bytes 196612
  1.5 0.8 %copy-start.1 = (bf16[32,1,4,64]{3,2,1,0:T(4,128)(2,1)S(1)}, bf16[32,1,4,64]{3,2,1,0:T(4,128)(2,1)}, u32[]{:S(2)}) copy-start(bf16[32,1,4,64]{3,2,1,0:T(4,128)(2,1)} %param.7) | copy-start | bytes 49156
  2.8 6.6 %collective-permute-start.2 = (bf16[320,128]{1,0:T(8,128)(2,1)S(1)}, bf16[320,128]{1,0:T(8,128)(2,1)S(1)}, u32[]{:S(2)}, u32[]{:S(2)}) collective-permute-start(bf16[320,128]{1,0:T(8,128)(2,1)S(1)} %shard_map.67.i0), channel_id=1, source_target_pairs={{0,6},{2,4},{4,2},{6,0},{8,14},{10,12},{12,10},{14,8},{16,22},{18,... | collective-permute-start | bytes 245768 | tf_op jit(solution)/shard_map/ppermute | solution.py:460
  6.8 4.4 %collective-permute-start.1 = (bf16[320,128]{1,0:T(8,128)(2,1)S(1)}, bf16[320,128]{1,0:T(8,128)(2,1)S(1)}, u32[]{:S(2)}, u32[]{:S(2)}) collective-permute-start(bf16[320,128]{1,0:T(8,128)(2,1)S(1)} %shard_map.67.i0), channel_id=1, source_target_pairs={{0,4},{2,6},{4,0},{6,2},{8,12},{10,14},{12,8},{14,10},{16,20},{18,... | collective-permute-start | bytes 245768 | tf_op jit(solution)/shard_map/ppermute | solution.py:460
  7.3 4.4 %collective-permute-start = (bf16[320,128]{1,0:T(8,128)(2,1)S(1)}, bf16[320,128]{1,0:T(8,128)(2,1)S(1)}, u32[]{:S(2)}, u32[]{:S(2)}) collective-permute-start(bf16[320,128]{1,0:T(8,128)(2,1)S(1)} %shard_map.67.i0), channel_id=1, source_target_pairs={{0,2},{2,0},{4,6},{6,4},{8,10},{10,8},{12,14},{14,12},{16,18},{18,... | collective-permute-start | bytes 245768 | tf_op jit(solution)/shard_map/ppermute | solution.py:460
  11.8 10.0 %collective-permute-start.6 = (bf16[1280,128]{1,0:T(8,128)(2,1)S(1)}, bf16[1280,128]{1,0:T(8,128)(2,1)S(1)}, u32[]{:S(2)}, u32[]{:S(2)}) collective-permute-start(bf16[1280,128]{1,0:T(8,128)(2,1)S(1)} %get-tuple-element.23.mi), channel_id=1, source_target_pairs={{0,1},{1,0},{2,3},{3,2},{4,5},{5,4},{6,7},{7,6},{8,9},{9,8},{10,11... | collective-permute-start | bytes 983048 | tf_op jit(solution)/shard_map/ppermute | solution.py:466
  11.9 5.9 %collective-permute-start.3 = (bf16[512,128]{1,0:T(8,128)(2,1)S(1)}, bf16[512,128]{1,0:T(8,128)(2,1)S(1)}, u32[]{:S(2)}, u32[]{:S(2)}) collective-permute-start(bf16[512,128]{1,0:T(8,128)(2,1)S(1)} %get-tuple-element.22), channel_id=1, source_target_pairs={{0,8},{2,10},{4,12},{6,14},{8,0},{10,2},{12,4},{14,6},{16,24},{18,... | collective-permute-start | bytes 393224 | tf_op jit(solution)/shard_map/ppermute | solution.py:477
  13.5 4.3 %collective-permute-start.4 = (bf16[512,128]{1,0:T(8,128)(2,1)S(1)}, bf16[512,128]{1,0:T(8,128)(2,1)S(1)}, u32[]{:S(2)}, u32[]{:S(2)}) collective-permute-start(bf16[512,128]{1,0:T(8,128)(2,1)S(1)} %get-tuple-element.24), channel_id=1, source_target_pairs={{0,0},{2,2},{4,4},{6,6},{8,16},{10,18},{12,20},{14,22},{16,8},{18,... | collective-permute-start | bytes 393224 | tf_op jit(solution)/shard_map/ppermute | solution.py:478
  17.8 14.7 %collective-permute-start.5 = (bf16[512,128]{1,0:T(8,128)(2,1)S(1)}, bf16[512,128]{1,0:T(8,128)(2,1)S(1)}, u32[]{:S(2)}, u32[]{:S(2)}) collective-permute-start(bf16[512,128]{1,0:T(8,128)(2,1)S(1)} %collective-permute-done.3.a), channel_id=1, source_target_pairs={{0,1},{1,0},{2,3},{3,2},{4,5},{5,4},{6,7},{7,6},{8,9},{9,8},{10,11... | collective-permute-start | bytes 393224 | tf_op jit(solution)/shard_map/ppermute | solution.py:466
  17.8 14.7 %collective-permute-start.7 = (bf16[512,128]{1,0:T(8,128)(2,1)S(1)}, bf16[512,128]{1,0:T(8,128)(2,1)S(1)}, u32[]{:S(2)}, u32[]{:S(2)}) collective-permute-start(bf16[512,128]{1,0:T(8,128)(2,1)S(1)} %collective-permute-done.4.b), channel_id=1, source_target_pairs={{0,1},{1,0},{2,3},{3,2},{4,5},{5,4},{6,7},{7,6},{8,9},{9,8},{10,11... | collective-permute-start | bytes 393224 | tf_op jit(solution)/shard_map/ppermute | solution.py:466
  18.3 0.9 %copy-start.2 = (bf16[32,32,27]{1,0,2:T(8,128)(2,1)S(1)}, bf16[32,32,27]{1,0,2:T(8,128)(2,1)}, u32[]{:S(2)}) copy-start(bf16[32,32,27]{1,0,2:T(8,128)(2,1)} %param.5) | copy-start | bytes 165892
  19.2 0.9 %copy-start.3 = (bf16[64,32,27]{0,1,2:T(8,128)(2,1)S(1)}, bf16[64,32,27]{0,1,2:T(8,128)(2,1)}, u32[]{:S(2)}) copy-start(bf16[64,32,27]{0,1,2:T(8,128)(2,1)} %param.6) | copy-start | bytes 331780
  24.7 10.7 %collective-permute-start.9 = (bf16[2,64,128]{2,1,0:T(8,128)(2,1)S(1)}, bf16[2,64,128]{2,1,0:T(8,128)(2,1)S(1)}, u32[]{:S(2)}, u32[]{:S(2)}) collective-permute-start(bf16[2,64,128]{2,1,0:T(8,128)(2,1)S(1)} %get-tuple-element.33.pooled), channel_id=1, source_target_pairs={{0,0},{2,2},{4,4},{6,6},{8,16},{10,18},{12,20},{14,22},{16,8},{18,... | collective-permute-start | bytes 98312 | tf_op jit(solution)/shard_map/ppermute | solution.py:478
  25.4 10.0 %collective-permute-start.8 = (bf16[2,64,128]{2,1,0:T(8,128)(2,1)S(1)}, bf16[2,64,128]{2,1,0:T(8,128)(2,1)S(1)}, u32[]{:S(2)}, u32[]{:S(2)}) collective-permute-start(bf16[2,64,128]{2,1,0:T(8,128)(2,1)S(1)} %get-tuple-element.33.pooled), channel_id=1, source_target_pairs={{0,8},{2,10},{4,12},{6,14},{8,0},{10,2},{12,4},{14,6},{16,24},{18,... | collective-permute-start | bytes 98312 | tf_op jit(solution)/shard_map/ppermute | solution.py:477
  38.9 7.6 %collective-permute-start.12 = (bf16[384,128]{1,0:T(8,128)(2,1)S(1)}, bf16[384,128]{1,0:T(8,128)(2,1)S(1)}, u32[]{:S(2)}, u32[]{:S(2)}) collective-permute-start(bf16[384,128]{1,0:T(8,128)(2,1)S(1)} %get-tuple-element.38.refs_0_), channel_id=1, source_target_pairs={{0,24},{2,26},{4,28},{6,30},{8,16},{10,18},{12,20},{14,22},{16,8},... | collective-permute-start | bytes 294920 | tf_op jit(solution)/shard_map/ppermute | solution.py:460
  40.1 10.2 %collective-permute-start.11 = (bf16[384,128]{1,0:T(8,128)(2,1)S(1)}, bf16[384,128]{1,0:T(8,128)(2,1)S(1)}, u32[]{:S(2)}, u32[]{:S(2)}) collective-permute-start(bf16[384,128]{1,0:T(8,128)(2,1)S(1)} %get-tuple-element.38.refs_0_), channel_id=1, source_target_pairs={{0,16},{2,18},{4,20},{6,22},{8,24},{10,26},{12,28},{14,30},{16,0},... | collective-permute-start | bytes 294920 | tf_op jit(solution)/shard_map/ppermute | solution.py:460
  41.4 8.9 %collective-permute-start.10 = (bf16[384,128]{1,0:T(8,128)(2,1)S(1)}, bf16[384,128]{1,0:T(8,128)(2,1)S(1)}, u32[]{:S(2)}, u32[]{:S(2)}) collective-permute-start(bf16[384,128]{1,0:T(8,128)(2,1)S(1)} %get-tuple-element.38.refs_0_), channel_id=1, source_target_pairs={{0,8},{2,10},{4,12},{6,14},{8,0},{10,2},{12,4},{14,6},{16,24},{18,... | collective-permute-start | bytes 294920 | tf_op jit(solution)/shard_map/ppermute | solution.py:460

commit v3 on v2

--- a/solution.py
+++ b/solution.py
@@ -59,6 +59,10 @@
     before = jnp.where(at == 0, 0.0, pltpu.roll(x, 1, 0))
     after = jnp.where(at == rows - 1, 0.0, pltpu.roll(x, rows - 1, 0))
     return before, after
+
+
+def sigmoid(x):
+    return 0.5 + 0.5 * jnp.tanh(0.5 * x)
 
 
 def slope_of(pre, sig):
@@ -178,15 +182,22 @@
     return one_hot(n == (g * d.height2 + (r >> 1)) * d.half + i, 0.125)
 
 
-def half_sum(d, xs, q, count, f1, g, pre):
+def stacked(ref, starts, count):
+    tall = [ref[q : q + count].reshape(count * ref.shape[1], ref.shape[2]) for q in starts]
+    return tall[0] if len(tall) == 1 else jnp.concatenate(tall, axis=0)
+
+
+def first_conv(d, halves, starts, count, f1):
     size = 3 * d.height * d.half
-    for a in range(3):
-        pre = pre + mm(xs[q + a - 1 : q + a - 1 + count].reshape(count * d.width, size), f1[a, g * size : (g + 1) * size])
+    pre = jnp.zeros((len(starts) * count * d.width, d.height * d.mid), F32)
+    for g, ref in enumerate(halves):
+        for a in range(3):
+            pre = pre + mm(stacked(ref, [q + a - 1 for q in starts], count), f1[a, g * size : (g + 1) * size])
     return pre
 
 
 def first_level(d, pre, count, pool, slopes, rows, at):
-    sig = jax.nn.sigmoid(pre)
+    sig = sigmoid(pre)
     slopes[at : at + count] = slope_of(pre, sig).reshape(count, d.width, -1)
     rows[at : at + count] = mm((pre * sig).astype(BF16), pool).reshape(count, d.width, -1)
 
@@ -214,11 +225,8 @@
         spread_plane(d, mi[at, :], xs, EDGE + p)
         spread_plane(d, mi_x[at, :], xs_x, EDGE + p)
     pool = pool_matrix(d)
-    for q in range(1, per - 1, 3):
-        pre = jnp.zeros((3 * d.width, d.height * d.mid), F32)
-        for g, ref in enumerate((xs, xs_x)):
-            pre = half_sum(d, ref, EDGE + q, 3, f1, g, pre)
-        first_level(d, pre, 3, pool, slopes, rows, q - 1)
+    pre = first_conv(d, (xs, xs_x), [EDGE + 1], per - 2, f1)
+    first_level(d, pre, per - 2, pool, slopes, rows, 0)
     for u in range(BLOCK - 2):
         pooled[u] = pool_pair(d, rows, 2 * u + 1, pair, u).astype(BF16)
 
@@ -234,135 +242,152 @@
             spread_plane(d, pick(True, even, x, y, first), ref, p)
             spread_plane(d, pick(False, even, x, y, last), ref, EDGE + per + p)
     pool = pool_matrix(d)
-    for k, q in enumerate((1, per + EDGE - 1)):
-        pre = jnp.zeros((3 * d.width, d.height * d.mid), F32)
-        for g, ref in enumerate((xs, xs_x)):
-            pre = half_sum(d, ref, q, 3, f1, g, pre)
-        first_level(d, pre, 3, pool, slopes, rows, 3 * k)
+    pre = first_conv(d, (xs, xs_x), [1, per + EDGE - 1], 3, f1)
+    first_level(d, pre, 6, pool, slopes, rows, 0)
+
+
+def spread_cell(cell, zs, u):
+    lanes = cell.shape[1]
+    before, after = shifted(cell)
+    zs[u, :, 0:lanes] = before.astype(BF16)
+    zs[u, :, lanes : 2 * lanes] = cell.astype(BF16)
+    zs[u, :, 2 * lanes :] = after.astype(BF16)
+
+
+def spread_grad(cell, gs, u):
+    lanes = cell.shape[1]
+    before, after = shifted(cell)
+    gs[u, :, 0:lanes] = after.astype(BF16)
+    gs[u, :, lanes : 2 * lanes] = cell.astype(BF16)
+    gs[u, :, 2 * lanes :] = before.astype(BF16)
+
+
+def second_conv(zs, starts, count, f2):
+    pre = None
+    for a in range(3):
+        part = mm(stacked(zs, [q + a - 1 for q in starts], count), f2[a])
+        pre = part if pre is None else pre + part
+    return pre
+
+
+def collect(d, parts, groups, height, chans, tiles, first_slot):
+    lane = lax.broadcasted_iota(jnp.int32, (chans, 128), 1)
+    tap_row = lane >> log2(d.half)
+    slots = 128 // d.half
+    for g in range(groups):
+        for m in range(9):
+            value = jnp.zeros((chans, 128), F32)
+            for r in range(height):
+                at = (g * height + r) * chans
+                tile = parts[m // 3][at : at + chans, (m % 3) * 128 : (m % 3 + 1) * 128]
+                tile = pltpu.roll(tile, (1 - r) * d.half % 128, 1)
+                if r == 0:
+                    tile = jnp.where(tap_row == 0, 0.0, tile)
+                if r == height - 1:
+                    tile = jnp.where(tap_row == 2, 0.0, tile)
+                value += tile
+            slot = first_slot + 27 * g + 3 * m
+            t, spot = slot // slots, slot % slots
+            if spot:
+                value = pltpu.roll(value, spot * d.half, 1)
+            here = (tap_row >= spot) & (tap_row < spot + 3)
+            tiles[t] = jnp.where(here, value, tiles.get(t, 0.0))
+            if spot + 3 > slots:
+                tiles[t + 1] = jnp.where(tap_row < spot + 3 - slots, value, 0.0)
+
+
+def second_kernel(d, mi, mi_x, pooled, rows_mid, rows_out, f2, zs, gs, sums, pair):
+    per, width = BLOCK * d.planes, d.width
+    width2 = width // 2
+    wide2 = d.height2 * 2 * d.half2
+    first, last = ends()
+    low = pool_pair(d, [rows_out[0], rows_out[1]], 0, pair, 0)
+    spread_cell(jnp.where(first, 0.0, low), zs, 0)
+    spread_cell(pool_pair(d, [rows_out[2], rows_mid[0]], 0, pair, 1), zs, 1)
+    for u in range(BLOCK - 2):
+        spread_cell(pooled[u].astype(F32), zs, 2 + u)
+    spread_cell(pool_pair(d, [rows_mid[per - 3], rows_out[3]], 0, pair, 2), zs, BLOCK)
+    high = pool_pair(d, [rows_out[4], rows_out[5]], 0, pair, 3)
+    spread_cell(jnp.where(last, 0.0, high), zs, BLOCK + 1)
+    pre = second_conv(zs, [1], BLOCK, f2)
+    slope = slope_of(pre, sigmoid(pre))
+    for u in range(BLOCK):
+        at = slice(per * width + u * width2, per * width + (u + 1) * width2)
+        cot = jnp.concatenate([mi[at, :], mi_x[at, :]], axis=1).astype(F32)
+        spread_grad(cot * slope[u * width2 : (u + 1) * width2], gs, u)
+    center = gs[:, :, wide2 : 2 * wide2].reshape(BLOCK * width2, wide2)
+    parts = [mm_t(center, stacked(zs, [a], BLOCK)) for a in range(3)]
+    tiles = {}
+    collect(d, parts, 2, d.height2, d.half2, tiles, 0)
+    for t, tile in tiles.items():
+        sums[t * d.half2 : (t + 1) * d.half2, :] = tile.astype(BF16)
 
 
 def main_kernel(
-    d, a, mi, b, a_x, mi_x, b_x, xs, slopes_mid, rows_mid, slopes_out, rows_out, pooled_a, pooled, pooled_b,
-    f2, b2, grads_out, sums_out, cs, sl, rows, pair, zs, gs, up, g1,
+    d, a, b, a_x, b_x, xs, slopes_mid, slopes_out, pooled_a, pooled_b, zs_in, gs_in, sums_in, f2, b2,
+    grads_out, late, sums_out, zs, gs, up, g1,
 ):
     place = lax.axis_index("depth")
     first, last = ends()
     even = parity()
     planes, width, wide1 = d.planes, d.width, d.height * d.mid
     width2 = width // 2
-    own1 = d.height * d.half
     wide2 = d.height2 * 2 * d.half2
-    own2 = d.height2 * d.half2
-    zl = d.height2 * d.mid
     per = BLOCK * planes
-
     side = EDGE * width
-    for g, (x, m, y) in enumerate(((a, mi, b), (a_x, mi_x, b_x))):
-        lanes = slice(g * own2, (g + 1) * own2)
-        x, y = x[side:, :], y[side:, :]
-        cs[0:2, :, lanes] = pick(True, even, x, y, first).reshape(2, width2, own2)
-        cs[2 : 2 + BLOCK, :, lanes] = m[per * width :, :].reshape(BLOCK, width2, own2)
-        cs[2 + BLOCK :, :, lanes] = pick(False, even, x, y, last).reshape(2, width2, own2)
-    inner = per - 2
-    for ref, outer, middle in ((sl, slopes_out, slopes_mid), (rows, rows_out, rows_mid)):
-        ref[0:3] = outer[0:3]
-        ref[3 : 3 + inner] = middle[...]
-        ref[3 + inner :] = outer[3:6]
-    for u in range(3 * BLOCK - 2):
-        coarse = 1 + u
-        if coarse < BLOCK - 1:
-            k = coarse - 1
-            cell = pick(True, even, pooled_a[k], pooled_b[k], first).astype(F32)
-        elif coarse > 2 * BLOCK:
-            k = coarse - 2 * BLOCK - 1
-            cell = pick(False, even, pooled_a[k], pooled_b[k], last).astype(F32)
-        elif BLOCK < coarse < 2 * BLOCK - 1:
-            cell = pooled[coarse - BLOCK - 1].astype(F32)
-        else:
-            cell = pool_pair(d, rows, 2 * coarse - per + 2, pair, u)
-        if coarse == BLOCK - 1:
-            cell = jnp.where(first, 0.0, cell)
-        if coarse == 2 * BLOCK:
-            cell = jnp.where(last, 0.0, cell)
-        before, after = shifted(cell)
-        zs[u, :, 0:zl] = before.astype(BF16)
-        zs[u, :, zl : 2 * zl] = cell.astype(BF16)
-        zs[u, :, 2 * zl :] = after.astype(BF16)
-
-    count = BLOCK + 4
-    pre = jnp.zeros((count * width2, wide2), F32)
-    for a in range(3):
-        pre += mm(zs[a : a + count].reshape(count * width2, 3 * zl), f2[a])
-    sig = jax.nn.sigmoid(pre)
-    grad_two = cs[...].reshape(count * width2, wide2).astype(F32) * slope_of(pre, sig)
-    for u in range(count):
-        g = grad_two[u * width2 : (u + 1) * width2]
-        before, after = shifted(g)
-        gs[u, :, 0:wide2] = after.astype(BF16)
-        gs[u, :, wide2 : 2 * wide2] = g.astype(BF16)
-        gs[u, :, 2 * wide2 :] = before.astype(BF16)
-
-    inner = count - 2
-    back = jnp.zeros((inner * width2, wide1), F32)
-    for a in range(3):
-        back += mm(gs[2 - a : 2 - a + inner].reshape(inner * width2, 3 * wide2), b2[a])
+
+    zs[2 : 4 + BLOCK] = zs_in[...]
+    gs[2 : 2 + BLOCK] = gs_in[...]
+    for k in range(2):
+        spread_cell(pick(True, even, pooled_a[k], pooled_b[k], first).astype(F32), zs, k)
+        spread_cell(pick(False, even, pooled_a[k], pooled_b[k], last).astype(F32), zs, 4 + BLOCK + k)
+    pre = second_conv(zs, [1, 3 + BLOCK], 2, f2)
+    slope = slope_of(pre, sigmoid(pre))
+    for k in range(4):
+        at = slice(side + (k % 2) * width2, side + (k % 2 + 1) * width2)
+        lower = k < 2
+        cot = [pick(lower, even, x[at, :], y[at, :], first if lower else last) for x, y in ((a, b), (a_x, b_x))]
+        cot = jnp.concatenate(cot, axis=1).astype(F32)
+        spread_grad(cot * slope[k * width2 : (k + 1) * width2], gs, k if lower else BLOCK + k)
+
+    inner = BLOCK + 2
+    back = None
+    for t in range(3):
+        part = mm(gs[2 - t : 2 - t + inner].reshape(inner * width2, 3 * wide2), b2[t])
+        back = part if back is None else back + part
     pieces = wide1 // 128
     for u in range(inner):
-        b = back[u * width2 : (u + 1) * width2]
+        x = back[u * width2 : (u + 1) * width2]
         for piece in range(pieces):
             lanes = slice(piece * 128, (piece + 1) * 128)
-            up[u * pieces + piece, pl.ds(0, width2, 2), :] = b[:, lanes]
-            up[u * pieces + piece, pl.ds(1, width2, 2), :] = b[:, lanes]
+            up[u * pieces + piece, pl.ds(0, width2, 2), :] = x[:, lanes]
+            up[u * pieces + piece, pl.ds(1, width2, 2), :] = x[:, lanes]
     for u in range(per + 2):
         q = per - 1 + u
         both = [up[(q - 6) // 2 * pieces + piece] for piece in range(pieces)]
-        g = jnp.concatenate(both, axis=1) * sl[q - per + 2]
+        if q <= per:
+            slope = slopes_out[q - per + 2]
+        elif q >= 2 * per - 1:
+            slope = slopes_out[q - 2 * per + 4]
+        else:
+            slope = slopes_mid[q - per - 1]
+        g = jnp.concatenate(both, axis=1) * slope
         if q < per:
             g = jnp.where(first, 0.0, g)
         if q >= 2 * per:
             g = jnp.where(last, 0.0, g)
         g1[u] = g.astype(BF16)
+
+    center = g1[1 : 1 + per].reshape(per * width, wide1)
+    parts = [mm_t(center, stacked(xs, [EDGE + t - 1], per)) for t in range(3)]
+    tiles = {}
+    collect(d, parts, 1, d.height, d.mid, tiles, 0)
+    kept = sums_in.shape[0]
+    sums_out[:kept, :] = sums_in[...]
+    for t, tile in tiles.items():
+        late[t * d.mid : (t + 1) * d.mid, :] = tile.astype(BF16)
+    sums_out[kept:, :] = late[...]
     grads_out[...] = g1[pl.ds((place & (BLOCK - 1)) * planes, planes + 2)]
-
-    def collect(parts, groups, height, chans, base):
-        lane = lax.broadcasted_iota(jnp.int32, (chans, 128), 1)
-        tap_row = lane >> log2(d.half)
-        for g in range(groups):
-            def total(m):
-                out = jnp.zeros((chans, 128), F32)
-                for r in range(height):
-                    at = (g * height + r) * chans
-                    tile = parts[m // 3][at : at + chans, (m % 3) * 128 : (m % 3 + 1) * 128]
-                    tile = pltpu.roll(tile, (1 - r) * d.half % 128, 1)
-                    if r == 0:
-                        tile = jnp.where(tap_row == 0, 0.0, tile)
-                    if r == height - 1:
-                        tile = jnp.where(tap_row == 2, 0.0, tile)
-                    out += tile
-                return out
-
-            def turned(x, lanes):
-                return pltpu.roll(x, lanes % 128, 1) if lanes % 128 else x
-
-            extra = total(8)
-            for tile in range(4):
-                out = jnp.where(lane < 3 * d.half, total(2 * tile), turned(total(2 * tile + 1), 3 * d.half))
-                if tile == 0:
-                    out = jnp.where(lane < 6 * d.half, out, turned(extra, 6 * d.half))
-                if tile == 1:
-                    out = jnp.where(lane < 6 * d.half, out, turned(extra, 4 * d.half))
-                at = base + (g * 4 + tile) * chans
-                sums_out[at : at + chans, :] = out.astype(BF16)
-
-    center = g1[1 : 1 + per].reshape(per * width, wide1)
-    parts = [
-        mm_t(center, xs[EDGE + a - 1 : EDGE + a - 1 + per].reshape(per * width, 3 * own1))
-        for a in range(3)
-    ]
-    collect(parts, 1, d.height, d.mid, 0)
-    center = gs[2 : 2 + BLOCK, :, wide2 : 2 * wide2].reshape(BLOCK * width2, wide2)
-    parts = [mm_t(center, zs[2 + a : 2 + a + BLOCK].reshape(BLOCK * width2, 3 * zl)) for a in range(3)]
-    collect(parts, 2, d.height2, d.half2, 4 * d.mid)
 
 
 def feats_kernel(d, g1, b1, out, wide):
@@ -383,28 +408,34 @@
 
 
 def final_kernel(d, *refs):
-    member = lax.axis_index("chan")
-    parts, (out1, out2) = refs[:-2], refs[-2:]
-    terms = [p[...].astype(F32) for p in parts]
+    swapped = lax.axis_index("chan") == 1
+    parts, (out1, out2, r) = list(refs[:-3]), refs[-3:]
+    rows = parts[0].shape[0]
+    terms = []
+    while parts:
+        pieces = [parts.pop(0)[...].astype(F32)]
+        while sum(piece.shape[0] for piece in pieces) < rows:
+            pieces.append(parts.pop(0)[...].astype(F32))
+        terms.append(pieces[0] if len(pieces) == 1 else jnp.concatenate(pieces, axis=0))
     while len(terms) > 1:
         terms = [terms[i] + terms[i + 1] for i in range(0, len(terms), 2)]
     total = terms[0]
-    half = d.half
-
-    def lay_out(base, groups, chans, out):
-        full = groups * chans
-        for tile in range(4):
-            rows = [total[base + (g * 4 + tile) * chans : base + (g * 4 + tile + 1) * chans] for g in range(groups)]
-            rows = jnp.concatenate(rows, axis=0) if groups > 1 else rows[0]
-            flat = pltpu.roll(rows, member * (full // 2), 0).T
-            spots = [(2 * tile, b, b) for b in range(3)] + [(2 * tile + 1, b, 3 + b) for b in range(3)]
-            spots += {0: [(8, 0, 6), (8, 1, 7)], 1: [(8, 2, 6)]}.get(tile, [])
-            for m, b, spot in spots:
-                tap = 9 * (m // 3) + 3 * b + m % 3
-                out[tap * half : (tap + 1) * half, :] = flat[spot * half : (spot + 1) * half]
-
-    lay_out(0, 1, d.mid, out1)
-    lay_out(4 * d.mid, 2, d.half2, out2)
+    half, mid = d.half, d.mid
+    slots = 128 // half
+    for t in range(total.shape[0] // mid):
+        flat = total[t * mid : (t + 1) * mid].T
+        for spot in range(slots):
+            early = -(-2 * 27 // slots)
+            slot = slots * t + spot if t < early else slots * (t - early) + spot + 2 * 27
+            if slot >= (2 * 27 if t < early else 3 * 27):
+                continue
+            g, m, b = slot // 27, slot % 27 // 3, slot % 3
+            tap = 9 * (m // 3) + 3 * b + m % 3
+            r[g, tap * half : (tap + 1) * half, :] = flat[spot * half : (spot + 1) * half]
+    x, y = r[0], r[1]
+    out2[...] = jnp.concatenate([jnp.where(swapped, y, x), jnp.where(swapped, x, y)], axis=1)
+    x = r[2]
+    out1[...] = jnp.where(swapped, jnp.concatenate([x[:, half:], x[:, :half]], axis=1), x)
 
 
 class Sizes:
@@ -419,7 +450,7 @@
     d.half2, coarse, d.height2, width2 = cotangent.shape
     d.mid = weight_one.shape[0]
     assert d.planes == 2 and coarse == 1 and d.half * 8 == 128 and d.height2 * d.half2 == 128
-    assert d.width == 128 and d.height == 8 and d.mid == 32
+    assert d.width == 128 and d.height == 8 and d.mid == d.half2 == 32
     blocks = slabs // BLOCK
     per = BLOCK * d.planes
     wide1 = d.height * d.mid
@@ -529,33 +560,61 @@
         aliases={4: 0, 5: 1},
     )(a, b, a_x, b_x, xs_mid, xs_mid_x, f1)
 
-    grads, sums = call(
+    fan = min(4, blocks)
+
+    def move(x, k):
+        return xor(x, BLOCK * k)
+
+    early_rows, late_rows = -(-2 * 27 // 8) * d.half2, -(-27 // 8) * d.mid
+    zs, gs, early = call(
+        second_kernel,
+        [
+            ((BLOCK + 2, width2, 3 * zl), BF16),
+            ((BLOCK, width2, 3 * wide2), BF16),
+            ((early_rows, 128), BF16),
+        ],
+        [pltpu.VMEM((BLOCK, d.width, zl), F32)],
+        flops=1 << 30,
+    )(mid, mid_x, pooled, rows_mid, rows_out, f2)
+    early = [early] + [move(early, k) for k in range(2, fan)]
+    grads, late, sums = call(
         main_kernel,
-        [((d.planes + 2, d.width, wide1), BF16), ((4 * d.mid + 8 * d.half2, 128), BF16)],
-        [
-            pltpu.VMEM((BLOCK + 4, width2, wide2), BF16),
-            pltpu.VMEM((per + 4, d.width, wide1), F32),
-            pltpu.VMEM((per + 4, d.width, zl), F32),
-            pltpu.VMEM((3 * BLOCK - 2, d.width, zl), F32),
+        [
+            ((d.planes + 2, d.width, wide1), BF16),
+            ((late_rows, 128), BF16),
+            ((early_rows + late_rows, 128), BF16),
+        ],
+        [
             pltpu.VMEM((3 * BLOCK - 2, width2, 3 * zl), BF16),
             pltpu.VMEM((BLOCK + 4, width2, 3 * wide2), BF16),
             pltpu.VMEM(((BLOCK + 2) * (wide1 // 128), d.width, 128), F32),
             pltpu.VMEM((per + 2, d.width, wide1), BF16),
         ],
         flops=1 << 32,
-    )(a, mid, b, a_x, mid_x, b_x, xs, slopes_mid, rows_mid, slopes_out, rows_out, pooled_a, pooled, pooled_b, f2, b2)
-
-    parts = [sums]
-    radix = 1
+    )(a, b, a_x, b_x, xs, slopes_mid, slopes_out, pooled_a, pooled_b, zs, gs, early[0], f2, b2)
+
+    parts = [(sums,)]
+    for k in range(fan - 1, 1, -1):
+        parts.append((early[k - 1], move(late, k)))
+    if fan > 1:
+        parts.append((move(sums, 1),))
+    parts = [parts[i] for i in (0, -1, -2, -3)[: len(parts)]]
+    radix = fan
     while radix < blocks:
+        whole = [p[0] if len(p) == 1 else jnp.concatenate(p) for p in parts]
+        mine = sum_parts(whole)
         fan = min(4, blocks // radix)
-        mine = parts[0] if len(parts) == 1 else sum_parts(parts)
-        parts = [mine] + [xor(mine, BLOCK * radix * k) for k in range(1, fan)]
+        parts = [(mine,)] + [(xor(mine, BLOCK * radix * k),) for k in range(1, fan)]
         radix *= fan
+    parts = sum(parts, ())
     (grad,) = call(
         feats_kernel, [(feats_shape, BF16)], [pltpu.VMEM((d.planes + 2, d.width, 3 * wide1), BF16)], flops=1 << 30
     )(grads, b1)
-    out1, out2 = call(final_kernel, [((27 * d.half, d.mid), F32), ((27 * d.half, 2 * d.half2), F32)])(*parts)
+    out1, out2 = call(
+        final_kernel,
+        [((27 * d.half, d.mid), F32), ((27 * d.half, 2 * d.half2), F32)],
+        [pltpu.VMEM((3, 27 * d.half, d.mid), F32)],
+    )(*parts)
     return (
         grad.reshape(feats.shape),
         out1.reshape(27, d.half, d.mid).transpose(2, 1, 0),

time: 51.6 us -> 49.3 us (0.955)
  waiting for transfers between devices: 13.6 us -> 11.1 us
  starting transfers between devices: 19.8 us -> 21.3 us
  Pallas kernels: 13.7 us -> 12.4 us
    ppermute x6 -> x8, waiting for transfers between devices: 10 us -> 7.48 us  [xor(): return lax.ppermute(x, 'depth', [(i, i ^ k) for i in range(slabs)])]
    ppermute x6 -> x8, starting transfers between devices: 9.08 us -> 10.6 us  [xor(): return lax.ppermute(x, 'depth', [(i, i ^ k) for i in range(slabs)])]
    pallas_call x8 -> x9, Pallas kernels: 13.7 us -> 12.4 us  [run(): pl.pallas_call(functools.partial(kernel, d), out_shape=[jax.ShapeDtypeStr...]
  transfers between devices with their start and end apart: 13 -> 15, of which waited for: 6 -> 7; matrix products, arithmetic and copies ran while one was open for 0% -> 0% of each run, Pallas kernels for 17% -> 22%
where the time goes in v3:
time: 49.3 us; the launch traced here: 49 us
  starting transfers between devices  21.3 us (43%)
  Pallas kernels  12.4 us (25%)
  waiting for transfers between devices  11.1 us (23%)
  local copies, waits for them, and re-layouts  3.46 us (7%)
  between operations  0.72 us (1%)
    pallas_call x9, Pallas kernels, run(): pl.pallas_call(functools.partial(kernel, d), out_shape=[jax.ShapeDtypeStr...  12.4 us
    ppermute x8, starting transfers between devices, xor(): return lax.ppermute(x, 'depth', [(i, i ^ k) for i in range(slabs)])  10.6 us
    ppermute x2, starting transfers between devices, trade(): a = lax.ppermute(x_a, 'depth', pair_a)  8.77 us
    ppermute x8, waiting for transfers between devices, xor(): return lax.ppermute(x, 'depth', [(i, i ^ k) for i in range(slabs)])  7.48 us
    ppermute x2, waiting for transfers between devices, trade(): a = lax.ppermute(x_a, 'depth', pair_a)  3.6 us
    unnamed x8, local copies, waits for them, and re-layouts  3.46 us
    ppermute x2, starting transfers between devices, trade(): b = lax.ppermute(x_b, 'depth', pair_b)  1.32 us
  transfers between devices with their start and end apart: 15, of which 7 were waited for; matrix products, arithmetic and copies ran while one was open for 0% of the time, Pallas kernels for 22%

profile of v3, /device:TPU:0, one launch (start us, length us, event | category | flops | bytes accessed | tf_op | source)
XLA Modules:
  0.0 49.0 jit_solution(8939383561729782615)
XLA Ops:
  0.6 0.8 %copy-done = bf16[16,2,8,128]{3,2,1,0:T(8,128)(2,1)S(1)} copy-done((bf16[16,2,8,128]{3,2,1,0:T(8,128)(2,1)S(1)}, bf16[16,2,8,128]{3,2,1,0:T(8,128)(2,1)}, u32[]{:S(2)}) %copy-start) | copy-done | bytes 65560
  1.5 0.8 %copy-done.1 = bf16[32,1,4,64]{3,2,1,0:T(4,128)(2,1)S(1)} copy-done((bf16[32,1,4,64]{3,2,1,0:T(4,128)(2,1)S(1)}, bf16[32,1,4,64]{3,2,1,0:T(4,128)(2,1)}, u32[]{:S(2)}) %copy-start.1) | copy-done | bytes 16408
  2.2 0.6 %shard_map.67.i0 = bf16[320,128]{1,0:T(8,128)(2,1)S(1)} custom-call(bf16[256,128]{1,0:T(8,128)(2,1)S(1)} %bitcast.15, bf16[128,64]{1,0:T(8,128)(2,1)S(1)} %bitcast.16), custom_call_target="tpu_custom_call" | custom-call | bytes 1048576 | tf_op jit(solution)/shard_map/pallas_call | solution.py:463
  2.8 4.0 %collective-permute-start.2 = (bf16[320,128]{1,0:T(8,128)(2,1)S(1)}, bf16[320,128]{1,0:T(8,128)(2,1)S(1)}, u32[]{:S(2)}, u32[]{:S(2)}) collective-permute-start(bf16[320,128]{1,0:T(8,128)(2,1)S(1)} %shard_map.67.i0), channel_id=1, source_target_pairs={{0,6},{2,4},{4,2},{6,0},{8,14},{10,12},{12,10},{14,8},{16,22},{18,... | collective-permute-start | bytes 245768 | tf_op jit(solution)/shard_map/ppermute | solution.py:491
  6.8 0.5 %collective-permute-start.1 = (bf16[320,128]{1,0:T(8,128)(2,1)S(1)}, bf16[320,128]{1,0:T(8,128)(2,1)S(1)}, u32[]{:S(2)}, u32[]{:S(2)}) collective-permute-start(bf16[320,128]{1,0:T(8,128)(2,1)S(1)} %shard_map.67.i0), channel_id=1, source_target_pairs={{0,4},{2,6},{4,0},{6,2},{8,12},{10,14},{12,8},{14,10},{16,20},{18,... | collective-permute-start | bytes 245768 | tf_op jit(solution)/shard_map/ppermute | solution.py:491
  7.3 0.1 collective-permute-start
  7.4 1.9 %collective-permute-done.2.i3 = bf16[320,128]{1,0:T(8,128)(2,1)S(1)} collective-permute-done((bf16[320,128]{1,0:T(8,128)(2,1)S(1)}, bf16[320,128]{1,0:T(8,128)(2,1)S(1)}, u32[]{:S(2)}, u32[]{:S(2)}) %collective-permute-start.2) | collective-permute-done | bytes 81952 | tf_op jit(solution)/shard_map/ppermute | solution.py:491
  9.4 1.9 %collective-permute-done.1.i2 = bf16[320,128]{1,0:T(8,128)(2,1)S(1)} collective-permute-done((bf16[320,128]{1,0:T(8,128)(2,1)S(1)}, bf16[320,128]{1,0:T(8,128)(2,1)S(1)}, u32[]{:S(2)}, u32[]{:S(2)}) %collective-permute-start.1) | collective-permute-done | bytes 81952 | tf_op jit(solution)/shard_map/ppermute | solution.py:491
  11.2 0.5 %collective-permute-done.i1 = bf16[320,128]{1,0:T(8,128)(2,1)S(1)} collective-permute-done((bf16[320,128]{1,0:T(8,128)(2,1)S(1)}, bf16[320,128]{1,0:T(8,128)(2,1)S(1)}, u32[]{:S(2)}, u32[]{:S(2)}) %collective-permute-start) | collective-permute-done | bytes 81952 | tf_op jit(solution)/shard_map/ppermute | solution.py:491
  11.8 0.1 collective-permute-start.7
  11.9 1.6 %collective-permute-start.3 = (bf16[512,128]{1,0:T(8,128)(2,1)S(1)}, bf16[512,128]{1,0:T(8,128)(2,1)S(1)}, u32[]{:S(2)}, u32[]{:S(2)}) collective-permute-start(bf16[512,128]{1,0:T(8,128)(2,1)S(1)} %get-tuple-element.26), channel_id=1, source_target_pairs={{0,8},{2,10},{4,12},{6,14},{8,0},{10,2},{12,4},{14,6},{16,24},{18,... | collective-permute-start | bytes 393224 | tf_op jit(solution)/shard_map/ppermute | solution.py:508
  13.5 0.7 %collective-permute-start.4 = (bf16[512,128]{1,0:T(8,128)(2,1)S(1)}, bf16[512,128]{1,0:T(8,128)(2,1)S(1)}, u32[]{:S(2)}, u32[]{:S(2)}) collective-permute-start(bf16[512,128]{1,0:T(8,128)(2,1)S(1)} %get-tuple-element.27), channel_id=1, source_target_pairs={{0,0},{2,2},{4,4},{6,6},{8,16},{10,18},{12,20},{14,22},{16,8},{18,... | collective-permute-start | bytes 393224 | tf_op jit(solution)/shard_map/ppermute | solution.py:509
  14.2 3.6 %collective-permute-done.3.a = bf16[512,128]{1,0:T(8,128)(2,1)S(1)} collective-permute-done((bf16[512,128]{1,0:T(8,128)(2,1)S(1)}, bf16[512,128]{1,0:T(8,128)(2,1)S(1)}, u32[]{:S(2)}, u32[]{:S(2)}) %collective-permute-start.3) | collective-permute-done | bytes 131104 | tf_op jit(solution)/shard_map/ppermute | solution.py:508
  17.8 0.5 %collective-permute-start.6 = (bf16[512,128]{1,0:T(8,128)(2,1)S(1)}, bf16[512,128]{1,0:T(8,128)(2,1)S(1)}, u32[]{:S(2)}, u32[]{:S(2)}) collective-permute-start(bf16[512,128]{1,0:T(8,128)(2,1)S(1)} %collective-permute-done.4.b), channel_id=1, source_target_pairs={{0,1},{1,0},{2,3},{3,2},{4,5},{5,4},{6,7},{7,6},{8,9},{9,8},{10,11... | collective-permute-start | bytes 393224 | tf_op jit(solution)/shard_map/ppermute | solution.py:497
  18.3 0.9 %copy-done.2 = bf16[32,32,27]{1,0,2:T(8,128)(2,1)S(1)} copy-done((bf16[32,32,27]{1,0,2:T(8,128)(2,1)S(1)}, bf16[32,32,27]{1,0,2:T(8,128)(2,1)}, u32[]{:S(2)}) %copy-start.2) | copy-done | bytes 55320
  19.2 0.9 %copy-done.3 = bf16[64,32,27]{0,1,2:T(8,128)(2,1)S(1)} copy-done((bf16[64,32,27]{0,1,2:T(8,128)(2,1)S(1)}, bf16[64,32,27]{0,1,2:T(8,128)(2,1)}, u32[]{:S(2)}) %copy-start.3) | copy-done | bytes 110616
  20.2 1.7 %shard_map.69 = (bf16[3,768,256]{2,1,0:T(8,128)(2,1)S(1)}, bf16[3,768,128]{2,1,0:T(8,128)(2,1)S(1)}, bf16[3,384,256]{2,1,0:T(8,128)(2,1)S(1)}, bf16[3,768,256]{2,1,0:T(8,128)(2,1)S(1)}) custom-call(bf16[864,32]{1,0:T(8,128)(2,1)S(1)} %bitcast.17, bf16[864,64]{1,0:T(8,128)(2,1)S(1)} %bitcast.18), custom_call_target="tpu_custom_call" | custom-call | flops 1073741824 | bytes 1048576 | tf_op jit(solution)/shard_map/pallas_call | solution.py:463
  21.8 1.7 %shard_map.70 = (bf16[14,128,384]{2,1,0:T(8,128)(2,1)S(1)}, bf16[14,128,384]{2,1,0:T(8,128)(2,1)S(1)}, f32[6,128,256]{2,1,0:T(8,128)S(1)}, f32[6,128,128]{2,1,0:T(8,128)S(1)}, bf16[2,64,128]{2,1,0:T(8,128)(2,1)S(1)}) custom-call(bf16[1280,128]{1,0:T(8,128)(2,1)S(1)} %get-tuple-element.28.mi, bf16[1280,128]{1,0:T(8,128)(2,1)S(1)} %collective-permute-done.7.mi_x, ...), custom_call_target="tpu_custom_call" | custom-call | flops 1073741824 | bytes 1048576 | tf_op jit(solution)/shard_map/pallas_call | solution.py:463
  23.5 0.7 %collective-permute-start.9 = (bf16[2,64,128]{2,1,0:T(8,128)(2,1)S(1)}, bf16[2,64,128]{2,1,0:T(8,128)(2,1)S(1)}, u32[]{:S(2)}, u32[]{:S(2)}) collective-permute-start(bf16[2,64,128]{2,1,0:T(8,128)(2,1)S(1)} %get-tuple-element.35.pooled), channel_id=1, source_target_pairs={{0,0},{2,2},{4,4},{6,6},{8,16},{10,18},{12,20},{14,22},{16,8},{18,... | collective-permute-start | bytes 98312 | tf_op jit(solution)/shard_map/ppermute | solution.py:509
  24.2 7.1 %collective-permute-start.8 = (bf16[2,64,128]{2,1,0:T(8,128)(2,1)S(1)}, bf16[2,64,128]{2,1,0:T(8,128)(2,1)S(1)}, u32[]{:S(2)}, u32[]{:S(2)}) collective-permute-start(bf16[2,64,128]{2,1,0:T(8,128)(2,1)S(1)} %get-tuple-element.35.pooled), channel_id=1, source_target_pairs={{0,8},{2,10},{4,12},{6,14},{8,0},{10,2},{12,4},{14,6},{16,24},{18,... | collective-permute-start | bytes 98312 | tf_op jit(solution)/shard_map/ppermute | solution.py:508
  31.3 1.7 %shard_map.71 = (bf16[14,128,384]{2,1,0:T(8,128)(2,1)S(1)}, bf16[14,128,384]{2,1,0:T(8,128)(2,1)S(1)}, f32[6,128,256]{2,1,0:T(8,128)S(1)}, f32[6,128,128]{2,1,0:T(8,128)S(1)}) custom-call(bf16[512,128]{1,0:T(8,128)(2,1)S(1)} %collective-permute-done.3.a, ...), custom_call_target="tpu_custom_call", output_to_operand_aliasing={{0}: (4, {}), {1}: (5, {})} | custom-call | flops 1073741824 | bytes 1048576 | tf_op jit(solution)/shard_map/pallas_call | solution.py:463
  33.0 1.4 %shard_map.72 = (bf16[6,64,384]{2,1,0:T(8,128)(2,1)S(1)}, bf16[4,64,768]{2,1,0:T(8,128)(2,1)S(1)}, bf16[224,128]{1,0:T(8,128)(2,1)S(1)}) custom-call(bf16[1280,128]{1,0:T(8,128)(2,1)S(1)} %get-tuple-element.28.mi, bf16[1280,128]{1,0:T(8,128)(2,1)S(1)} %collective-permute-done.7.mi_x, bf16[2,64,128]{2,1,0:T(8,128)(2,1)S(1)} %get-tuple-element.35.pooled, ...), custom_call_target="tpu_custom_call" | custom-call | flops 1073741824 | bytes 1048576 | tf_op jit(solution)/shard_map/pallas_call | solution.py:463
  34.4 1.2 %collective-permute-start.13 = (bf16[224,128]{1,0:T(8,128)(2,1)S(1)}, bf16[224,128]{1,0:T(8,128)(2,1)S(1)}, u32[]{:S(2)}, u32[]{:S(2)}) collective-permute-start(bf16[224,128]{1,0:T(8,128)(2,1)S(1)} %get-tuple-element.41.sums_in), channel_id=1, source_target_pairs={{0,24},{2,26},{4,28},{6,30},{8,16},{10,18},{12,20},{14,22},{16,8},... | collective-permute-start | bytes 172040 | tf_op jit(solution)/shard_map/ppermute | solution.py:491
  35.6 0.3 collective-permute-start.11
  35.9 2.9 %shard_map.73 = (bf16[4,128,256]{2,1,0:T(8,128)(2,1)S(1)}, bf16[128,128]{1,0:T(8,128)(2,1)S(1)}, bf16[352,128]{1,0:T(8,128)(2,1)S(1)}) custom-call(bf16[512,128]{1,0:T(8,128)(2,1)S(1)} %collective-permute-done.3.a, bf16[512,128]{1,0:T(8,128)(2,1)S(1)} %collective-permute-done.4.b, bf16[512,128]{1,0:T(8,128)(2,1)S(1)} %collective-permute-done.5.a_x, ...), custom_call_target="tpu_custom_call" | custom-call | flops 4294967296 | bytes 1048576 | tf_op jit(solution)/shard_map/pallas_call | solution.py:463
  38.9 2.4 %collective-permute-start.14 = (bf16[128,128]{1,0:T(8,128)(2,1)S(1)}, bf16[128,128]{1,0:T(8,128)(2,1)S(1)}, u32[]{:S(2)}, u32[]{:S(2)}) collective-permute-start(bf16[128,128]{1,0:T(8,128)(2,1)S(1)} %get-tuple-element.46), channel_id=1, source_target_pairs={{0,24},{2,26},{4,28},{6,30},{8,16},{10,18},{12,20},{14,22},{16,8},... | collective-permute-start | bytes 98312 | tf_op jit(solution)/shard_map/ppermute | solution.py:491
  41.3 2.0 %collective-permute-start.12 = (bf16[128,128]{1,0:T(8,128)(2,1)S(1)}, bf16[128,128]{1,0:T(8,128)(2,1)S(1)}, u32[]{:S(2)}, u32[]{:S(2)}) collective-permute-start(bf16[128,128]{1,0:T(8,128)(2,1)S(1)} %get-tuple-element.46), channel_id=1, source_target_pairs={{0,16},{2,18},{4,20},{6,22},{8,24},{10,26},{12,28},{14,30},{16,0},... | collective-permute-start | bytes 98312 | tf_op jit(solution)/shard_map/ppermute | solution.py:491
  43.3 1.3 %shard_map.74 = bf16[256,128]{1,0:T(8,128)(2,1)} custom-call(bf16[4,128,256]{2,1,0:T(8,128)(2,1)S(1)} %get-tuple-element.43.g1, bf16[3,768,128]{2,1,0:T(8,128)(2,1)S(1)} %get-tuple-element.44.b1), custom_call_target="tpu_custom_call" | custom-call | flops 1073741824 | bytes 1048576 | tf_op jit(solution)/shard_map/pallas_call | solution.py:463
  44.7 0.5 collective-permute-done.14.refs_5_
  45.1 1.0 %collective-permute-done.12.refs_3_ = bf16[128,128]{1,0:T(8,128)(2,1)S(1)} collective-permute-done((bf16[128,128]{1,0:T(8,128)(2,1)S(1)}, bf16[128,128]{1,0:T(8,128)(2,1)S(1)}, u32[]{:S(2)}, u32[]{:S(2)}) %collective-permute-start.12) | collective-permute-done | bytes 32800 | tf_op jit(solution)/shard_map/ppermute | solution.py:491
  46.2 1.7 %collective-permute-done.10.refs_1_ = bf16[352,128]{1,0:T(8,128)(2,1)S(1)} collective-permute-done((bf16[352,128]{1,0:T(8,128)(2,1)S(1)}, bf16[352,128]{1,0:T(8,128)(2,1)S(1)}, u32[]{:S(2)}, u32[]{:S(2)}) %collective-permute-start.10) | collective-permute-done | bytes 90144 | tf_op jit(solution)/shard_map/ppermute | solution.py:491
  47.8 1.2 %shard_map.75 = (f32[432,32]{1,0:T(8,128)}, f32[432,64]{1,0:T(8,128)}) custom-call(bf16[352,128]{1,0:T(8,128)(2,1)S(1)} %get-tuple-element.45.refs_0_, bf16[352,128]{1,0:T(8,128)(2,1)S(1)} %collective-permute-done.10.refs_1_, bf16[224,128]{1,0:T(8,128)(2,1)S(1)} %collective-permute-done.11.refs_2_, bf16[128,128]{1,0:T(8,128)(2,1)S(1)} %collective-permute-done.12.refs_3_, ...), custom_call_target="tpu_custom_call" | custom-call | bytes 1048576 | tf_op jit(solution)/shard_map/pallas_call | solution.py:463
  (15 shorter events, 0.1 us)
Async XLA Ops:
  0.6 0.8 %copy-start = (bf16[16,2,8,128]{3,2,1,0:T(8,128)(2,1)S(1)}, bf16[16,2,8,128]{3,2,1,0:T(8,128)(2,1)}, u32[]{:S(2)}) copy-start(bf16[16,2,8,128]{3,2,1,0:T(8,128)(2,1)} %param.4) | copy-start | bytes 196612
  1.5 0.8 %copy-start.1 = (bf16[32,1,4,64]{3,2,1,0:T(4,128)(2,1)S(1)}, bf16[32,1,4,64]{3,2,1,0:T(4,128)(2,1)}, u32[]{:S(2)}) copy-start(bf16[32,1,4,64]{3,2,1,0:T(4,128)(2,1)} %param.7) | copy-start | bytes 49156
  2.8 6.6 %collective-permute-start.2 = (bf16[320,128]{1,0:T(8,128)(2,1)S(1)}, bf16[320,128]{1,0:T(8,128)(2,1)S(1)}, u32[]{:S(2)}, u32[]{:S(2)}) collective-permute-start(bf16[320,128]{1,0:T(8,128)(2,1)S(1)} %shard_map.67.i0), channel_id=1, source_target_pairs={{0,6},{2,4},{4,2},{6,0},{8,14},{10,12},{12,10},{14,8},{16,22},{18,... | collective-permute-start | bytes 245768 | tf_op jit(solution)/shard_map/ppermute | solution.py:491
  6.8 4.4 %collective-permute-start.1 = (bf16[320,128]{1,0:T(8,128)(2,1)S(1)}, bf16[320,128]{1,0:T(8,128)(2,1)S(1)}, u32[]{:S(2)}, u32[]{:S(2)}) collective-permute-start(bf16[320,128]{1,0:T(8,128)(2,1)S(1)} %shard_map.67.i0), channel_id=1, source_target_pairs={{0,4},{2,6},{4,0},{6,2},{8,12},{10,14},{12,8},{14,10},{16,20},{18,... | collective-permute-start | bytes 245768 | tf_op jit(solution)/shard_map/ppermute | solution.py:491
  7.3 4.4 %collective-permute-start = (bf16[320,128]{1,0:T(8,128)(2,1)S(1)}, bf16[320,128]{1,0:T(8,128)(2,1)S(1)}, u32[]{:S(2)}, u32[]{:S(2)}) collective-permute-start(bf16[320,128]{1,0:T(8,128)(2,1)S(1)} %shard_map.67.i0), channel_id=1, source_target_pairs={{0,2},{2,0},{4,6},{6,4},{8,10},{10,8},{12,14},{14,12},{16,18},{18,... | collective-permute-start | bytes 245768 | tf_op jit(solution)/shard_map/ppermute | solution.py:491
  11.8 10.0 %collective-permute-start.7 = (bf16[1280,128]{1,0:T(8,128)(2,1)S(1)}, bf16[1280,128]{1,0:T(8,128)(2,1)S(1)}, u32[]{:S(2)}, u32[]{:S(2)}) collective-permute-start(bf16[1280,128]{1,0:T(8,128)(2,1)S(1)} %get-tuple-element.28.mi), channel_id=1, source_target_pairs={{0,1},{1,0},{2,3},{3,2},{4,5},{5,4},{6,7},{7,6},{8,9},{9,8},{10,11... | collective-permute-start | bytes 983048 | tf_op jit(solution)/shard_map/ppermute | solution.py:497
  11.9 5.9 %collective-permute-start.3 = (bf16[512,128]{1,0:T(8,128)(2,1)S(1)}, bf16[512,128]{1,0:T(8,128)(2,1)S(1)}, u32[]{:S(2)}, u32[]{:S(2)}) collective-permute-start(bf16[512,128]{1,0:T(8,128)(2,1)S(1)} %get-tuple-element.26), channel_id=1, source_target_pairs={{0,8},{2,10},{4,12},{6,14},{8,0},{10,2},{12,4},{14,6},{16,24},{18,... | collective-permute-start | bytes 393224 | tf_op jit(solution)/shard_map/ppermute | solution.py:508
  13.5 4.3 %collective-permute-start.4 = (bf16[512,128]{1,0:T(8,128)(2,1)S(1)}, bf16[512,128]{1,0:T(8,128)(2,1)S(1)}, u32[]{:S(2)}, u32[]{:S(2)}) collective-permute-start(bf16[512,128]{1,0:T(8,128)(2,1)S(1)} %get-tuple-element.27), channel_id=1, source_target_pairs={{0,0},{2,2},{4,4},{6,6},{8,16},{10,18},{12,20},{14,22},{16,8},{18,... | collective-permute-start | bytes 393224 | tf_op jit(solution)/shard_map/ppermute | solution.py:509
  17.8 13.6 %collective-permute-start.5 = (bf16[512,128]{1,0:T(8,128)(2,1)S(1)}, bf16[512,128]{1,0:T(8,128)(2,1)S(1)}, u32[]{:S(2)}, u32[]{:S(2)}) collective-permute-start(bf16[512,128]{1,0:T(8,128)(2,1)S(1)} %collective-permute-done.3.a), channel_id=1, source_target_pairs={{0,1},{1,0},{2,3},{3,2},{4,5},{5,4},{6,7},{7,6},{8,9},{9,8},{10,11... | collective-permute-start | bytes 393224 | tf_op jit(solution)/shard_map/ppermute | solution.py:497
  17.8 13.6 %collective-permute-start.6 = (bf16[512,128]{1,0:T(8,128)(2,1)S(1)}, bf16[512,128]{1,0:T(8,128)(2,1)S(1)}, u32[]{:S(2)}, u32[]{:S(2)}) collective-permute-start(bf16[512,128]{1,0:T(8,128)(2,1)S(1)} %collective-permute-done.4.b), channel_id=1, source_target_pairs={{0,1},{1,0},{2,3},{3,2},{4,5},{5,4},{6,7},{7,6},{8,9},{9,8},{10,11... | collective-permute-start | bytes 393224 | tf_op jit(solution)/shard_map/ppermute | solution.py:497
  18.3 0.9 %copy-start.2 = (bf16[32,32,27]{1,0,2:T(8,128)(2,1)S(1)}, bf16[32,32,27]{1,0,2:T(8,128)(2,1)}, u32[]{:S(2)}) copy-start(bf16[32,32,27]{1,0,2:T(8,128)(2,1)} %param.5) | copy-start | bytes 165892
  19.2 0.9 %copy-start.3 = (bf16[64,32,27]{0,1,2:T(8,128)(2,1)S(1)}, bf16[64,32,27]{0,1,2:T(8,128)(2,1)}, u32[]{:S(2)}) copy-start(bf16[64,32,27]{0,1,2:T(8,128)(2,1)} %param.6) | copy-start | bytes 331780
  23.5 12.4 %collective-permute-start.9 = (bf16[2,64,128]{2,1,0:T(8,128)(2,1)S(1)}, bf16[2,64,128]{2,1,0:T(8,128)(2,1)S(1)}, u32[]{:S(2)}, u32[]{:S(2)}) collective-permute-start(bf16[2,64,128]{2,1,0:T(8,128)(2,1)S(1)} %get-tuple-element.35.pooled), channel_id=1, source_target_pairs={{0,0},{2,2},{4,4},{6,6},{8,16},{10,18},{12,20},{14,22},{16,8},{18,... | collective-permute-start | bytes 98312 | tf_op jit(solution)/shard_map/ppermute | solution.py:509
  24.2 11.7 %collective-permute-start.8 = (bf16[2,64,128]{2,1,0:T(8,128)(2,1)S(1)}, bf16[2,64,128]{2,1,0:T(8,128)(2,1)S(1)}, u32[]{:S(2)}, u32[]{:S(2)}) collective-permute-start(bf16[2,64,128]{2,1,0:T(8,128)(2,1)S(1)} %get-tuple-element.35.pooled), channel_id=1, source_target_pairs={{0,8},{2,10},{4,12},{6,14},{8,0},{10,2},{12,4},{14,6},{16,24},{18,... | collective-permute-start | bytes 98312 | tf_op jit(solution)/shard_map/ppermute | solution.py:508
  34.4 10.3 %collective-permute-start.13 = (bf16[224,128]{1,0:T(8,128)(2,1)S(1)}, bf16[224,128]{1,0:T(8,128)(2,1)S(1)}, u32[]{:S(2)}, u32[]{:S(2)}) collective-permute-start(bf16[224,128]{1,0:T(8,128)(2,1)S(1)} %get-tuple-element.41.sums_in), channel_id=1, source_target_pairs={{0,24},{2,26},{4,28},{6,30},{8,16},{10,18},{12,20},{14,22},{16,8},... | collective-permute-start | bytes 172040 | tf_op jit(solution)/shard_map/ppermute | solution.py:491
  35.6 9.0 %collective-permute-start.11 = (bf16[224,128]{1,0:T(8,128)(2,1)S(1)}, bf16[224,128]{1,0:T(8,128)(2,1)S(1)}, u32[]{:S(2)}, u32[]{:S(2)}) collective-permute-start(bf16[224,128]{1,0:T(8,128)(2,1)S(1)} %get-tuple-element.41.sums_in), channel_id=1, source_target_pairs={{0,16},{2,18},{4,20},{6,22},{8,24},{10,26},{12,28},{14,30},{16,0},... | collective-permute-start | bytes 172040 | tf_op jit(solution)/shard_map/ppermute | solution.py:491
  38.9 6.3 %collective-permute-start.14 = (bf16[128,128]{1,0:T(8,128)(2,1)S(1)}, bf16[128,128]{1,0:T(8,128)(2,1)S(1)}, u32[]{:S(2)}, u32[]{:S(2)}) collective-permute-start(bf16[128,128]{1,0:T(8,128)(2,1)S(1)} %get-tuple-element.46), channel_id=1, source_target_pairs={{0,24},{2,26},{4,28},{6,30},{8,16},{10,18},{12,20},{14,22},{16,8},... | collective-permute-start | bytes 98312 | tf_op jit(solution)/shard_map/ppermute | solution.py:491
  41.3 4.9 %collective-permute-start.12 = (bf16[128,128]{1,0:T(8,128)(2,1)S(1)}, bf16[128,128]{1,0:T(8,128)(2,1)S(1)}, u32[]{:S(2)}, u32[]{:S(2)}) collective-permute-start(bf16[128,128]{1,0:T(8,128)(2,1)S(1)} %get-tuple-element.46), channel_id=1, source_target_pairs={{0,16},{2,18},{4,20},{6,22},{8,24},{10,26},{12,28},{14,30},{16,0},... | collective-permute-start | bytes 98312 | tf_op jit(solution)/shard_map/ppermute | solution.py:491
  43.3 4.5 %collective-permute-start.10 = (bf16[352,128]{1,0:T(8,128)(2,1)S(1)}, bf16[352,128]{1,0:T(8,128)(2,1)S(1)}, u32[]{:S(2)}, u32[]{:S(2)}) collective-permute-start(bf16[352,128]{1,0:T(8,128)(2,1)S(1)} %get-tuple-element.45.refs_0_), channel_id=1, source_target_pairs={{0,8},{2,10},{4,12},{6,14},{8,0},{10,2},{12,4},{14,6},{16,24},{18,... | collective-permute-start | bytes 270344 | tf_op jit(solution)/shard_map/ppermute | solution.py:491

commit v4 on v3

--- a/solution.py
+++ b/solution.py
@@ -69,23 +69,15 @@
     return sig * (1.0 + pre * (1.0 - sig))
 
 
-def pack_kernel(d, feats, cot, out, feats_in, cot_in, sems):
-    copies = [
-        pltpu.make_async_copy(feats, feats_in, sems.at[0]),
-        pltpu.make_async_copy(cot, cot_in, sems.at[1]),
-    ]
-    for copy in copies:
-        copy.start()
+def pack_kernel(d, raw, out):
     planes, width = d.planes, d.width
     lanes = d.height * d.half
-    turn = order_matrix(d.half, planes, d.height)
-    turn2 = order_matrix(d.half2, 1, d.height2)
-    copies[0].wait()
-    f = mm_t(feats_in[...], turn).astype(BF16)
+    rows = planes * lanes
+    f = mm_t(raw[:rows, :], order_matrix(d.half, planes, d.height)).astype(BF16)
     for p in range(planes):
         out[p * width : (p + 1) * width, :] = f[:, p * lanes : (p + 1) * lanes]
-    copies[1].wait()
-    out[planes * width :, :] = mm_t(cot_in[...], turn2).astype(BF16)
+    c = mm_t(raw[rows:, :], order_matrix(d.half2, 1, d.height2)).astype(BF16)
+    out[planes * width :, :] = c[: width // 2]
 
 
 def parity():
@@ -104,8 +96,7 @@
         mid[pl.ds(per + at * width2, width2), :] = ref[body:, :]
     side = EDGE * width
     for out, top in ((to_a, 1 - odd), (to_b, odd)):
-        out[:side, :] = mid[pl.ds(pl.multiple_of(top * (per - side), side // EDGE), side), :]
-        out[side:, :] = mid[pl.ds(pl.multiple_of(per + top * 2 * width2, width2), 2 * width2), :]
+        out[...] = mid[pl.ds(pl.multiple_of(top * (per - side), width), side), :]
 
 
 def band(out, a, at, size, groups, row, shift):
@@ -187,12 +178,12 @@
     return tall[0] if len(tall) == 1 else jnp.concatenate(tall, axis=0)
 
 
-def first_conv(d, halves, starts, count, f1):
+def first_conv(d, halves, starts, count, f1, pre=None):
     size = 3 * d.height * d.half
-    pre = jnp.zeros((len(starts) * count * d.width, d.height * d.mid), F32)
     for g, ref in enumerate(halves):
-        for a in range(3):
-            pre = pre + mm(stacked(ref, [q + a - 1 for q in starts], count), f1[a, g * size : (g + 1) * size])
+        for a in range(3 if ref is not None else 0):
+            term = mm(stacked(ref, [q + a - 1 for q in starts], count), f1[a, g * size : (g + 1) * size])
+            pre = term if pre is None else pre + term
     return pre
 
 
@@ -218,7 +209,7 @@
     return place < BLOCK, place >= lax.axis_size("depth") - BLOCK
 
 
-def middle_kernel(d, mi, mi_x, f1, xs, xs_x, slopes, rows, pooled, pair):
+def middle_kernel(d, mi, mi_x, f1, xs, xs_x, slopes, rows, for_a, for_b, pair):
     per = BLOCK * d.planes
     for p in range(per):
         at = slice(p * d.width, (p + 1) * d.width)
@@ -227,23 +218,38 @@
     pool = pool_matrix(d)
     pre = first_conv(d, (xs, xs_x), [EDGE + 1], per - 2, f1)
     first_level(d, pre, per - 2, pool, slopes, rows, 0)
-    for u in range(BLOCK - 2):
-        pooled[u] = pool_pair(d, rows, 2 * u + 1, pair, u).astype(BF16)
-
-
-def outer_kernel(d, a, b, a_x, b_x, xs_in, xs_x_in, f1, xs, xs_x, slopes, rows):
-    del xs_in, xs_x_in
-    per = BLOCK * d.planes
+    width2 = d.width // 2
+    odd = (lax.axis_index("depth") >> log2(BLOCK)) & 1
+    for u in range(2):
+        cell = pool_pair(d, rows, 2 * u + 1, pair, u).astype(BF16)
+        for out, top in ((for_a, 1 - odd), (for_b, odd)):
+            out[u * width2 : (u + 1) * width2, :] = cell
+            for g, ref in enumerate((mi, mi_x)):
+                at = pl.multiple_of(per * d.width + (top * (BLOCK - 2) + u) * width2, width2)
+                to = (2 + 2 * g + u) * width2
+                out[to : to + width2, :] = ref[pl.ds(at, width2), :]
+
+
+def spread_ends(d, a, b, xs):
     even = parity()
     first, last = ends()
-    for pair, ref in (((a, b), xs), ((a_x, b_x), xs_x)):
-        for p in range(EDGE):
-            x, y = (r[p * d.width : (p + 1) * d.width, :] for r in pair)
-            spread_plane(d, pick(True, even, x, y, first), ref, p)
-            spread_plane(d, pick(False, even, x, y, last), ref, EDGE + per + p)
-    pool = pool_matrix(d)
-    pre = first_conv(d, (xs, xs_x), [1, per + EDGE - 1], 3, f1)
-    first_level(d, pre, 6, pool, slopes, rows, 0)
+    for p in range(EDGE):
+        x, y = (r[p * d.width : (p + 1) * d.width, :] for r in (a, b))
+        spread_plane(d, pick(True, even, x, y, first), xs, p)
+        spread_plane(d, pick(False, even, x, y, last), xs, EDGE + BLOCK * d.planes + p)
+
+
+def outer_kernel(d, a, b, xs_in, f1, xs, part):
+    del xs_in
+    spread_ends(d, a, b, xs)
+    part[...] = first_conv(d, (xs, None), [1, BLOCK * d.planes + EDGE - 1], 3, f1)
+
+
+def close_kernel(d, a, b, xs_in, f1, part, xs, slopes, rows):
+    del xs_in
+    spread_ends(d, a, b, xs)
+    pre = first_conv(d, (None, xs), [1, BLOCK * d.planes + EDGE - 1], 3, f1, part[...])
+    first_level(d, pre, 6, pool_matrix(d), slopes, rows, 0)
 
 
 def spread_cell(cell, zs, u):
@@ -305,7 +311,7 @@
     spread_cell(jnp.where(first, 0.0, low), zs, 0)
     spread_cell(pool_pair(d, [rows_out[2], rows_mid[0]], 0, pair, 1), zs, 1)
     for u in range(BLOCK - 2):
-        spread_cell(pooled[u].astype(F32), zs, 2 + u)
+        spread_cell(pooled[u * width2 : (u + 1) * width2, :].astype(F32), zs, 2 + u)
     spread_cell(pool_pair(d, [rows_mid[per - 3], rows_out[3]], 0, pair, 2), zs, BLOCK)
     high = pool_pair(d, [rows_out[4], rows_out[5]], 0, pair, 3)
     spread_cell(jnp.where(last, 0.0, high), zs, BLOCK + 1)
@@ -324,7 +330,7 @@
 
 
 def main_kernel(
-    d, a, b, a_x, b_x, xs, slopes_mid, slopes_out, pooled_a, pooled_b, zs_in, gs_in, sums_in, f2, b2,
+    d, xs, slopes_mid, slopes_out, from_a, from_b, zs_in, gs_in, sums_in, f2, b2,
     grads_out, late, sums_out, zs, gs, up, g1,
 ):
     place = lax.axis_index("depth")
@@ -334,20 +340,21 @@
     width2 = width // 2
     wide2 = d.height2 * 2 * d.half2
     per = BLOCK * planes
-    side = EDGE * width
+
+    def adjacent(lower, k):
+        at = slice(k * width2, (k + 1) * width2)
+        return pick(lower, even, from_a[at, :], from_b[at, :], first if lower else last)
 
     zs[2 : 4 + BLOCK] = zs_in[...]
     gs[2 : 2 + BLOCK] = gs_in[...]
     for k in range(2):
-        spread_cell(pick(True, even, pooled_a[k], pooled_b[k], first).astype(F32), zs, k)
-        spread_cell(pick(False, even, pooled_a[k], pooled_b[k], last).astype(F32), zs, 4 + BLOCK + k)
+        spread_cell(adjacent(True, k).astype(F32), zs, k)
+        spread_cell(adjacent(False, k).astype(F32), zs, 4 + BLOCK + k)
     pre = second_conv(zs, [1, 3 + BLOCK], 2, f2)
     slope = slope_of(pre, sigmoid(pre))
     for k in range(4):
-        at = slice(side + (k % 2) * width2, side + (k % 2 + 1) * width2)
         lower = k < 2
-        cot = [pick(lower, even, x[at, :], y[at, :], first if lower else last) for x, y in ((a, b), (a_x, b_x))]
-        cot = jnp.concatenate(cot, axis=1).astype(F32)
+        cot = jnp.concatenate([adjacent(lower, 2 + 2 * g + k % 2) for g in range(2)], axis=1).astype(F32)
         spread_grad(cot * slope[k * width2 : (k + 1) * width2], gs, k if lower else BLOCK + k)
 
     inner = BLOCK + 2
@@ -475,17 +482,9 @@
 
     rows = d.planes * d.width + width2
     feats_shape = (d.half * d.planes * d.height, d.width)
-    (item,) = call(
-        pack_kernel,
-        [((rows, 128), BF16)],
-        [
-            pltpu.VMEM(feats_shape, BF16),
-            pltpu.VMEM((d.half2 * d.height2, width2), BF16),
-            pltpu.SemaphoreType.DMA((2,)),
-        ],
-        ins=pltpu.HBM,
-        mib=24,
-    )(feats.reshape(feats_shape), cotangent.reshape(-1, width2))
+    cells = jnp.pad(cotangent.reshape(-1, width2), ((0, 0), (0, d.width - width2)))
+    raw = jnp.concatenate([feats.reshape(feats_shape), cells])
+    (item,) = call(pack_kernel, [((rows, 128), BF16)])(raw)
 
     def xor(x, k):
         return lax.ppermute(x, "depth", [(i, i ^ k) for i in range(slabs)])
@@ -496,9 +495,10 @@
     def swap(x):
         return lax.ppermute(x, "chan", [(0, 1), (1, 0)])
 
-    side_rows = EDGE * d.width + 2 * width2
+    side_rows = EDGE * d.width
     mid, to_a, to_b = call(
-        sort_kernel, [((BLOCK * rows, 128), BF16), ((side_rows, 128), BF16), ((side_rows, 128), BF16)]
+        sort_kernel,
+        [((BLOCK * rows, 128), BF16), ((side_rows, 128), BF16), ((side_rows, 128), BF16)],
     )(item, *[gather(k) for k in range(1, BLOCK)])
     pair_a = [(i, i ^ BLOCK) for i in range(slabs)]
     inside = range(BLOCK, slabs - BLOCK)
@@ -535,30 +535,37 @@
         ins=pltpu.HBM,
         mib=24,
     )(w1, w2)
-    xs_mid, xs_mid_x, slopes_mid, rows_mid, pooled = call(
+    xs_mid, xs_mid_x, slopes_mid, rows_mid, for_a, for_b = call(
         middle_kernel,
         [
             ((per + 2 * EDGE, d.width, 3 * own1), BF16),
             ((per + 2 * EDGE, d.width, 3 * own1), BF16),
             ((per - 2, d.width, wide1), F32),
             ((per - 2, d.width, zl), F32),
-            ((BLOCK - 2, width2, zl), BF16),
+            ((6 * width2, zl), BF16),
+            ((6 * width2, zl), BF16),
         ],
         [pltpu.VMEM((BLOCK - 2, d.width, zl), F32)],
         flops=1 << 30,
     )(mid, mid_x, f1)
-    pooled_a, pooled_b = trade(pooled, pooled)
-    xs, _, slopes_out, rows_out = call(
+    from_a, from_b = trade(for_a, for_b)
+    ends_shape = (6 * d.width, wide1)
+    xs, part = call(
         outer_kernel,
+        [((per + 2 * EDGE, d.width, 3 * own1), BF16), (ends_shape, F32)],
+        flops=1 << 30,
+        aliases={2: 0},
+    )(a, b, xs_mid, f1)
+    _, slopes_out, rows_out = call(
+        close_kernel,
         [
-            ((per + 2 * EDGE, d.width, 3 * own1), BF16),
             ((per + 2 * EDGE, d.width, 3 * own1), BF16),
             ((6, d.width, wide1), F32),
             ((6, d.width, zl), F32),
         ],
         flops=1 << 30,
-        aliases={4: 0, 5: 1},
-    )(a, b, a_x, b_x, xs_mid, xs_mid_x, f1)
+        aliases={2: 0},
+    )(a_x, b_x, xs_mid_x, f1, part)
 
     fan = min(4, blocks)
 
@@ -575,7 +582,7 @@
         ],
         [pltpu.VMEM((BLOCK, d.width, zl), F32)],
         flops=1 << 30,
-    )(mid, mid_x, pooled, rows_mid, rows_out, f2)
+    )(mid, mid_x, for_a, rows_mid, rows_out, f2)
     early = [early] + [move(early, k) for k in range(2, fan)]
     grads, late, sums = call(
         main_kernel,
@@ -591,7 +598,7 @@
             pltpu.VMEM((per + 2, d.width, wide1), BF16),
         ],
         flops=1 << 32,
-    )(a, b, a_x, b_x, xs, slopes_mid, slopes_out, pooled_a, pooled_b, zs, gs, early[0], f2, b2)
+    )(xs, slopes_mid, slopes_out, from_a, from_b, zs, gs, early[0], f2, b2)
 
     parts = [(sums,)]
     for k in range(fan - 1, 1, -1):
@@ -608,7 +615,10 @@
         radix *= fan
     parts = sum(parts, ())
     (grad,) = call(
-        feats_kernel, [(feats_shape, BF16)], [pltpu.VMEM((d.planes + 2, d.width, 3 * wide1), BF16)], flops=1 << 30
+        feats_kernel,
+        [(feats_shape, BF16)],
+        [pltpu.VMEM((d.planes + 2, d.width, 3 * wide1), BF16)],
+        flops=1 << 30,
     )(grads, b1)
     out1, out2 = call(
         final_kernel,

time: 49.3 us -> 44 us (0.89)
  waiting for transfers between devices: 11.1 us -> 7.5 us
  local copies, waits for them, and re-layouts: 3.46 us -> 1.87 us
  other arithmetic: 0 us -> 0.87 us
  starting transfers between devices: 21.3 us -> 20.5 us
    ppermute x2, waiting for transfers between devices: 3.6 us -> 0.01 us  [trade(): a = lax.ppermute(x_a, 'depth', pair_a)]
    ppermute x2, starting transfers between devices: 8.77 us -> 6.1 us  [trade(): a = lax.ppermute(x_a, 'depth', pair_a)]
    ppermute x8, starting transfers between devices: 10.6 us -> 12.5 us  [xor(): return lax.ppermute(x, 'depth', [(i, i ^ k) for i in range(slabs)])]
    unnamed x8 -> x4, local copies, waits for them, and re-layouts: 3.46 us -> 1.87 us
    concatenate x0 -> x1, other arithmetic: none -> 0.87 us  [shards(): raw = jnp.concatenate([feats.reshape(feats_shape), cells])]
    pallas_call x9 -> x10, Pallas kernels: 12.4 us -> 12.2 us  [run(): pl.pallas_call(functools.partial(kernel, d), out_shape=[jax.ShapeDtypeStr...]
  transfers between devices with their start and end apart: 15 -> 15, of which waited for: 7 -> 6; matrix products, arithmetic and copies ran while one was open for 0% -> 0% of each run, Pallas kernels for 22% -> 25%
where the time goes in v4:
time: 44 us; the launch traced here: 43.8 us
  starting transfers between devices  20.5 us (47%)
  Pallas kernels  12.2 us (28%)
  waiting for transfers between devices  7.5 us (17%)
  local copies, waits for them, and re-layouts  1.87 us (4%)
  other arithmetic  0.87 us (2%)
  between operations  0.76 us (2%)
    ppermute x8, starting transfers between devices, xor(): return lax.ppermute(x, 'depth', [(i, i ^ k) for i in range(slabs)])  12.5 us
    pallas_call x10, Pallas kernels, run(): pl.pallas_call(functools.partial(kernel, d), out_shape=[jax.ShapeDtypeStr...  12.2 us
    ppermute x8, waiting for transfers between devices, xor(): return lax.ppermute(x, 'depth', [(i, i ^ k) for i in range(slabs)])  7.48 us
    ppermute x2, starting transfers between devices, trade(): a = lax.ppermute(x_a, 'depth', pair_a)  6.1 us
    unnamed x4, local copies, waits for them, and re-layouts  1.87 us
    ppermute x2, starting transfers between devices, trade(): b = lax.ppermute(x_b, 'depth', pair_b)  1.31 us
  transfers between devices with their start and end apart: 15, of which 6 were waited for; matrix products, arithmetic and copies ran while one was open for 0% of the time, Pallas kernels for 25%

profile of v4, /device:TPU:0, one launch (start us, length us, event | category | flops | bytes accessed | tf_op | source)
XLA Modules:
  0.0 43.8 jit_solution(5489419432911353225)
XLA Ops:
  0.6 0.9 %fusion.1.raw = bf16[384,128]{1,0:T(8,128)(2,1)S(1)} fusion(bf16[128,64]{1,0:T(8,128)(2,1)} %bitcast.18, bf16[256,128]{1,0:T(8,128)(2,1)} %bitcast.17), kind=kLoop, calls=%fused_computation.2 | loop fusion | flops 294912 | bytes 180224 | tf_op jit(solution)/shard_map/concatenate | solution.py:486
  1.5 0.2 shard_map.67.i0
  1.7 3.0 %collective-permute-start = (bf16[320,128]{1,0:T(8,128)(2,1)S(1)}, bf16[320,128]{1,0:T(8,128)(2,1)S(1)}, u32[]{:S(2)}, u32[]{:S(2)}) collective-permute-start(bf16[320,128]{1,0:T(8,128)(2,1)S(1)} %shard_map.67.i0), channel_id=1, source_target_pairs={{0,2},{2,0},{4,6},{6,4},{8,10},{10,8},{12,14},{14,12},{16,18},{18,... | collective-permute-start | bytes 245768 | tf_op jit(solution)/shard_map/ppermute | solution.py:490
  4.8 1.5 %collective-permute-start.1 = (bf16[320,128]{1,0:T(8,128)(2,1)S(1)}, bf16[320,128]{1,0:T(8,128)(2,1)S(1)}, u32[]{:S(2)}, u32[]{:S(2)}) collective-permute-start(bf16[320,128]{1,0:T(8,128)(2,1)S(1)} %shard_map.67.i0), channel_id=1, source_target_pairs={{0,4},{2,6},{4,0},{6,2},{8,12},{10,14},{12,8},{14,10},{16,20},{18,... | collective-permute-start | bytes 245768 | tf_op jit(solution)/shard_map/ppermute | solution.py:490
  6.3 1.2 %collective-permute-done.i1 = bf16[320,128]{1,0:T(8,128)(2,1)S(1)} collective-permute-done((bf16[320,128]{1,0:T(8,128)(2,1)S(1)}, bf16[320,128]{1,0:T(8,128)(2,1)S(1)}, u32[]{:S(2)}, u32[]{:S(2)}) %collective-permute-start) | collective-permute-done | bytes 81952 | tf_op jit(solution)/shard_map/ppermute | solution.py:490
  7.5 2.6 %collective-permute-done.1.i2 = bf16[320,128]{1,0:T(8,128)(2,1)S(1)} collective-permute-done((bf16[320,128]{1,0:T(8,128)(2,1)S(1)}, bf16[320,128]{1,0:T(8,128)(2,1)S(1)}, u32[]{:S(2)}, u32[]{:S(2)}) %collective-permute-start.1) | collective-permute-done | bytes 81952 | tf_op jit(solution)/shard_map/ppermute | solution.py:490
  10.1 1.5 %collective-permute-done.2.i3 = bf16[320,128]{1,0:T(8,128)(2,1)S(1)} collective-permute-done((bf16[320,128]{1,0:T(8,128)(2,1)S(1)}, bf16[320,128]{1,0:T(8,128)(2,1)S(1)}, u32[]{:S(2)}, u32[]{:S(2)}) %collective-permute-start.2) | collective-permute-done | bytes 81952 | tf_op jit(solution)/shard_map/ppermute | solution.py:490
  11.7 0.1 collective-permute-start.5
  11.7 1.6 %collective-permute-start.3 = (bf16[384,128]{1,0:T(8,128)(2,1)S(1)}, bf16[384,128]{1,0:T(8,128)(2,1)S(1)}, u32[]{:S(2)}, u32[]{:S(2)}) collective-permute-start(bf16[384,128]{1,0:T(8,128)(2,1)S(1)} %get-tuple-element.28), channel_id=1, source_target_pairs={{0,8},{2,10},{4,12},{6,14},{8,0},{10,2},{12,4},{14,6},{16,24},{18,... | collective-permute-start | bytes 294920 | tf_op jit(solution)/shard_map/ppermute | solution.py:508
  13.4 0.7 %collective-permute-start.4 = (bf16[384,128]{1,0:T(8,128)(2,1)S(1)}, bf16[384,128]{1,0:T(8,128)(2,1)S(1)}, u32[]{:S(2)}, u32[]{:S(2)}) collective-permute-start(bf16[384,128]{1,0:T(8,128)(2,1)S(1)} %get-tuple-element.29), channel_id=1, source_target_pairs={{0,0},{2,2},{4,4},{6,6},{8,16},{10,18},{12,20},{14,22},{16,8},{18,... | collective-permute-start | bytes 294920 | tf_op jit(solution)/shard_map/ppermute | solution.py:509
  14.1 0.9 %copy-done = bf16[32,32,27]{1,0,2:T(8,128)(2,1)S(1)} copy-done((bf16[32,32,27]{1,0,2:T(8,128)(2,1)S(1)}, bf16[32,32,27]{1,0,2:T(8,128)(2,1)}, u32[]{:S(2)}) %copy-start) | copy-done | bytes 55320
  15.0 0.9 %copy-done.1 = bf16[64,32,27]{0,1,2:T(8,128)(2,1)S(1)} copy-done((bf16[64,32,27]{0,1,2:T(8,128)(2,1)S(1)}, bf16[64,32,27]{0,1,2:T(8,128)(2,1)}, u32[]{:S(2)}) %copy-start.1) | copy-done | bytes 110616
  15.9 1.7 %shard_map.69 = (bf16[3,768,256]{2,1,0:T(8,128)(2,1)S(1)}, bf16[3,768,128]{2,1,0:T(8,128)(2,1)S(1)}, bf16[3,384,256]{2,1,0:T(8,128)(2,1)S(1)}, bf16[3,768,256]{2,1,0:T(8,128)(2,1)S(1)}) custom-call(bf16[864,32]{1,0:T(8,128)(2,1)S(1)} %bitcast.15, bf16[864,64]{1,0:T(8,128)(2,1)S(1)} %bitcast.16), custom_call_target="tpu_custom_call" | custom-call | flops 1073741824 | bytes 1048576 | tf_op jit(solution)/shard_map/pallas_call | solution.py:470
  17.6 0.2 collective-permute-start.6
  17.8 0.3 collective-permute-start.7
  18.2 1.7 %shard_map.70 = (bf16[14,128,384]{2,1,0:T(8,128)(2,1)S(1)}, bf16[14,128,384]{2,1,0:T(8,128)(2,1)S(1)}, f32[6,128,256]{2,1,0:T(8,128)S(1)}, f32[6,128,128]{2,1,0:...) custom-call(bf16[1280,128]{1,0:T(8,128)(2,1)S(1)} %get-tuple-element.30.mi, ...), custom_call_target="tpu_custom_call" | custom-call | flops 1073741824 | bytes 1048576 | tf_op jit(solution)/shard_map/pallas_call | solution.py:470
  19.9 4.5 %collective-permute-start.8 = (bf16[384,128]{1,0:T(8,128)(2,1)S(1)}, bf16[384,128]{1,0:T(8,128)(2,1)S(1)}, u32[]{:S(2)}, u32[]{:S(2)}) collective-permute-start(bf16[384,128]{1,0:T(8,128)(2,1)S(1)} %get-tuple-element.38.pooled), channel_id=1, source_target_pairs={{0,8},{2,10},{4,12},{6,14},{8,0},{10,2},{12,4},{14,6},{16,24},{18,... | collective-permute-start | bytes 294920 | tf_op jit(solution)/shard_map/ppermute | solution.py:508
  24.3 0.7 %collective-permute-start.9 = (bf16[384,128]{1,0:T(8,128)(2,1)S(1)}, bf16[384,128]{1,0:T(8,128)(2,1)S(1)}, u32[]{:S(2)}, u32[]{:S(2)}) collective-permute-start(bf16[384,128]{1,0:T(8,128)(2,1)S(1)} %get-tuple-element.39), channel_id=1, source_target_pairs={{0,0},{2,2},{4,4},{6,6},{8,16},{10,18},{12,20},{14,22},{16,8},{18,... | collective-permute-start | bytes 294920 | tf_op jit(solution)/shard_map/ppermute | solution.py:509
  25.0 0.8 %shard_map.71 = (bf16[14,128,384]{2,1,0:T(8,128)(2,1)S(1)}, f32[768,256]{1,0:T(8,128)S(1)}) custom-call(bf16[384,128]{1,0:T(8,128)(2,1)S(1)} %collective-permute-done.3.a, bf16[384,128]{1,0:T(8,128)(2,1)S(1)} %collective-permute-done.4.b, bf16[14,128,384]{2,1,0:T(8,128)(2,1)S(1)} %get-tuple-element.32.xs_in, ...), custom_call_target="tpu_custom_call", output_to_operand_aliasing={{0}: (2, {})} | custom-call | flops 1073741824 | bytes 1048576 | tf_op jit(solution)/shard_map/pallas_call | solution.py:470
  25.8 1.1 %shard_map.72 = (bf16[14,128,384]{2,1,0:T(8,128)(2,1)S(1)}, f32[6,128,256]{2,1,0:T(8,128)S(1)}, f32[6,128,128]{2,1,0:T(8,128)S(1)}) custom-call(bf16[384,128]{1,0:T(8,128)(2,1)S(1)} %collective-permute-done.6.a, bf16[384,128]{1,0:T(8,128)(2,1)S(1)} %collective-permute-done.7.b, ...), custom_call_target="tpu_custom_call", output_to_operand_aliasing={{0}: (2, {})} | custom-call | flops 1073741824 | bytes 1048576 | tf_op jit(solution)/shard_map/pallas_call | solution.py:470
  26.9 1.4 %shard_map.73 = (bf16[6,64,384]{2,1,0:T(8,128)(2,1)S(1)}, bf16[4,64,768]{2,1,0:T(8,128)(2,1)S(1)}, bf16[224,128]{1,0:T(8,128)(2,1)S(1)}) custom-call(bf16[1280,128]{1,0:T(8,128)(2,1)S(1)} %get-tuple-element.30.mi, bf16[1280,128]{1,0:T(8,128)(2,1)S(1)} %collective-permute-done.5.mi_x, bf16[384,128]{1,0:T(8,128)(2,1)S(1)} %get-tuple-element.38.pooled, ...), custom_call_target="tpu_custom_call" | custom-call | flops 1073741824 | bytes 1048576 | tf_op jit(solution)/shard_map/pallas_call | solution.py:470
  28.3 2.8 %collective-permute-start.11 = (bf16[224,128]{1,0:T(8,128)(2,1)S(1)}, bf16[224,128]{1,0:T(8,128)(2,1)S(1)}, u32[]{:S(2)}, u32[]{:S(2)}) collective-permute-start(bf16[224,128]{1,0:T(8,128)(2,1)S(1)} %get-tuple-element.45.sums_in), channel_id=1, source_target_pairs={{0,16},{2,18},{4,20},{6,22},{8,24},{10,26},{12,28},{14,30},{16,0},... | collective-permute-start | bytes 172040 | tf_op jit(solution)/shard_map/ppermute | solution.py:490
  31.0 1.6 %collective-permute-start.13 = (bf16[224,128]{1,0:T(8,128)(2,1)S(1)}, bf16[224,128]{1,0:T(8,128)(2,1)S(1)}, u32[]{:S(2)}, u32[]{:S(2)}) collective-permute-start(bf16[224,128]{1,0:T(8,128)(2,1)S(1)} %get-tuple-element.45.sums_in), channel_id=1, source_target_pairs={{0,24},{2,26},{4,28},{6,30},{8,16},{10,18},{12,20},{14,22},{16,8},... | collective-permute-start | bytes 172040 | tf_op jit(solution)/shard_map/ppermute | solution.py:490
  32.6 2.9 %shard_map.74 = (bf16[4,128,256]{2,1,0:T(8,128)(2,1)S(1)}, bf16[128,128]{1,0:T(8,128)(2,1)S(1)}, bf16[352,128]{1,0:T(8,128)(2,1)S(1)}) custom-call(bf16[14,128,384]{2,1,0:T(8,128)(2,1)S(1)} %get-tuple-element.33.xs, f32[6,128,256]{2,1,0:T(8,128)S(1)} %get-tuple-element.34.slopes_mid, f32[6,128,256]{2,1,0:T(8,128)S(1)} %get-tuple-element.37.slopes_out, ...), custom_call_target="tpu_custom_call" | custom-call | flops 4294967296 | bytes 1048576 | tf_op jit(solution)/shard_map/pallas_call | solution.py:470
  35.6 0.1 collective-permute-start.12
  35.7 2.3 %collective-permute-start.14 = (bf16[128,128]{1,0:T(8,128)(2,1)S(1)}, bf16[128,128]{1,0:T(8,128)(2,1)S(1)}, u32[]{:S(2)}, u32[]{:S(2)}) collective-permute-start(bf16[128,128]{1,0:T(8,128)(2,1)S(1)} %get-tuple-element.50), channel_id=1, source_target_pairs={{0,24},{2,26},{4,28},{6,30},{8,16},{10,18},{12,20},{14,22},{16,8},... | collective-permute-start | bytes 98312 | tf_op jit(solution)/shard_map/ppermute | solution.py:490
  37.9 1.2 %collective-permute-start.10 = (bf16[352,128]{1,0:T(8,128)(2,1)S(1)}, bf16[352,128]{1,0:T(8,128)(2,1)S(1)}, u32[]{:S(2)}, u32[]{:S(2)}) collective-permute-start(bf16[352,128]{1,0:T(8,128)(2,1)S(1)} %get-tuple-element.49.refs_0_), channel_id=1, source_target_pairs={{0,8},{2,10},{4,12},{6,14},{8,0},{10,2},{12,4},{14,6},{16,24},{18,... | collective-permute-start | bytes 270344 | tf_op jit(solution)/shard_map/ppermute | solution.py:490
  39.1 1.3 %shard_map.75 = bf16[256,128]{1,0:T(8,128)(2,1)} custom-call(bf16[4,128,256]{2,1,0:T(8,128)(2,1)S(1)} %get-tuple-element.47.g1, bf16[3,768,128]{2,1,0:T(8,128)(2,1)S(1)} %get-tuple-element.48.b1), custom_call_target="tpu_custom_call" | custom-call | flops 1073741824 | bytes 1048576 | tf_op jit(solution)/shard_map/pallas_call | solution.py:470
  40.5 0.4 collective-permute-done.12.refs_3_
  40.8 1.0 %collective-permute-done.14.refs_5_ = bf16[128,128]{1,0:T(8,128)(2,1)S(1)} collective-permute-done((bf16[128,128]{1,0:T(8,128)(2,1)S(1)}, bf16[128,128]{1,0:T(8,128)(2,1)S(1)}, u32[]{:S(2)}, u32[]{:S(2)}) %collective-permute-start.14) | collective-permute-done | bytes 32800 | tf_op jit(solution)/shard_map/ppermute | solution.py:490
  41.8 0.8 %collective-permute-done.10.refs_1_ = bf16[352,128]{1,0:T(8,128)(2,1)S(1)} collective-permute-done((bf16[352,128]{1,0:T(8,128)(2,1)S(1)}, bf16[352,128]{1,0:T(8,128)(2,1)S(1)}, u32[]{:S(2)}, u32[]{:S(2)}) %collective-permute-start.10) | collective-permute-done | bytes 90144 | tf_op jit(solution)/shard_map/ppermute | solution.py:490
  42.6 1.2 %shard_map.76 = (f32[432,32]{1,0:T(8,128)}, f32[432,64]{1,0:T(8,128)}) custom-call(bf16[352,128]{1,0:T(8,128)(2,1)S(1)} %get-tuple-element.49.refs_0_, bf16[352,128]{1,0:T(8,128)(2,1)S(1)} %collective-permute-done.10.refs_1_, bf16[224,128]{1,0:T(8,128)(2,1)S(1)} %collective-permute-done.11.refs_2_, bf16[128,128]{1,0:T(8,128)(2,1)S(1)} %collective-permute-done.12.refs_3_, ...), custom_call_target="tpu_custom_call" | custom-call | bytes 1048576 | tf_op jit(solution)/shard_map/pallas_call | solution.py:470
  (13 shorter events, 0.1 us)
Async XLA Ops:
  1.7 5.7 %collective-permute-start = (bf16[320,128]{1,0:T(8,128)(2,1)S(1)}, bf16[320,128]{1,0:T(8,128)(2,1)S(1)}, u32[]{:S(2)}, u32[]{:S(2)}) collective-permute-start(bf16[320,128]{1,0:T(8,128)(2,1)S(1)} %shard_map.67.i0), channel_id=1, source_target_pairs={{0,2},{2,0},{4,6},{6,4},{8,10},{10,8},{12,14},{14,12},{16,18},{18,... | collective-permute-start | bytes 245768 | tf_op jit(solution)/shard_map/ppermute | solution.py:490
  4.8 5.3 %collective-permute-start.1 = (bf16[320,128]{1,0:T(8,128)(2,1)S(1)}, bf16[320,128]{1,0:T(8,128)(2,1)S(1)}, u32[]{:S(2)}, u32[]{:S(2)}) collective-permute-start(bf16[320,128]{1,0:T(8,128)(2,1)S(1)} %shard_map.67.i0), channel_id=1, source_target_pairs={{0,4},{2,6},{4,0},{6,2},{8,12},{10,14},{12,8},{14,10},{16,20},{18,... | collective-permute-start | bytes 245768 | tf_op jit(solution)/shard_map/ppermute | solution.py:490
  6.3 5.3 %collective-permute-start.2 = (bf16[320,128]{1,0:T(8,128)(2,1)S(1)}, bf16[320,128]{1,0:T(8,128)(2,1)S(1)}, u32[]{:S(2)}, u32[]{:S(2)}) collective-permute-start(bf16[320,128]{1,0:T(8,128)(2,1)S(1)} %shard_map.67.i0), channel_id=1, source_target_pairs={{0,6},{2,4},{4,2},{6,0},{8,14},{10,12},{12,10},{14,8},{16,22},{18,... | collective-permute-start | bytes 245768 | tf_op jit(solution)/shard_map/ppermute | solution.py:490
  11.7 6.5 %collective-permute-start.5 = (bf16[1280,128]{1,0:T(8,128)(2,1)S(1)}, bf16[1280,128]{1,0:T(8,128)(2,1)S(1)}, u32[]{:S(2)}, u32[]{:S(2)}) collective-permute-start(bf16[1280,128]{1,0:T(8,128)(2,1)S(1)} %get-tuple-element.30.mi), channel_id=1, source_target_pairs={{0,1},{1,0},{2,3},{3,2},{4,5},{5,4},{6,7},{7,6},{8,9},{9,8},{10,11... | collective-permute-start | bytes 983048 | tf_op jit(solution)/shard_map/ppermute | solution.py:496
  11.7 5.8 %collective-permute-start.3 = (bf16[384,128]{1,0:T(8,128)(2,1)S(1)}, bf16[384,128]{1,0:T(8,128)(2,1)S(1)}, u32[]{:S(2)}, u32[]{:S(2)}) collective-permute-start(bf16[384,128]{1,0:T(8,128)(2,1)S(1)} %get-tuple-element.28), channel_id=1, source_target_pairs={{0,8},{2,10},{4,12},{6,14},{8,0},{10,2},{12,4},{14,6},{16,24},{18,... | collective-permute-start | bytes 294920 | tf_op jit(solution)/shard_map/ppermute | solution.py:508
  13.4 4.4 %collective-permute-start.4 = (bf16[384,128]{1,0:T(8,128)(2,1)S(1)}, bf16[384,128]{1,0:T(8,128)(2,1)S(1)}, u32[]{:S(2)}, u32[]{:S(2)}) collective-permute-start(bf16[384,128]{1,0:T(8,128)(2,1)S(1)} %get-tuple-element.29), channel_id=1, source_target_pairs={{0,0},{2,2},{4,4},{6,6},{8,16},{10,18},{12,20},{14,22},{16,8},{18,... | collective-permute-start | bytes 294920 | tf_op jit(solution)/shard_map/ppermute | solution.py:509
  14.1 0.9 %copy-start = (bf16[32,32,27]{1,0,2:T(8,128)(2,1)S(1)}, bf16[32,32,27]{1,0,2:T(8,128)(2,1)}, u32[]{:S(2)}) copy-start(bf16[32,32,27]{1,0,2:T(8,128)(2,1)} %param.5) | copy-start | bytes 165892
  15.0 0.9 %copy-start.1 = (bf16[64,32,27]{0,1,2:T(8,128)(2,1)S(1)}, bf16[64,32,27]{0,1,2:T(8,128)(2,1)}, u32[]{:S(2)}) copy-start(bf16[64,32,27]{0,1,2:T(8,128)(2,1)} %param.6) | copy-start | bytes 331780
  17.6 8.2 %collective-permute-start.6 = (bf16[384,128]{1,0:T(8,128)(2,1)S(1)}, bf16[384,128]{1,0:T(8,128)(2,1)S(1)}, u32[]{:S(2)}, u32[]{:S(2)}) collective-permute-start(bf16[384,128]{1,0:T(8,128)(2,1)S(1)} %collective-permute-done.3.a), channel_id=1, source_target_pairs={{0,1},{1,0},{2,3},{3,2},{4,5},{5,4},{6,7},{7,6},{8,9},{9,8},{10,11... | collective-permute-start | bytes 294920 | tf_op jit(solution)/shard_map/ppermute | solution.py:496
  17.8 8.0 %collective-permute-start.7 = (bf16[384,128]{1,0:T(8,128)(2,1)S(1)}, bf16[384,128]{1,0:T(8,128)(2,1)S(1)}, u32[]{:S(2)}, u32[]{:S(2)}) collective-permute-start(bf16[384,128]{1,0:T(8,128)(2,1)S(1)} %collective-permute-done.4.b), channel_id=1, source_target_pairs={{0,1},{1,0},{2,3},{3,2},{4,5},{5,4},{6,7},{7,6},{8,9},{9,8},{10,11... | collective-permute-start | bytes 294920 | tf_op jit(solution)/shard_map/ppermute | solution.py:496
  19.9 12.7 %collective-permute-start.8 = (bf16[384,128]{1,0:T(8,128)(2,1)S(1)}, bf16[384,128]{1,0:T(8,128)(2,1)S(1)}, u32[]{:S(2)}, u32[]{:S(2)}) collective-permute-start(bf16[384,128]{1,0:T(8,128)(2,1)S(1)} %get-tuple-element.38.pooled), channel_id=1, source_target_pairs={{0,8},{2,10},{4,12},{6,14},{8,0},{10,2},{12,4},{14,6},{16,24},{18,... | collective-permute-start | bytes 294920 | tf_op jit(solution)/shard_map/ppermute | solution.py:508
  24.3 8.3 %collective-permute-start.9 = (bf16[384,128]{1,0:T(8,128)(2,1)S(1)}, bf16[384,128]{1,0:T(8,128)(2,1)S(1)}, u32[]{:S(2)}, u32[]{:S(2)}) collective-permute-start(bf16[384,128]{1,0:T(8,128)(2,1)S(1)} %get-tuple-element.39), channel_id=1, source_target_pairs={{0,0},{2,2},{4,4},{6,6},{8,16},{10,18},{12,20},{14,22},{16,8},{18,... | collective-permute-start | bytes 294920 | tf_op jit(solution)/shard_map/ppermute | solution.py:509
  28.3 12.2 %collective-permute-start.11 = (bf16[224,128]{1,0:T(8,128)(2,1)S(1)}, bf16[224,128]{1,0:T(8,128)(2,1)S(1)}, u32[]{:S(2)}, u32[]{:S(2)}) collective-permute-start(bf16[224,128]{1,0:T(8,128)(2,1)S(1)} %get-tuple-element.45.sums_in), channel_id=1, source_target_pairs={{0,16},{2,18},{4,20},{6,22},{8,24},{10,26},{12,28},{14,30},{16,0},... | collective-permute-start | bytes 172040 | tf_op jit(solution)/shard_map/ppermute | solution.py:490
  31.0 9.5 %collective-permute-start.13 = (bf16[224,128]{1,0:T(8,128)(2,1)S(1)}, bf16[224,128]{1,0:T(8,128)(2,1)S(1)}, u32[]{:S(2)}, u32[]{:S(2)}) collective-permute-start(bf16[224,128]{1,0:T(8,128)(2,1)S(1)} %get-tuple-element.45.sums_in), channel_id=1, source_target_pairs={{0,24},{2,26},{4,28},{6,30},{8,16},{10,18},{12,20},{14,22},{16,8},... | collective-permute-start | bytes 172040 | tf_op jit(solution)/shard_map/ppermute | solution.py:490
  35.6 5.2 %collective-permute-start.12 = (bf16[128,128]{1,0:T(8,128)(2,1)S(1)}, bf16[128,128]{1,0:T(8,128)(2,1)S(1)}, u32[]{:S(2)}, u32[]{:S(2)}) collective-permute-start(bf16[128,128]{1,0:T(8,128)(2,1)S(1)} %get-tuple-element.50), channel_id=1, source_target_pairs={{0,16},{2,18},{4,20},{6,22},{8,24},{10,26},{12,28},{14,30},{16,0},... | collective-permute-start | bytes 98312 | tf_op jit(solution)/shard_map/ppermute | solution.py:490
  35.7 6.1 %collective-permute-start.14 = (bf16[128,128]{1,0:T(8,128)(2,1)S(1)}, bf16[128,128]{1,0:T(8,128)(2,1)S(1)}, u32[]{:S(2)}, u32[]{:S(2)}) collective-permute-start(bf16[128,128]{1,0:T(8,128)(2,1)S(1)} %get-tuple-element.50), channel_id=1, source_target_pairs={{0,24},{2,26},{4,28},{6,30},{8,16},{10,18},{12,20},{14,22},{16,8},... | collective-permute-start | bytes 98312 | tf_op jit(solution)/shard_map/ppermute | solution.py:490
  37.9 4.7 %collective-permute-start.10 = (bf16[352,128]{1,0:T(8,128)(2,1)S(1)}, bf16[352,128]{1,0:T(8,128)(2,1)S(1)}, u32[]{:S(2)}, u32[]{:S(2)}) collective-permute-start(bf16[352,128]{1,0:T(8,128)(2,1)S(1)} %get-tuple-element.49.refs_0_), channel_id=1, source_target_pairs={{0,8},{2,10},{4,12},{6,14},{8,0},{10,2},{12,4},{14,6},{16,24},{18,... | collective-permute-start | bytes 270344 | tf_op jit(solution)/shard_map/ppermute | solution.py:490

commit v5 on v4

--- a/solution.py
+++ b/solution.py
@@ -180,11 +180,10 @@
 
 def first_conv(d, halves, starts, count, f1, pre=None):
     size = 3 * d.height * d.half
-    for g, ref in enumerate(halves):
-        for a in range(3 if ref is not None else 0):
-            term = mm(stacked(ref, [q + a - 1 for q in starts], count), f1[a, g * size : (g + 1) * size])
-            pre = term if pre is None else pre + term
-    return pre
+    taps = [(g, ref, a) for g, ref in enumerate(halves) if ref is not None for a in range(3)]
+    fields = jnp.concatenate([stacked(ref, [q + a - 1 for q in starts], count) for g, ref, a in taps], axis=1)
+    out = mm(fields, jnp.concatenate([f1[a, g * size : (g + 1) * size] for g, ref, a in taps], axis=0))
+    return out if pre is None else out + pre
 
 
 def first_level(d, pre, count, pool, slopes, rows, at):
@@ -269,11 +268,15 @@
 
 
 def second_conv(zs, starts, count, f2):
-    pre = None
-    for a in range(3):
-        part = mm(stacked(zs, [q + a - 1 for q in starts], count), f2[a])
-        pre = part if pre is None else pre + part
-    return pre
+    fields = jnp.concatenate([stacked(zs, [q + a - 1 for q in starts], count) for a in range(3)], axis=1)
+    return mm(fields, f2[...].reshape(-1, f2.shape[2]))
+
+
+def weight_product(center, ref, starts, count):
+    fields = jnp.concatenate([stacked(ref, [q], count) for q in starts], axis=1)
+    out = mm_t(center, fields)
+    size = ref.shape[2]
+    return [out[:, k * size : (k + 1) * size] for k in range(len(starts))]
 
 
 def collect(d, parts, groups, height, chans, tiles, first_slot):
@@ -322,7 +325,7 @@
         cot = jnp.concatenate([mi[at, :], mi_x[at, :]], axis=1).astype(F32)
         spread_grad(cot * slope[u * width2 : (u + 1) * width2], gs, u)
     center = gs[:, :, wide2 : 2 * wide2].reshape(BLOCK * width2, wide2)
-    parts = [mm_t(center, stacked(zs, [a], BLOCK)) for a in range(3)]
+    parts = weight_product(center, zs, range(3), BLOCK)
     tiles = {}
     collect(d, parts, 2, d.height2, d.half2, tiles, 0)
     for t, tile in tiles.items():
@@ -330,15 +333,14 @@
 
 
 def main_kernel(
-    d, xs, slopes_mid, slopes_out, from_a, from_b, zs_in, gs_in, sums_in, f2, b2,
-    grads_out, late, sums_out, zs, gs, up, g1,
+    d, xs, slopes_mid, slopes_out, from_a, from_b, zs_in, gs_in, f2, b2,
+    grads_out, late, zs, gs, up, g1,
 ):
     place = lax.axis_index("depth")
     first, last = ends()
     even = parity()
     planes, width, wide1 = d.planes, d.width, d.height * d.mid
     width2 = width // 2
-    wide2 = d.height2 * 2 * d.half2
     per = BLOCK * planes
 
     def adjacent(lower, k):
@@ -358,10 +360,8 @@
         spread_grad(cot * slope[k * width2 : (k + 1) * width2], gs, k if lower else BLOCK + k)
 
     inner = BLOCK + 2
-    back = None
-    for t in range(3):
-        part = mm(gs[2 - t : 2 - t + inner].reshape(inner * width2, 3 * wide2), b2[t])
-        back = part if back is None else back + part
+    fields = jnp.concatenate([stacked(gs, [2 - t], inner) for t in range(3)], axis=1)
+    back = mm(fields, b2[...].reshape(-1, wide1))
     pieces = wide1 // 128
     for u in range(inner):
         x = back[u * width2 : (u + 1) * width2]
@@ -386,18 +386,15 @@
         g1[u] = g.astype(BF16)
 
     center = g1[1 : 1 + per].reshape(per * width, wide1)
-    parts = [mm_t(center, stacked(xs, [EDGE + t - 1], per)) for t in range(3)]
+    parts = weight_product(center, xs, range(EDGE - 1, EDGE + 2), per)
     tiles = {}
     collect(d, parts, 1, d.height, d.mid, tiles, 0)
-    kept = sums_in.shape[0]
-    sums_out[:kept, :] = sums_in[...]
     for t, tile in tiles.items():
         late[t * d.mid : (t + 1) * d.mid, :] = tile.astype(BF16)
-    sums_out[kept:, :] = late[...]
     grads_out[...] = g1[pl.ds((place & (BLOCK - 1)) * planes, planes + 2)]
 
 
-def feats_kernel(d, g1, b1, out, wide):
+def feats_grad(d, g1, b1, out, wide):
     planes, width, wide1 = d.planes, d.width, d.height * d.mid
     for u in range(planes + 2):
         g = g1[u]
@@ -405,44 +402,43 @@
         wide[u, :, 0:wide1] = after.astype(BF16)
         wide[u, :, wide1 : 2 * wide1] = g
         wide[u, :, 2 * wide1 :] = before.astype(BF16)
-    grad = jnp.zeros((planes * width, d.height * d.half), F32)
-    for a in range(3):
-        grad += mm(wide[2 - a : 2 - a + planes].reshape(planes * width, 3 * wide1), b1[a])
-    grad = grad.astype(BF16)
+    fields = jnp.concatenate([stacked(wide, [2 - a], planes) for a in range(3)], axis=1)
+    grad = mm(fields, b1[...].reshape(-1, d.height * d.half)).astype(BF16)
     grad = jnp.concatenate([grad[p * width : (p + 1) * width] for p in range(planes)], axis=1)
     turn = order_matrix(d.half, planes, d.height)
     out[...] = lax.dot_general(turn, grad, (((1,), (1,)), ((), ())), preferred_element_type=F32).astype(BF16)
 
 
-def final_kernel(d, *refs):
-    swapped = lax.axis_index("chan") == 1
-    parts, (out1, out2, r) = list(refs[:-3]), refs[-3:]
-    rows = parts[0].shape[0]
-    terms = []
-    while parts:
-        pieces = [parts.pop(0)[...].astype(F32)]
-        while sum(piece.shape[0] for piece in pieces) < rows:
-            pieces.append(parts.pop(0)[...].astype(F32))
-        terms.append(pieces[0] if len(pieces) == 1 else jnp.concatenate(pieces, axis=0))
-    while len(terms) > 1:
-        terms = [terms[i] + terms[i + 1] for i in range(0, len(terms), 2)]
-    total = terms[0]
+def final_tiles(d, parts, groups):
     half, mid = d.half, d.mid
     slots = 128 // half
-    for t in range(total.shape[0] // mid):
-        flat = total[t * mid : (t + 1) * mid].T
-        for spot in range(slots):
-            early = -(-2 * 27 // slots)
-            slot = slots * t + spot if t < early else slots * (t - early) + spot + 2 * 27
-            if slot >= (2 * 27 if t < early else 3 * 27):
-                continue
+    for t in range(parts[0].shape[0] // mid):
+        terms = [p[t * mid : (t + 1) * mid, :].astype(F32) for p in parts]
+        while len(terms) > 1:
+            terms = [terms[i] + terms[i + 1] for i in range(0, len(terms), 2)]
+        tile = terms[0]
+        if groups == 1:
+            tile = pltpu.roll(tile, lax.axis_index("chan") * half, 0)
+        flat = tile.T
+        for slot in range(slots * t, min(slots * (t + 1), 27 * groups)):
             g, m, b = slot // 27, slot % 27 // 3, slot % 3
-            tap = 9 * (m // 3) + 3 * b + m % 3
-            r[g, tap * half : (tap + 1) * half, :] = flat[spot * half : (spot + 1) * half]
-    x, y = r[0], r[1]
-    out2[...] = jnp.concatenate([jnp.where(swapped, y, x), jnp.where(swapped, x, y)], axis=1)
-    x = r[2]
-    out1[...] = jnp.where(swapped, jnp.concatenate([x[:, half:], x[:, :half]], axis=1), x)
+            spot = slot % slots
+            yield g, 9 * (m // 3) + 3 * b + m % 3, flat[spot * half : (spot + 1) * half]
+
+
+def fill_kernel(d, g1, b1, *refs):
+    feats_out, out, wide, r = refs[-4:]
+    feats_grad(d, g1, b1, feats_out, wide)
+    member = lax.axis_index("chan")
+    for g, tap, piece in final_tiles(d, refs[:-4], 2):
+        r[g ^ member, tap * d.half : (tap + 1) * d.half, :] = piece
+    out[...] = jnp.concatenate([r[0], r[1]], axis=1)
+
+
+def final_kernel(d, *refs):
+    out = refs[-1]
+    for g, tap, piece in final_tiles(d, refs[:-1], 1):
+        out[tap * d.half : (tap + 1) * d.half, :] = piece
 
 
 class Sizes:
@@ -497,8 +493,7 @@
 
     side_rows = EDGE * d.width
     mid, to_a, to_b = call(
-        sort_kernel,
-        [((BLOCK * rows, 128), BF16), ((side_rows, 128), BF16), ((side_rows, 128), BF16)],
+        sort_kernel, [((BLOCK * rows, 128), BF16), ((side_rows, 128), BF16), ((side_rows, 128), BF16)]
     )(item, *[gather(k) for k in range(1, BLOCK)])
     pair_a = [(i, i ^ BLOCK) for i in range(slabs)]
     inside = range(BLOCK, slabs - BLOCK)
@@ -551,10 +546,7 @@
     from_a, from_b = trade(for_a, for_b)
     ends_shape = (6 * d.width, wide1)
     xs, part = call(
-        outer_kernel,
-        [((per + 2 * EDGE, d.width, 3 * own1), BF16), (ends_shape, F32)],
-        flops=1 << 30,
-        aliases={2: 0},
+        outer_kernel, [((per + 2 * EDGE, d.width, 3 * own1), BF16), (ends_shape, F32)], flops=1 << 30, aliases={2: 0}
     )(a, b, xs_mid, f1)
     _, slopes_out, rows_out = call(
         close_kernel,
@@ -567,10 +559,18 @@
         aliases={2: 0},
     )(a_x, b_x, xs_mid_x, f1, part)
 
-    fan = min(4, blocks)
-
-    def move(x, k):
-        return xor(x, BLOCK * k)
+    def gather_sums(x):
+        radix = 1
+        parts = [x]
+        while radix < blocks:
+            x = sum_parts(parts)
+            fan = min(4, blocks // radix)
+            parts = [None] * fan
+            for k in range(fan - 1, 0, -1):
+                parts[k] = xor(x, BLOCK * radix * k)
+            parts[0] = x
+            radix *= fan
+        return parts
 
     early_rows, late_rows = -(-2 * 27 // 8) * d.half2, -(-27 // 8) * d.mid
     zs, gs, early = call(
@@ -583,13 +583,12 @@
         [pltpu.VMEM((BLOCK, d.width, zl), F32)],
         flops=1 << 30,
     )(mid, mid_x, for_a, rows_mid, rows_out, f2)
-    early = [early] + [move(early, k) for k in range(2, fan)]
-    grads, late, sums = call(
+    early = gather_sums(early)
+    grads, late = call(
         main_kernel,
         [
             ((d.planes + 2, d.width, wide1), BF16),
             ((late_rows, 128), BF16),
-            ((early_rows + late_rows, 128), BF16),
         ],
         [
             pltpu.VMEM((3 * BLOCK - 2, width2, 3 * zl), BF16),
@@ -598,33 +597,19 @@
             pltpu.VMEM((per + 2, d.width, wide1), BF16),
         ],
         flops=1 << 32,
-    )(xs, slopes_mid, slopes_out, from_a, from_b, zs, gs, early[0], f2, b2)
-
-    parts = [(sums,)]
-    for k in range(fan - 1, 1, -1):
-        parts.append((early[k - 1], move(late, k)))
-    if fan > 1:
-        parts.append((move(sums, 1),))
-    parts = [parts[i] for i in (0, -1, -2, -3)[: len(parts)]]
-    radix = fan
-    while radix < blocks:
-        whole = [p[0] if len(p) == 1 else jnp.concatenate(p) for p in parts]
-        mine = sum_parts(whole)
-        fan = min(4, blocks // radix)
-        parts = [(mine,)] + [(xor(mine, BLOCK * radix * k),) for k in range(1, fan)]
-        radix *= fan
-    parts = sum(parts, ())
-    (grad,) = call(
-        feats_kernel,
-        [(feats_shape, BF16)],
-        [pltpu.VMEM((d.planes + 2, d.width, 3 * wide1), BF16)],
+    )(xs, slopes_mid, slopes_out, from_a, from_b, zs, gs, f2, b2)
+
+    late = gather_sums(late)
+    grad, out2 = call(
+        fill_kernel,
+        [(feats_shape, BF16), ((27 * d.half, 2 * d.half2), F32)],
+        [
+            pltpu.VMEM((d.planes + 2, d.width, 3 * wide1), BF16),
+            pltpu.VMEM((2, 27 * d.half, d.mid), F32),
+        ],
         flops=1 << 30,
-    )(grads, b1)
-    out1, out2 = call(
-        final_kernel,
-        [((27 * d.half, d.mid), F32), ((27 * d.half, 2 * d.half2), F32)],
-        [pltpu.VMEM((3, 27 * d.half, d.mid), F32)],
-    )(*parts)
+    )(grads, b1, *early)
+    (out1,) = call(final_kernel, [((27 * d.half, d.mid), F32)])(*late)
     return (
         grad.reshape(feats.shape),
         out1.reshape(27, d.half, d.mid).transpose(2, 1, 0),
@@ -633,6 +618,8 @@
 
 
 def sum_parts(parts):
+    if len(parts) == 1:
+        return parts[0]
     terms = [p.astype(F32) for p in parts]
     while len(terms) > 1:
         terms = [terms[i] + terms[i + 1] for i in range(0, len(terms), 2)]

time: 44 us -> 44.5 us (1.011)
  Pallas kernels: 12.2 us -> 11.2 us
  starting transfers between devices: 20.5 us -> 21.5 us
  waiting for transfers between devices: 7.5 us -> 8.11 us
    pallas_call x10, Pallas kernels: 12.2 us -> 11.2 us  [run(): pl.pallas_call(functools.partial(kernel, d), out_shape=[jax.ShapeDtypeStr...]
    ppermute x8 -> x9, starting transfers between devices: 12.5 us -> 13.5 us  [xor(): return lax.ppermute(x, 'depth', [(i, i ^ k) for i in range(slabs)])]
    ppermute x8 -> x9, waiting for transfers between devices: 7.48 us -> 8.1 us  [xor(): return lax.ppermute(x, 'depth', [(i, i ^ k) for i in range(slabs)])]
  transfers between devices with their start and end apart: 15 -> 16, of which waited for: 6 -> 5; matrix products, arithmetic and copies ran while one was open for 0% -> 0% of each run, Pallas kernels for 25% -> 23%
where the time goes in v5:
time: 44.5 us; the launch traced here: 44.3 us
  starting transfers between devices  21.5 us (48%)
  Pallas kernels  11.2 us (25%)
  waiting for transfers between devices  8.11 us (18%)
  local copies, waits for them, and re-layouts  1.87 us (4%)
  other arithmetic  0.87 us (2%)
  between operations  0.75 us (2%)
    ppermute x9, starting transfers between devices, xor(): return lax.ppermute(x, 'depth', [(i, i ^ k) for i in range(slabs)])  13.5 us
    pallas_call x10, Pallas kernels, run(): pl.pallas_call(functools.partial(kernel, d), out_shape=[jax.ShapeDtypeStr...  11.2 us
    ppermute x9, waiting for transfers between devices, xor(): return lax.ppermute(x, 'depth', [(i, i ^ k) for i in range(slabs)])  8.1 us
    ppermute x2, starting transfers between devices, trade(): a = lax.ppermute(x_a, 'depth', pair_a)  6.1 us
    unnamed x4, local copies, waits for them, and re-layouts  1.87 us
    ppermute x2, starting transfers between devices, trade(): b = lax.ppermute(x_b, 'depth', pair_b)  1.31 us
  transfers between devices with their start and end apart: 16, of which 5 were waited for; matrix products, arithmetic and copies ran while one was open for 0% of the time, Pallas kernels for 23%

profile of v5, /device:TPU:0, one launch (start us, length us, event | category | flops | bytes accessed | tf_op | source)
XLA Modules:
  0.0 44.3 jit_solution(1444480608389452361)
XLA Ops:
  0.6 0.9 %fusion.1.raw = bf16[384,128]{1,0:T(8,128)(2,1)S(1)} fusion(bf16[128,64]{1,0:T(8,128)(2,1)} %bitcast.19, bf16[256,128]{1,0:T(8,128)(2,1)} %bitcast.18), kind=kLoop, calls=%fused_computation.2 | loop fusion | flops 294912 | bytes 180224 | tf_op jit(solution)/shard_map/concatenate | solution.py:482
  1.5 0.2 shard_map.67.i0
  1.7 3.0 %collective-permute-start = (bf16[320,128]{1,0:T(8,128)(2,1)S(1)}, bf16[320,128]{1,0:T(8,128)(2,1)S(1)}, u32[]{:S(2)}, u32[]{:S(2)}) collective-permute-start(bf16[320,128]{1,0:T(8,128)(2,1)S(1)} %shard_map.67.i0), channel_id=1, source_target_pairs={{0,2},{2,0},{4,6},{6,4},{8,10},{10,8},{12,14},{14,12},{16,18},{18,... | collective-permute-start | bytes 245768 | tf_op jit(solution)/shard_map/ppermute | solution.py:486
  4.8 1.5 %collective-permute-start.1 = (bf16[320,128]{1,0:T(8,128)(2,1)S(1)}, bf16[320,128]{1,0:T(8,128)(2,1)S(1)}, u32[]{:S(2)}, u32[]{:S(2)}) collective-permute-start(bf16[320,128]{1,0:T(8,128)(2,1)S(1)} %shard_map.67.i0), channel_id=1, source_target_pairs={{0,4},{2,6},{4,0},{6,2},{8,12},{10,14},{12,8},{14,10},{16,20},{18,... | collective-permute-start | bytes 245768 | tf_op jit(solution)/shard_map/ppermute | solution.py:486
  6.3 1.2 %collective-permute-done.i1 = bf16[320,128]{1,0:T(8,128)(2,1)S(1)} collective-permute-done((bf16[320,128]{1,0:T(8,128)(2,1)S(1)}, bf16[320,128]{1,0:T(8,128)(2,1)S(1)}, u32[]{:S(2)}, u32[]{:S(2)}) %collective-permute-start) | collective-permute-done | bytes 81952 | tf_op jit(solution)/shard_map/ppermute | solution.py:486
  7.5 2.6 %collective-permute-done.1.i2 = bf16[320,128]{1,0:T(8,128)(2,1)S(1)} collective-permute-done((bf16[320,128]{1,0:T(8,128)(2,1)S(1)}, bf16[320,128]{1,0:T(8,128)(2,1)S(1)}, u32[]{:S(2)}, u32[]{:S(2)}) %collective-permute-start.1) | collective-permute-done | bytes 81952 | tf_op jit(solution)/shard_map/ppermute | solution.py:486
  10.1 1.5 %collective-permute-done.2.i3 = bf16[320,128]{1,0:T(8,128)(2,1)S(1)} collective-permute-done((bf16[320,128]{1,0:T(8,128)(2,1)S(1)}, bf16[320,128]{1,0:T(8,128)(2,1)S(1)}, u32[]{:S(2)}, u32[]{:S(2)}) %collective-permute-start.2) | collective-permute-done | bytes 81952 | tf_op jit(solution)/shard_map/ppermute | solution.py:486
  11.7 0.1 collective-permute-start.5
  11.7 1.6 %collective-permute-start.3 = (bf16[384,128]{1,0:T(8,128)(2,1)S(1)}, bf16[384,128]{1,0:T(8,128)(2,1)S(1)}, u32[]{:S(2)}, u32[]{:S(2)}) collective-permute-start(bf16[384,128]{1,0:T(8,128)(2,1)S(1)} %get-tuple-element.27), channel_id=1, source_target_pairs={{0,8},{2,10},{4,12},{6,14},{8,0},{10,2},{12,4},{14,6},{16,24},{18,... | collective-permute-start | bytes 294920 | tf_op jit(solution)/shard_map/ppermute | solution.py:503
  13.4 0.7 %collective-permute-start.4 = (bf16[384,128]{1,0:T(8,128)(2,1)S(1)}, bf16[384,128]{1,0:T(8,128)(2,1)S(1)}, u32[]{:S(2)}, u32[]{:S(2)}) collective-permute-start(bf16[384,128]{1,0:T(8,128)(2,1)S(1)} %get-tuple-element.28), channel_id=1, source_target_pairs={{0,0},{2,2},{4,4},{6,6},{8,16},{10,18},{12,20},{14,22},{16,8},{18,... | collective-permute-start | bytes 294920 | tf_op jit(solution)/shard_map/ppermute | solution.py:504
  14.1 0.9 %copy-done = bf16[32,32,27]{1,0,2:T(8,128)(2,1)S(1)} copy-done((bf16[32,32,27]{1,0,2:T(8,128)(2,1)S(1)}, bf16[32,32,27]{1,0,2:T(8,128)(2,1)}, u32[]{:S(2)}) %copy-start) | copy-done | bytes 55320
  15.0 0.9 %copy-done.1 = bf16[64,32,27]{0,1,2:T(8,128)(2,1)S(1)} copy-done((bf16[64,32,27]{0,1,2:T(8,128)(2,1)S(1)}, bf16[64,32,27]{0,1,2:T(8,128)(2,1)}, u32[]{:S(2)}) %copy-start.1) | copy-done | bytes 110616
  15.9 1.7 %shard_map.69 = (bf16[3,768,256]{2,1,0:T(8,128)(2,1)S(1)}, bf16[3,768,128]{2,1,0:T(8,128)(2,1)S(1)}, bf16[3,384,256]{2,1,0:T(8,128)(2,1)S(1)}, bf16[3,768,256]{2,1,0:T(8,128)(2,1)S(1)}) custom-call(bf16[864,32]{1,0:T(8,128)(2,1)S(1)} %bitcast.15, bf16[864,64]{1,0:T(8,128)(2,1)S(1)} %bitcast.16), custom_call_target="tpu_custom_call" | custom-call | flops 1073741824 | bytes 1048576 | tf_op jit(solution)/shard_map/pallas_call | solution.py:466
  17.6 0.2 collective-permute-start.6
  17.8 0.3 collective-permute-start.7
  18.2 1.4 %shard_map.70 = (bf16[14,128,384]{2,1,0:T(8,128)(2,1)S(1)}, bf16[14,128,384]{2,1,0:T(8,128)(2,1)S(1)}, f32[6,128,256]{2,1,0:T(8,128)S(1)}, f32[6,128,128]{2,1,0:...) custom-call(bf16[1280,128]{1,0:T(8,128)(2,1)S(1)} %get-tuple-element.29.mi, ...), custom_call_target="tpu_custom_call" | custom-call | flops 1073741824 | bytes 1048576 | tf_op jit(solution)/shard_map/pallas_call | solution.py:466
  19.6 4.5 %collective-permute-start.8 = (bf16[384,128]{1,0:T(8,128)(2,1)S(1)}, bf16[384,128]{1,0:T(8,128)(2,1)S(1)}, u32[]{:S(2)}, u32[]{:S(2)}) collective-permute-start(bf16[384,128]{1,0:T(8,128)(2,1)S(1)} %get-tuple-element.37.pooled), channel_id=1, source_target_pairs={{0,8},{2,10},{4,12},{6,14},{8,0},{10,2},{12,4},{14,6},{16,24},{18,... | collective-permute-start | bytes 294920 | tf_op jit(solution)/shard_map/ppermute | solution.py:503
  24.1 0.7 %collective-permute-start.9 = (bf16[384,128]{1,0:T(8,128)(2,1)S(1)}, bf16[384,128]{1,0:T(8,128)(2,1)S(1)}, u32[]{:S(2)}, u32[]{:S(2)}) collective-permute-start(bf16[384,128]{1,0:T(8,128)(2,1)S(1)} %get-tuple-element.38), channel_id=1, source_target_pairs={{0,0},{2,2},{4,4},{6,6},{8,16},{10,18},{12,20},{14,22},{16,8},{18,... | collective-permute-start | bytes 294920 | tf_op jit(solution)/shard_map/ppermute | solution.py:504
  24.7 0.7 %shard_map.71 = (bf16[14,128,384]{2,1,0:T(8,128)(2,1)S(1)}, f32[768,256]{1,0:T(8,128)S(1)}) custom-call(bf16[384,128]{1,0:T(8,128)(2,1)S(1)} %collective-permute-done.3.a, bf16[384,128]{1,0:T(8,128)(2,1)S(1)} %collective-permute-done.4.b, bf16[14,128,384]{2,1,0:T(8,128)(2,1)S(1)} %get-tuple-element.31.xs_in, ...), custom_call_target="tpu_custom_call", output_to_operand_aliasing={{0}: (2, {})} | custom-call | flops 1073741824 | bytes 1048576 | tf_op jit(solution)/shard_map/pallas_call | solution.py:466
  25.5 1.0 %shard_map.72 = (bf16[14,128,384]{2,1,0:T(8,128)(2,1)S(1)}, f32[6,128,256]{2,1,0:T(8,128)S(1)}, f32[6,128,128]{2,1,0:T(8,128)S(1)}) custom-call(bf16[384,128]{1,0:T(8,128)(2,1)S(1)} %collective-permute-done.6.a, bf16[384,128]{1,0:T(8,128)(2,1)S(1)} %collective-permute-done.7.b, ...), custom_call_target="tpu_custom_call", output_to_operand_aliasing={{0}: (2, {})} | custom-call | flops 1073741824 | bytes 1048576 | tf_op jit(solution)/shard_map/pallas_call | solution.py:466
  26.5 1.2 %shard_map.73 = (bf16[6,64,384]{2,1,0:T(8,128)(2,1)S(1)}, bf16[4,64,768]{2,1,0:T(8,128)(2,1)S(1)}, bf16[224,128]{1,0:T(8,128)(2,1)S(1)}) custom-call(bf16[1280,128]{1,0:T(8,128)(2,1)S(1)} %get-tuple-element.29.mi, bf16[1280,128]{1,0:T(8,128)(2,1)S(1)} %collective-permute-done.5.mi_x, bf16[384,128]{1,0:T(8,128)(2,1)S(1)} %get-tuple-element.37.pooled, ...), custom_call_target="tpu_custom_call" | custom-call | flops 1073741824 | bytes 1048576 | tf_op jit(solution)/shard_map/pallas_call | solution.py:466
  27.7 2.0 %collective-permute-start.10 = (bf16[224,128]{1,0:T(8,128)(2,1)S(1)}, bf16[224,128]{1,0:T(8,128)(2,1)S(1)}, u32[]{:S(2)}, u32[]{:S(2)}) collective-permute-start(bf16[224,128]{1,0:T(8,128)(2,1)S(1)} %get-tuple-element.47.refs_0_), channel_id=1, source_target_pairs={{0,8},{2,10},{4,12},{6,14},{8,0},{10,2},{12,4},{14,6},{16,24},{18,... | collective-permute-start | bytes 172040 | tf_op jit(solution)/shard_map/ppermute | solution.py:486
  29.7 0.8 %collective-permute-start.11 = (bf16[224,128]{1,0:T(8,128)(2,1)S(1)}, bf16[224,128]{1,0:T(8,128)(2,1)S(1)}, u32[]{:S(2)}, u32[]{:S(2)}) collective-permute-start(bf16[224,128]{1,0:T(8,128)(2,1)S(1)} %get-tuple-element.47.refs_0_), channel_id=1, source_target_pairs={{0,16},{2,18},{4,20},{6,22},{8,24},{10,26},{12,28},{14,30},{16,0},... | collective-permute-start | bytes 172040 | tf_op jit(solution)/shard_map/ppermute | solution.py:486
  30.6 1.6 %collective-permute-start.12 = (bf16[224,128]{1,0:T(8,128)(2,1)S(1)}, bf16[224,128]{1,0:T(8,128)(2,1)S(1)}, u32[]{:S(2)}, u32[]{:S(2)}) collective-permute-start(bf16[224,128]{1,0:T(8,128)(2,1)S(1)} %get-tuple-element.47.refs_0_), channel_id=1, source_target_pairs={{0,24},{2,26},{4,28},{6,30},{8,16},{10,18},{12,20},{14,22},{16,8},... | collective-permute-start | bytes 172040 | tf_op jit(solution)/shard_map/ppermute | solution.py:486
  32.2 2.7 %shard_map.74 = (bf16[4,128,256]{2,1,0:T(8,128)(2,1)S(1)}, bf16[128,128]{1,0:T(8,128)(2,1)S(1)}) custom-call(bf16[14,128,384]{2,1,0:T(8,128)(2,1)S(1)} %get-tuple-element.32.xs, f32[6,128,256]{2,1,0:T(8,128)S(1)} %get-tuple-element.33.slopes_mid, f32[6,128,256]{2,1,0:T(8,128)S(1)} %get-tuple-element.36.slopes_out, ...), custom_call_target="tpu_custom_call" | custom-call | flops 4294967296 | bytes 1048576 | tf_op jit(solution)/shard_map/pallas_call | solution.py:466
  34.9 1.1 %collective-permute-start.13 = (bf16[128,128]{1,0:T(8,128)(2,1)S(1)}, bf16[128,128]{1,0:T(8,128)(2,1)S(1)}, u32[]{:S(2)}, u32[]{:S(2)}) collective-permute-start(bf16[128,128]{1,0:T(8,128)(2,1)S(1)} %get-tuple-element.49.refs_0_), channel_id=1, source_target_pairs={{0,8},{2,10},{4,12},{6,14},{8,0},{10,2},{12,4},{14,6},{16,24},{18,... | collective-permute-start | bytes 98312 | tf_op jit(solution)/shard_map/ppermute | solution.py:486
  36.0 1.7 %collective-permute-start.14 = (bf16[128,128]{1,0:T(8,128)(2,1)S(1)}, bf16[128,128]{1,0:T(8,128)(2,1)S(1)}, u32[]{:S(2)}, u32[]{:S(2)}) collective-permute-start(bf16[128,128]{1,0:T(8,128)(2,1)S(1)} %get-tuple-element.49.refs_0_), channel_id=1, source_target_pairs={{0,16},{2,18},{4,20},{6,22},{8,24},{10,26},{12,28},{14,30},{16,0},... | collective-permute-start | bytes 98312 | tf_op jit(solution)/shard_map/ppermute | solution.py:486
  37.7 1.6 %collective-permute-start.15 = (bf16[128,128]{1,0:T(8,128)(2,1)S(1)}, bf16[128,128]{1,0:T(8,128)(2,1)S(1)}, u32[]{:S(2)}, u32[]{:S(2)}) collective-permute-start(bf16[128,128]{1,0:T(8,128)(2,1)S(1)} %get-tuple-element.49.refs_0_), channel_id=1, source_target_pairs={{0,24},{2,26},{4,28},{6,30},{8,16},{10,18},{12,20},{14,22},{16,8},... | collective-permute-start | bytes 98312 | tf_op jit(solution)/shard_map/ppermute | solution.py:486
  39.4 1.3 %shard_map.75 = (bf16[256,128]{1,0:T(8,128)(2,1)}, f32[432,64]{1,0:T(8,128)}) custom-call(bf16[4,128,256]{2,1,0:T(8,128)(2,1)S(1)} %get-tuple-element.45.g1, bf16[3,768,128]{2,1,0:T(8,128)(2,1)S(1)} %get-tuple-element.46.b1, bf16[224,128]{1,0:T(8,128)(2,1)S(1)} %get-tuple-element.47.refs_0_, bf16[224,128]{1,0:T(8,128)(2,1)S(1)} %collective-permute-done.10.refs_1_, ...), custom_call_target="tpu_custom_call" | custom-call | flops 1073741824 | bytes 1048576 | tf_op jit(solution)/shard_map/pallas_call | solution.py:466
  40.7 0.1 collective-permute-done.14.refs_2_
  40.8 2.6 %collective-permute-done.15.refs_3_ = bf16[128,128]{1,0:T(8,128)(2,1)S(1)} collective-permute-done((bf16[128,128]{1,0:T(8,128)(2,1)S(1)}, bf16[128,128]{1,0:T(8,128)(2,1)S(1)}, u32[]{:S(2)}, u32[]{:S(2)}) %collective-permute-start.15) | collective-permute-done | bytes 32800 | tf_op jit(solution)/shard_map/ppermute | solution.py:486
  43.5 0.8 %shard_map.76 = f32[432,32]{1,0:T(8,128)} custom-call(bf16[128,128]{1,0:T(8,128)(2,1)S(1)} %get-tuple-element.49.refs_0_, bf16[128,128]{1,0:T(8,128)(2,1)S(1)} %collective-permute-done.13.refs_1_, bf16[128,128]{1,0:T(8,128)(2,1)S(1)} %collective-permute-done.14.refs_2_, bf16[128,128]{1,0:T(8,128)(2,1)S(1)} %collective-permute-done.15.refs_3_), custom_call_target="tpu_custom_call" | custom-call | bytes 1048576 | tf_op jit(solution)/shard_map/pallas_call | solution.py:466
  (15 shorter events, 0.1 us)
Async XLA Ops:
  1.7 5.7 %collective-permute-start = (bf16[320,128]{1,0:T(8,128)(2,1)S(1)}, bf16[320,128]{1,0:T(8,128)(2,1)S(1)}, u32[]{:S(2)}, u32[]{:S(2)}) collective-permute-start(bf16[320,128]{1,0:T(8,128)(2,1)S(1)} %shard_map.67.i0), channel_id=1, source_target_pairs={{0,2},{2,0},{4,6},{6,4},{8,10},{10,8},{12,14},{14,12},{16,18},{18,... | collective-permute-start | bytes 245768 | tf_op jit(solution)/shard_map/ppermute | solution.py:486
  4.8 5.3 %collective-permute-start.1 = (bf16[320,128]{1,0:T(8,128)(2,1)S(1)}, bf16[320,128]{1,0:T(8,128)(2,1)S(1)}, u32[]{:S(2)}, u32[]{:S(2)}) collective-permute-start(bf16[320,128]{1,0:T(8,128)(2,1)S(1)} %shard_map.67.i0), channel_id=1, source_target_pairs={{0,4},{2,6},{4,0},{6,2},{8,12},{10,14},{12,8},{14,10},{16,20},{18,... | collective-permute-start | bytes 245768 | tf_op jit(solution)/shard_map/ppermute | solution.py:486
  6.3 5.3 %collective-permute-start.2 = (bf16[320,128]{1,0:T(8,128)(2,1)S(1)}, bf16[320,128]{1,0:T(8,128)(2,1)S(1)}, u32[]{:S(2)}, u32[]{:S(2)}) collective-permute-start(bf16[320,128]{1,0:T(8,128)(2,1)S(1)} %shard_map.67.i0), channel_id=1, source_target_pairs={{0,6},{2,4},{4,2},{6,0},{8,14},{10,12},{12,10},{14,8},{16,22},{18,... | collective-permute-start | bytes 245768 | tf_op jit(solution)/shard_map/ppermute | solution.py:486
  11.7 6.5 %collective-permute-start.5 = (bf16[1280,128]{1,0:T(8,128)(2,1)S(1)}, bf16[1280,128]{1,0:T(8,128)(2,1)S(1)}, u32[]{:S(2)}, u32[]{:S(2)}) collective-permute-start(bf16[1280,128]{1,0:T(8,128)(2,1)S(1)} %get-tuple-element.29.mi), channel_id=1, source_target_pairs={{0,1},{1,0},{2,3},{3,2},{4,5},{5,4},{6,7},{7,6},{8,9},{9,8},{10,11... | collective-permute-start | bytes 983048 | tf_op jit(solution)/shard_map/ppermute | solution.py:492
  11.7 5.8 %collective-permute-start.3 = (bf16[384,128]{1,0:T(8,128)(2,1)S(1)}, bf16[384,128]{1,0:T(8,128)(2,1)S(1)}, u32[]{:S(2)}, u32[]{:S(2)}) collective-permute-start(bf16[384,128]{1,0:T(8,128)(2,1)S(1)} %get-tuple-element.27), channel_id=1, source_target_pairs={{0,8},{2,10},{4,12},{6,14},{8,0},{10,2},{12,4},{14,6},{16,24},{18,... | collective-permute-start | bytes 294920 | tf_op jit(solution)/shard_map/ppermute | solution.py:503
  13.4 4.4 %collective-permute-start.4 = (bf16[384,128]{1,0:T(8,128)(2,1)S(1)}, bf16[384,128]{1,0:T(8,128)(2,1)S(1)}, u32[]{:S(2)}, u32[]{:S(2)}) collective-permute-start(bf16[384,128]{1,0:T(8,128)(2,1)S(1)} %get-tuple-element.28), channel_id=1, source_target_pairs={{0,0},{2,2},{4,4},{6,6},{8,16},{10,18},{12,20},{14,22},{16,8},{18,... | collective-permute-start | bytes 294920 | tf_op jit(solution)/shard_map/ppermute | solution.py:504
  14.1 0.9 %copy-start = (bf16[32,32,27]{1,0,2:T(8,128)(2,1)S(1)}, bf16[32,32,27]{1,0,2:T(8,128)(2,1)}, u32[]{:S(2)}) copy-start(bf16[32,32,27]{1,0,2:T(8,128)(2,1)} %param.5) | copy-start | bytes 165892
  15.0 0.9 %copy-start.1 = (bf16[64,32,27]{0,1,2:T(8,128)(2,1)S(1)}, bf16[64,32,27]{0,1,2:T(8,128)(2,1)}, u32[]{:S(2)}) copy-start(bf16[64,32,27]{0,1,2:T(8,128)(2,1)} %param.6) | copy-start | bytes 331780
  17.6 7.8 %collective-permute-start.6 = (bf16[384,128]{1,0:T(8,128)(2,1)S(1)}, bf16[384,128]{1,0:T(8,128)(2,1)S(1)}, u32[]{:S(2)}, u32[]{:S(2)}) collective-permute-start(bf16[384,128]{1,0:T(8,128)(2,1)S(1)} %collective-permute-done.3.a), channel_id=1, source_target_pairs={{0,1},{1,0},{2,3},{3,2},{4,5},{5,4},{6,7},{7,6},{8,9},{9,8},{10,11... | collective-permute-start | bytes 294920 | tf_op jit(solution)/shard_map/ppermute | solution.py:492
  17.8 7.6 %collective-permute-start.7 = (bf16[384,128]{1,0:T(8,128)(2,1)S(1)}, bf16[384,128]{1,0:T(8,128)(2,1)S(1)}, u32[]{:S(2)}, u32[]{:S(2)}) collective-permute-start(bf16[384,128]{1,0:T(8,128)(2,1)S(1)} %collective-permute-done.4.b), channel_id=1, source_target_pairs={{0,1},{1,0},{2,3},{3,2},{4,5},{5,4},{6,7},{7,6},{8,9},{9,8},{10,11... | collective-permute-start | bytes 294920 | tf_op jit(solution)/shard_map/ppermute | solution.py:492
  19.6 12.6 %collective-permute-start.8 = (bf16[384,128]{1,0:T(8,128)(2,1)S(1)}, bf16[384,128]{1,0:T(8,128)(2,1)S(1)}, u32[]{:S(2)}, u32[]{:S(2)}) collective-permute-start(bf16[384,128]{1,0:T(8,128)(2,1)S(1)} %get-tuple-element.37.pooled), channel_id=1, source_target_pairs={{0,8},{2,10},{4,12},{6,14},{8,0},{10,2},{12,4},{14,6},{16,24},{18,... | collective-permute-start | bytes 294920 | tf_op jit(solution)/shard_map/ppermute | solution.py:503
  24.1 8.1 %collective-permute-start.9 = (bf16[384,128]{1,0:T(8,128)(2,1)S(1)}, bf16[384,128]{1,0:T(8,128)(2,1)S(1)}, u32[]{:S(2)}, u32[]{:S(2)}) collective-permute-start(bf16[384,128]{1,0:T(8,128)(2,1)S(1)} %get-tuple-element.38), channel_id=1, source_target_pairs={{0,0},{2,2},{4,4},{6,6},{8,16},{10,18},{12,20},{14,22},{16,8},{18,... | collective-permute-start | bytes 294920 | tf_op jit(solution)/shard_map/ppermute | solution.py:504
  27.7 10.0 %collective-permute-start.10 = (bf16[224,128]{1,0:T(8,128)(2,1)S(1)}, bf16[224,128]{1,0:T(8,128)(2,1)S(1)}, u32[]{:S(2)}, u32[]{:S(2)}) collective-permute-start(bf16[224,128]{1,0:T(8,128)(2,1)S(1)} %get-tuple-element.47.refs_0_), channel_id=1, source_target_pairs={{0,8},{2,10},{4,12},{6,14},{8,0},{10,2},{12,4},{14,6},{16,24},{18,... | collective-permute-start | bytes 172040 | tf_op jit(solution)/shard_map/ppermute | solution.py:486
  29.7 9.6 %collective-permute-start.11 = (bf16[224,128]{1,0:T(8,128)(2,1)S(1)}, bf16[224,128]{1,0:T(8,128)(2,1)S(1)}, u32[]{:S(2)}, u32[]{:S(2)}) collective-permute-start(bf16[224,128]{1,0:T(8,128)(2,1)S(1)} %get-tuple-element.47.refs_0_), channel_id=1, source_target_pairs={{0,16},{2,18},{4,20},{6,22},{8,24},{10,26},{12,28},{14,30},{16,0},... | collective-permute-start | bytes 172040 | tf_op jit(solution)/shard_map/ppermute | solution.py:486
  30.6 8.8 %collective-permute-start.12 = (bf16[224,128]{1,0:T(8,128)(2,1)S(1)}, bf16[224,128]{1,0:T(8,128)(2,1)S(1)}, u32[]{:S(2)}, u32[]{:S(2)}) collective-permute-start(bf16[224,128]{1,0:T(8,128)(2,1)S(1)} %get-tuple-element.47.refs_0_), channel_id=1, source_target_pairs={{0,24},{2,26},{4,28},{6,30},{8,16},{10,18},{12,20},{14,22},{16,8},... | collective-permute-start | bytes 172040 | tf_op jit(solution)/shard_map/ppermute | solution.py:486
  34.9 5.8 %collective-permute-start.13 = (bf16[128,128]{1,0:T(8,128)(2,1)S(1)}, bf16[128,128]{1,0:T(8,128)(2,1)S(1)}, u32[]{:S(2)}, u32[]{:S(2)}) collective-permute-start(bf16[128,128]{1,0:T(8,128)(2,1)S(1)} %get-tuple-element.49.refs_0_), channel_id=1, source_target_pairs={{0,8},{2,10},{4,12},{6,14},{8,0},{10,2},{12,4},{14,6},{16,24},{18,... | collective-permute-start | bytes 98312 | tf_op jit(solution)/shard_map/ppermute | solution.py:486
  36.0 4.8 %collective-permute-start.14 = (bf16[128,128]{1,0:T(8,128)(2,1)S(1)}, bf16[128,128]{1,0:T(8,128)(2,1)S(1)}, u32[]{:S(2)}, u32[]{:S(2)}) collective-permute-start(bf16[128,128]{1,0:T(8,128)(2,1)S(1)} %get-tuple-element.49.refs_0_), channel_id=1, source_target_pairs={{0,16},{2,18},{4,20},{6,22},{8,24},{10,26},{12,28},{14,30},{16,0},... | collective-permute-start | bytes 98312 | tf_op jit(solution)/shard_map/ppermute | solution.py:486
  37.7 5.7 %collective-permute-start.15 = (bf16[128,128]{1,0:T(8,128)(2,1)S(1)}, bf16[128,128]{1,0:T(8,128)(2,1)S(1)}, u32[]{:S(2)}, u32[]{:S(2)}) collective-permute-start(bf16[128,128]{1,0:T(8,128)(2,1)S(1)} %get-tuple-element.49.refs_0_), channel_id=1, source_target_pairs={{0,24},{2,26},{4,28},{6,30},{8,16},{10,18},{12,20},{14,22},{16,8},... | collective-permute-start | bytes 98312 | tf_op jit(solution)/shard_map/ppermute | solution.py:486

commit v6 on v5

--- a/solution.py
+++ b/solution.py
@@ -106,10 +106,7 @@
     out[a, at : at + size, :] = strip
 
 
-def weight_kernel(d, w1, w2, f1, b1, f2, b2, w1_in, w2_in, t1, t2, t3, t4, sems):
-    copies = [pltpu.make_async_copy(w1, w1_in, sems.at[0]), pltpu.make_async_copy(w2, w2_in, sems.at[1])]
-    for copy in copies:
-        copy.start()
+def weight_kernel(d, both, f1, b1, f2, b2, t1, t2, t3, t4):
     member = lax.axis_index("chan")
     mid, half, half2 = d.mid, d.half, d.half2
     h1, h2 = d.height, d.height2
@@ -118,17 +115,16 @@
     wide2 = h2 * 2 * half2
     k, n = iotas(mid, wide1)
     own_first = (k ^ (member * half)) == (n & (mid - 1))
-    for copy in copies:
-        copy.wait()
+    w1_in, w2_in = both[: 27 * mid, :mid], both[27 * mid :, :]
     for t in range(27):
         at = slice(t * mid, (t + 1) * mid)
-        t1[at, :] = mm_t(w1_in[at, :], one_hot(own_first)).astype(BF16)
-        t4[t * 2 * half2 : (t + 1) * 2 * half2, :] = mm_t(w2_in[at, :], one_hot(own_first, 0.125)).astype(BF16)
+        t1[at, :] = mm_t(w1_in[at], one_hot(own_first)).astype(BF16)
+        t4[t * 2 * half2 : (t + 1) * 2 * half2, :] = mm_t(w2_in[at], one_hot(own_first, 0.125)).astype(BF16)
     k, n = iotas(mid, own1)
-    t2[...] = mm(w1_in[...], one_hot((k ^ (member * half)) == (n & (half - 1)))).astype(BF16)
+    t2[...] = mm(w1_in, one_hot((k ^ (member * half)) == (n & (half - 1)))).astype(BF16)
     k, n = iotas(2 * half2, wide2)
     g2, _, o2 = digits(n, 2, h2, half2)
-    t3[...] = mm(w2_in[...], one_hot((k ^ (member * half2)) == g2 * half2 + o2)).astype(BF16)
+    t3[...] = mm(w2_in, one_hot((k ^ (member * half2)) == g2 * half2 + o2)).astype(BF16)
 
     def rows_of(ref, a, c, size, total, group):
         at = [(9 * a + 3 * b + c) * total + (group ^ member) * size for b in range(3)]
@@ -509,6 +505,7 @@
 
     w1 = jnp.transpose(weight_one, (2, 0, 1)).reshape(27 * d.mid, d.mid)
     w2 = jnp.transpose(weight_two, (2, 1, 0)).reshape(27 * d.mid, 2 * d.half2)
+    w1 = jnp.pad(w1, ((0, 0), (0, w2.shape[1] - w1.shape[1])))
     f1, b1, f2, b2 = call(
         weight_kernel,
         [
@@ -518,18 +515,13 @@
             ((3, 3 * wide2, wide1), BF16),
         ],
         [
-            pltpu.VMEM(w1.shape, BF16),
-            pltpu.VMEM(w2.shape, BF16),
             pltpu.VMEM((27 * d.mid, wide1), BF16),
             pltpu.VMEM((27 * d.mid, own1), BF16),
             pltpu.VMEM((27 * d.mid, wide2), BF16),
             pltpu.VMEM((27 * 2 * d.half2, wide1), BF16),
-            pltpu.SemaphoreType.DMA((2,)),
         ],
         flops=1 << 30,
-        ins=pltpu.HBM,
-        mib=24,
-    )(w1, w2)
+    )(jnp.concatenate([w1, w2]))
     xs_mid, xs_mid_x, slopes_mid, rows_mid, for_a, for_b = call(
         middle_kernel,
         [

time: 44.5 us -> 45.1 us (1.013)
  local copies, waits for them, and re-layouts: 1.87 us -> 0 us
  waiting for transfers between devices: 8.11 us -> 9.35 us
  other arithmetic: 0.87 us -> 2.01 us
  starting transfers between devices: 21.5 us -> 22.2 us
  Pallas kernels: 11.2 us -> 10.6 us
    ppermute x2, waiting for transfers between devices: 0.01 us -> 1.88 us  [trade(): a = lax.ppermute(x_a, 'depth', pair_a)]
    unnamed x4 -> x0, local copies, waits for them, and re-layouts: 1.87 us -> none
    concatenate x0 -> x1, other arithmetic: none -> 1.13 us  [shards(): jnp.concatenate([w1, w2])]
    ppermute x9, starting transfers between devices: 13.5 us -> 14.5 us  [xor(): return lax.ppermute(x, 'depth', [(i, i ^ k) for i in range(slabs)])]
    ppermute x9, waiting for transfers between devices: 8.1 us -> 7.45 us  [xor(): return lax.ppermute(x, 'depth', [(i, i ^ k) for i in range(slabs)])]
    pallas_call x10, Pallas kernels: 11.2 us -> 10.6 us  [run(): pl.pallas_call(functools.partial(kernel, d), out_shape=[jax.ShapeDtypeStr...]
  transfers between devices with their start and end apart: 16 -> 16, of which waited for: 5 -> 6; matrix products, arithmetic and copies ran while one was open for 0% -> 3% of each run, Pallas kernels for 23% -> 21%
where the time goes in v6:
time: 45.1 us; the launch traced here: 44.8 us
  starting transfers between devices  22.2 us (49%)
  Pallas kernels  10.6 us (24%)
  waiting for transfers between devices  9.35 us (21%)
  other arithmetic  2.01 us (4%)
  between operations  0.74 us (2%)
    ppermute x9, starting transfers between devices, xor(): return lax.ppermute(x, 'depth', [(i, i ^ k) for i in range(slabs)])  14.5 us
    pallas_call x10, Pallas kernels, run(): pl.pallas_call(functools.partial(kernel, d), out_shape=[jax.ShapeDtypeStr...  10.6 us
    ppermute x9, waiting for transfers between devices, xor(): return lax.ppermute(x, 'depth', [(i, i ^ k) for i in range(slabs)])  7.45 us
    ppermute x2, starting transfers between devices, trade(): a = lax.ppermute(x_a, 'depth', pair_a)  5.79 us
    ppermute x2, waiting for transfers between devices, trade(): a = lax.ppermute(x_a, 'depth', pair_a)  1.88 us
    ppermute x2, starting transfers between devices, trade(): b = lax.ppermute(x_b, 'depth', pair_b)  1.31 us
    concatenate x1, other arithmetic, shards(): jnp.concatenate([w1, w2])  1.13 us
  transfers between devices with their start and end apart: 16, of which 6 were waited for; matrix products, arithmetic and copies ran while one was open for 3% of the time, Pallas kernels for 21%

profile of v6, /device:TPU:0, one launch (start us, length us, event | category | flops | bytes accessed | tf_op | source)
XLA Modules:
  0.0 44.8 jit_solution(7420806585547804520)
XLA Ops:
  0.6 0.9 %fusion.3.raw = bf16[384,128]{1,0:T(8,128)(2,1)S(1)} fusion(bf16[128,64]{1,0:T(8,128)(2,1)} %bitcast.19, bf16[256,128]{1,0:T(8,128)(2,1)} %bitcast.18), kind=kLoop, calls=%fused_computation.5 | loop fusion | flops 294912 | bytes 180224 | tf_op jit(solution)/shard_map/concatenate | solution.py:478
  1.5 0.2 shard_map.67.i0
  1.7 3.0 %collective-permute-start = (bf16[320,128]{1,0:T(8,128)(2,1)S(1)}, bf16[320,128]{1,0:T(8,128)(2,1)S(1)}, u32[]{:S(2)}, u32[]{:S(2)}) collective-permute-start(bf16[320,128]{1,0:T(8,128)(2,1)S(1)} %shard_map.67.i0), channel_id=1, source_target_pairs={{0,2},{2,0},{4,6},{6,4},{8,10},{10,8},{12,14},{14,12},{16,18},{18,... | collective-permute-start | bytes 245768 | tf_op jit(solution)/shard_map/ppermute | solution.py:482
  4.8 1.5 %collective-permute-start.1 = (bf16[320,128]{1,0:T(8,128)(2,1)S(1)}, bf16[320,128]{1,0:T(8,128)(2,1)S(1)}, u32[]{:S(2)}, u32[]{:S(2)}) collective-permute-start(bf16[320,128]{1,0:T(8,128)(2,1)S(1)} %shard_map.67.i0), channel_id=1, source_target_pairs={{0,4},{2,6},{4,0},{6,2},{8,12},{10,14},{12,8},{14,10},{16,20},{18,... | collective-permute-start | bytes 245768 | tf_op jit(solution)/shard_map/ppermute | solution.py:482
  6.3 0.0 collective-permute-start.2
  6.3 1.2 %collective-permute-done.i1 = bf16[320,128]{1,0:T(8,128)(2,1)S(1)} collective-permute-done((bf16[320,128]{1,0:T(8,128)(2,1)S(1)}, bf16[320,128]{1,0:T(8,128)(2,1)S(1)}, u32[]{:S(2)}, u32[]{:S(2)}) %collective-permute-start) | collective-permute-done | bytes 81952 | tf_op jit(solution)/shard_map/ppermute | solution.py:482
  7.5 2.6 %collective-permute-done.1.i2 = bf16[320,128]{1,0:T(8,128)(2,1)S(1)} collective-permute-done((bf16[320,128]{1,0:T(8,128)(2,1)S(1)}, bf16[320,128]{1,0:T(8,128)(2,1)S(1)}, u32[]{:S(2)}, u32[]{:S(2)}) %collective-permute-start.1) | collective-permute-done | bytes 81952 | tf_op jit(solution)/shard_map/ppermute | solution.py:482
  10.1 1.5 %collective-permute-done.2.i3 = bf16[320,128]{1,0:T(8,128)(2,1)S(1)} collective-permute-done((bf16[320,128]{1,0:T(8,128)(2,1)S(1)}, bf16[320,128]{1,0:T(8,128)(2,1)S(1)}, u32[]{:S(2)}, u32[]{:S(2)}) %collective-permute-start.2) | collective-permute-done | bytes 81952 | tf_op jit(solution)/shard_map/ppermute | solution.py:482
  11.7 0.1 collective-permute-start.5
  11.7 1.1 %fusion.1.both = bf16[1728,64]{1,0:T(8,128)(2,1)S(1)} fusion(bf16[864,32]{1,0:T(8,128)(2,1)} %bitcast.15, bf16[864,64]{1,0:T(8,128)(2,1)} %bitcast.16), kind=kLoop, calls=%fused_computation.2 | loop fusion | flops 663552 | bytes 387072 | tf_op jit(solution)/shard_map/concatenate | solution.py:524
  12.9 1.6 %collective-permute-start.3 = (bf16[384,128]{1,0:T(8,128)(2,1)S(1)}, bf16[384,128]{1,0:T(8,128)(2,1)S(1)}, u32[]{:S(2)}, u32[]{:S(2)}) collective-permute-start(bf16[384,128]{1,0:T(8,128)(2,1)S(1)} %get-tuple-element.27), channel_id=1, source_target_pairs={{0,8},{2,10},{4,12},{6,14},{8,0},{10,2},{12,4},{14,6},{16,24},{18,... | collective-permute-start | bytes 294920 | tf_op jit(solution)/shard_map/ppermute | solution.py:499
  14.5 0.7 %collective-permute-start.4 = (bf16[384,128]{1,0:T(8,128)(2,1)S(1)}, bf16[384,128]{1,0:T(8,128)(2,1)S(1)}, u32[]{:S(2)}, u32[]{:S(2)}) collective-permute-start(bf16[384,128]{1,0:T(8,128)(2,1)S(1)} %get-tuple-element.28), channel_id=1, source_target_pairs={{0,0},{2,2},{4,4},{6,6},{8,16},{10,18},{12,20},{14,22},{16,8},{18,... | collective-permute-start | bytes 294920 | tf_op jit(solution)/shard_map/ppermute | solution.py:500
  15.2 1.1 %shard_map.69 = (bf16[3,768,256]{2,1,0:T(8,128)(2,1)S(1)}, bf16[3,768,128]{2,1,0:T(8,128)(2,1)S(1)}, bf16[3,384,256]{2,1,0:T(8,128)(2,1)S(1)}, bf16[3,768,256]{2,1,0:T(8,128)(2,1)S(1)}) custom-call(bf16[1728,64]{1,0:T(8,128)(2,1)S(1)} %fusion.1.both), custom_call_target="tpu_custom_call" | custom-call | flops 1073741824 | bytes 1048576 | tf_op jit(solution)/shard_map/pallas_call | solution.py:462
  16.3 1.9 %collective-permute-done.3.a = bf16[384,128]{1,0:T(8,128)(2,1)S(1)} collective-permute-done((bf16[384,128]{1,0:T(8,128)(2,1)S(1)}, bf16[384,128]{1,0:T(8,128)(2,1)S(1)}, u32[]{:S(2)}, u32[]{:S(2)}) %collective-permute-start.3) | collective-permute-done | bytes 98336 | tf_op jit(solution)/shard_map/ppermute | solution.py:499
  18.1 0.5 %collective-permute-start.7 = (bf16[384,128]{1,0:T(8,128)(2,1)S(1)}, bf16[384,128]{1,0:T(8,128)(2,1)S(1)}, u32[]{:S(2)}, u32[]{:S(2)}) collective-permute-start(bf16[384,128]{1,0:T(8,128)(2,1)S(1)} %collective-permute-done.4.b), channel_id=1, source_target_pairs={{0,1},{1,0},{2,3},{3,2},{4,5},{5,4},{6,7},{7,6},{8,9},{9,8},{10,11... | collective-permute-start | bytes 294920 | tf_op jit(solution)/shard_map/ppermute | solution.py:488
  18.7 1.4 %shard_map.70 = (bf16[14,128,384]{2,1,0:T(8,128)(2,1)S(1)}, bf16[14,128,384]{2,1,0:T(8,128)(2,1)S(1)}, f32[6,128,256]{2,1,0:T(8,128)S(1)}, f32[6,128,128]{2,1,0:...) custom-call(bf16[1280,128]{1,0:T(8,128)(2,1)S(1)} %get-tuple-element.29.mi, ...), custom_call_target="tpu_custom_call" | custom-call | flops 1073741824 | bytes 1048576 | tf_op jit(solution)/shard_map/pallas_call | solution.py:462
  20.1 4.2 %collective-permute-start.8 = (bf16[384,128]{1,0:T(8,128)(2,1)S(1)}, bf16[384,128]{1,0:T(8,128)(2,1)S(1)}, u32[]{:S(2)}, u32[]{:S(2)}) collective-permute-start(bf16[384,128]{1,0:T(8,128)(2,1)S(1)} %get-tuple-element.37.pooled), channel_id=1, source_target_pairs={{0,8},{2,10},{4,12},{6,14},{8,0},{10,2},{12,4},{14,6},{16,24},{18,... | collective-permute-start | bytes 294920 | tf_op jit(solution)/shard_map/ppermute | solution.py:499
  24.2 0.7 %collective-permute-start.9 = (bf16[384,128]{1,0:T(8,128)(2,1)S(1)}, bf16[384,128]{1,0:T(8,128)(2,1)S(1)}, u32[]{:S(2)}, u32[]{:S(2)}) collective-permute-start(bf16[384,128]{1,0:T(8,128)(2,1)S(1)} %get-tuple-element.38), channel_id=1, source_target_pairs={{0,0},{2,2},{4,4},{6,6},{8,16},{10,18},{12,20},{14,22},{16,8},{18,... | collective-permute-start | bytes 294920 | tf_op jit(solution)/shard_map/ppermute | solution.py:500
  24.9 0.7 %shard_map.71 = (bf16[14,128,384]{2,1,0:T(8,128)(2,1)S(1)}, f32[768,256]{1,0:T(8,128)S(1)}) custom-call(bf16[384,128]{1,0:T(8,128)(2,1)S(1)} %collective-permute-done.3.a, bf16[384,128]{1,0:T(8,128)(2,1)S(1)} %collective-permute-done.4.b, bf16[14,128,384]{2,1,0:T(8,128)(2,1)S(1)} %get-tuple-element.31.xs_in, ...), custom_call_target="tpu_custom_call", output_to_operand_aliasing={{0}: (2, {})} | custom-call | flops 1073741824 | bytes 1048576 | tf_op jit(solution)/shard_map/pallas_call | solution.py:462
  25.6 1.0 %shard_map.72 = (bf16[14,128,384]{2,1,0:T(8,128)(2,1)S(1)}, f32[6,128,256]{2,1,0:T(8,128)S(1)}, f32[6,128,128]{2,1,0:T(8,128)S(1)}) custom-call(bf16[384,128]{1,0:T(8,128)(2,1)S(1)} %collective-permute-done.6.a, bf16[384,128]{1,0:T(8,128)(2,1)S(1)} %collective-permute-done.7.b, ...), custom_call_target="tpu_custom_call", output_to_operand_aliasing={{0}: (2, {})} | custom-call | flops 1073741824 | bytes 1048576 | tf_op jit(solution)/shard_map/pallas_call | solution.py:462
  26.7 1.2 %shard_map.73 = (bf16[6,64,384]{2,1,0:T(8,128)(2,1)S(1)}, bf16[4,64,768]{2,1,0:T(8,128)(2,1)S(1)}, bf16[224,128]{1,0:T(8,128)(2,1)S(1)}) custom-call(bf16[1280,128]{1,0:T(8,128)(2,1)S(1)} %get-tuple-element.29.mi, bf16[1280,128]{1,0:T(8,128)(2,1)S(1)} %collective-permute-done.5.mi_x, bf16[384,128]{1,0:T(8,128)(2,1)S(1)} %get-tuple-element.37.pooled, ...), custom_call_target="tpu_custom_call" | custom-call | flops 1073741824 | bytes 1048576 | tf_op jit(solution)/shard_map/pallas_call | solution.py:462
  27.9 3.0 %collective-permute-start.10 = (bf16[224,128]{1,0:T(8,128)(2,1)S(1)}, bf16[224,128]{1,0:T(8,128)(2,1)S(1)}, u32[]{:S(2)}, u32[]{:S(2)}) collective-permute-start(bf16[224,128]{1,0:T(8,128)(2,1)S(1)} %get-tuple-element.47.refs_0_), channel_id=1, source_target_pairs={{0,8},{2,10},{4,12},{6,14},{8,0},{10,2},{12,4},{14,6},{16,24},{18,... | collective-permute-start | bytes 172040 | tf_op jit(solution)/shard_map/ppermute | solution.py:482
  30.9 0.2 collective-permute-start.11
  31.1 2.2 %collective-permute-start.12 = (bf16[224,128]{1,0:T(8,128)(2,1)S(1)}, bf16[224,128]{1,0:T(8,128)(2,1)S(1)}, u32[]{:S(2)}, u32[]{:S(2)}) collective-permute-start(bf16[224,128]{1,0:T(8,128)(2,1)S(1)} %get-tuple-element.47.refs_0_), channel_id=1, source_target_pairs={{0,24},{2,26},{4,28},{6,30},{8,16},{10,18},{12,20},{14,22},{16,8},... | collective-permute-start | bytes 172040 | tf_op jit(solution)/shard_map/ppermute | solution.py:482
  33.4 2.7 %shard_map.74 = (bf16[4,128,256]{2,1,0:T(8,128)(2,1)S(1)}, bf16[128,128]{1,0:T(8,128)(2,1)S(1)}) custom-call(bf16[14,128,384]{2,1,0:T(8,128)(2,1)S(1)} %get-tuple-element.32.xs, f32[6,128,256]{2,1,0:T(8,128)S(1)} %get-tuple-element.33.slopes_mid, f32[6,128,256]{2,1,0:T(8,128)S(1)} %get-tuple-element.36.slopes_out, ...), custom_call_target="tpu_custom_call" | custom-call | flops 4294967296 | bytes 1048576 | tf_op jit(solution)/shard_map/pallas_call | solution.py:462
  36.1 1.1 %collective-permute-start.13 = (bf16[128,128]{1,0:T(8,128)(2,1)S(1)}, bf16[128,128]{1,0:T(8,128)(2,1)S(1)}, u32[]{:S(2)}, u32[]{:S(2)}) collective-permute-start(bf16[128,128]{1,0:T(8,128)(2,1)S(1)} %get-tuple-element.49.refs_0_), channel_id=1, source_target_pairs={{0,8},{2,10},{4,12},{6,14},{8,0},{10,2},{12,4},{14,6},{16,24},{18,... | collective-permute-start | bytes 98312 | tf_op jit(solution)/shard_map/ppermute | solution.py:482
  37.2 1.1 %collective-permute-start.14 = (bf16[128,128]{1,0:T(8,128)(2,1)S(1)}, bf16[128,128]{1,0:T(8,128)(2,1)S(1)}, u32[]{:S(2)}, u32[]{:S(2)}) collective-permute-start(bf16[128,128]{1,0:T(8,128)(2,1)S(1)} %get-tuple-element.49.refs_0_), channel_id=1, source_target_pairs={{0,16},{2,18},{4,20},{6,22},{8,24},{10,26},{12,28},{14,30},{16,0},... | collective-permute-start | bytes 98312 | tf_op jit(solution)/shard_map/ppermute | solution.py:482
  38.3 2.2 %collective-permute-start.15 = (bf16[128,128]{1,0:T(8,128)(2,1)S(1)}, bf16[128,128]{1,0:T(8,128)(2,1)S(1)}, u32[]{:S(2)}, u32[]{:S(2)}) collective-permute-start(bf16[128,128]{1,0:T(8,128)(2,1)S(1)} %get-tuple-element.49.refs_0_), channel_id=1, source_target_pairs={{0,24},{2,26},{4,28},{6,30},{8,16},{10,18},{12,20},{14,22},{16,8},... | collective-permute-start | bytes 98312 | tf_op jit(solution)/shard_map/ppermute | solution.py:482
  40.6 1.3 %shard_map.75 = (bf16[256,128]{1,0:T(8,128)(2,1)}, f32[432,64]{1,0:T(8,128)}) custom-call(bf16[4,128,256]{2,1,0:T(8,128)(2,1)S(1)} %get-tuple-element.45.g1, bf16[3,768,128]{2,1,0:T(8,128)(2,1)S(1)} %get-tuple-element.46.b1, bf16[224,128]{1,0:T(8,128)(2,1)S(1)} %get-tuple-element.47.refs_0_, bf16[224,128]{1,0:T(8,128)(2,1)S(1)} %collective-permute-done.10.refs_1_, ...), custom_call_target="tpu_custom_call" | custom-call | flops 1073741824 | bytes 1048576 | tf_op jit(solution)/shard_map/pallas_call | solution.py:462
  41.9 0.8 %collective-permute-done.14.refs_2_ = bf16[128,128]{1,0:T(8,128)(2,1)S(1)} collective-permute-done((bf16[128,128]{1,0:T(8,128)(2,1)S(1)}, bf16[128,128]{1,0:T(8,128)(2,1)S(1)}, u32[]{:S(2)}, u32[]{:S(2)}) %collective-permute-start.14) | collective-permute-done | bytes 32800 | tf_op jit(solution)/shard_map/ppermute | solution.py:482
  42.7 1.4 %collective-permute-done.15.refs_3_ = bf16[128,128]{1,0:T(8,128)(2,1)S(1)} collective-permute-done((bf16[128,128]{1,0:T(8,128)(2,1)S(1)}, bf16[128,128]{1,0:T(8,128)(2,1)S(1)}, u32[]{:S(2)}, u32[]{:S(2)}) %collective-permute-start.15) | collective-permute-done | bytes 32800 | tf_op jit(solution)/shard_map/ppermute | solution.py:482
  44.0 0.8 %shard_map.76 = f32[432,32]{1,0:T(8,128)} custom-call(bf16[128,128]{1,0:T(8,128)(2,1)S(1)} %get-tuple-element.49.refs_0_, bf16[128,128]{1,0:T(8,128)(2,1)S(1)} %collective-permute-done.13.refs_1_, bf16[128,128]{1,0:T(8,128)(2,1)S(1)} %collective-permute-done.14.refs_2_, bf16[128,128]{1,0:T(8,128)(2,1)S(1)} %collective-permute-done.15.refs_3_), custom_call_target="tpu_custom_call" | custom-call | bytes 1048576 | tf_op jit(solution)/shard_map/pallas_call | solution.py:462
  (12 shorter events, 0.1 us)
Async XLA Ops:
  1.7 5.7 %collective-permute-start = (bf16[320,128]{1,0:T(8,128)(2,1)S(1)}, bf16[320,128]{1,0:T(8,128)(2,1)S(1)}, u32[]{:S(2)}, u32[]{:S(2)}) collective-permute-start(bf16[320,128]{1,0:T(8,128)(2,1)S(1)} %shard_map.67.i0), channel_id=1, source_target_pairs={{0,2},{2,0},{4,6},{6,4},{8,10},{10,8},{12,14},{14,12},{16,18},{18,... | collective-permute-start | bytes 245768 | tf_op jit(solution)/shard_map/ppermute | solution.py:482
  4.8 5.3 %collective-permute-start.1 = (bf16[320,128]{1,0:T(8,128)(2,1)S(1)}, bf16[320,128]{1,0:T(8,128)(2,1)S(1)}, u32[]{:S(2)}, u32[]{:S(2)}) collective-permute-start(bf16[320,128]{1,0:T(8,128)(2,1)S(1)} %shard_map.67.i0), channel_id=1, source_target_pairs={{0,4},{2,6},{4,0},{6,2},{8,12},{10,14},{12,8},{14,10},{16,20},{18,... | collective-permute-start | bytes 245768 | tf_op jit(solution)/shard_map/ppermute | solution.py:482
  6.3 5.3 %collective-permute-start.2 = (bf16[320,128]{1,0:T(8,128)(2,1)S(1)}, bf16[320,128]{1,0:T(8,128)(2,1)S(1)}, u32[]{:S(2)}, u32[]{:S(2)}) collective-permute-start(bf16[320,128]{1,0:T(8,128)(2,1)S(1)} %shard_map.67.i0), channel_id=1, source_target_pairs={{0,6},{2,4},{4,2},{6,0},{8,14},{10,12},{12,10},{14,8},{16,22},{18,... | collective-permute-start | bytes 245768 | tf_op jit(solution)/shard_map/ppermute | solution.py:482
  11.7 7.0 %collective-permute-start.5 = (bf16[1280,128]{1,0:T(8,128)(2,1)S(1)}, bf16[1280,128]{1,0:T(8,128)(2,1)S(1)}, u32[]{:S(2)}, u32[]{:S(2)}) collective-permute-start(bf16[1280,128]{1,0:T(8,128)(2,1)S(1)} %get-tuple-element.29.mi), channel_id=1, source_target_pairs={{0,1},{1,0},{2,3},{3,2},{4,5},{5,4},{6,7},{7,6},{8,9},{9,8},{10,11... | collective-permute-start | bytes 983048 | tf_op jit(solution)/shard_map/ppermute | solution.py:488
  12.9 5.3 %collective-permute-start.3 = (bf16[384,128]{1,0:T(8,128)(2,1)S(1)}, bf16[384,128]{1,0:T(8,128)(2,1)S(1)}, u32[]{:S(2)}, u32[]{:S(2)}) collective-permute-start(bf16[384,128]{1,0:T(8,128)(2,1)S(1)} %get-tuple-element.27), channel_id=1, source_target_pairs={{0,8},{2,10},{4,12},{6,14},{8,0},{10,2},{12,4},{14,6},{16,24},{18,... | collective-permute-start | bytes 294920 | tf_op jit(solution)/shard_map/ppermute | solution.py:499
  14.5 3.6 %collective-permute-start.4 = (bf16[384,128]{1,0:T(8,128)(2,1)S(1)}, bf16[384,128]{1,0:T(8,128)(2,1)S(1)}, u32[]{:S(2)}, u32[]{:S(2)}) collective-permute-start(bf16[384,128]{1,0:T(8,128)(2,1)S(1)} %get-tuple-element.28), channel_id=1, source_target_pairs={{0,0},{2,2},{4,4},{6,6},{8,16},{10,18},{12,20},{14,22},{16,8},{18,... | collective-permute-start | bytes 294920 | tf_op jit(solution)/shard_map/ppermute | solution.py:500
  18.1 7.5 %collective-permute-start.6 = (bf16[384,128]{1,0:T(8,128)(2,1)S(1)}, bf16[384,128]{1,0:T(8,128)(2,1)S(1)}, u32[]{:S(2)}, u32[]{:S(2)}) collective-permute-start(bf16[384,128]{1,0:T(8,128)(2,1)S(1)} %collective-permute-done.3.a), channel_id=1, source_target_pairs={{0,1},{1,0},{2,3},{3,2},{4,5},{5,4},{6,7},{7,6},{8,9},{9,8},{10,11... | collective-permute-start | bytes 294920 | tf_op jit(solution)/shard_map/ppermute | solution.py:488
  18.1 7.5 %collective-permute-start.7 = (bf16[384,128]{1,0:T(8,128)(2,1)S(1)}, bf16[384,128]{1,0:T(8,128)(2,1)S(1)}, u32[]{:S(2)}, u32[]{:S(2)}) collective-permute-start(bf16[384,128]{1,0:T(8,128)(2,1)S(1)} %collective-permute-done.4.b), channel_id=1, source_target_pairs={{0,1},{1,0},{2,3},{3,2},{4,5},{5,4},{6,7},{7,6},{8,9},{9,8},{10,11... | collective-permute-start | bytes 294920 | tf_op jit(solution)/shard_map/ppermute | solution.py:488
  20.1 13.3 %collective-permute-start.8 = (bf16[384,128]{1,0:T(8,128)(2,1)S(1)}, bf16[384,128]{1,0:T(8,128)(2,1)S(1)}, u32[]{:S(2)}, u32[]{:S(2)}) collective-permute-start(bf16[384,128]{1,0:T(8,128)(2,1)S(1)} %get-tuple-element.37.pooled), channel_id=1, source_target_pairs={{0,8},{2,10},{4,12},{6,14},{8,0},{10,2},{12,4},{14,6},{16,24},{18,... | collective-permute-start | bytes 294920 | tf_op jit(solution)/shard_map/ppermute | solution.py:499
  24.2 9.1 %collective-permute-start.9 = (bf16[384,128]{1,0:T(8,128)(2,1)S(1)}, bf16[384,128]{1,0:T(8,128)(2,1)S(1)}, u32[]{:S(2)}, u32[]{:S(2)}) collective-permute-start(bf16[384,128]{1,0:T(8,128)(2,1)S(1)} %get-tuple-element.38), channel_id=1, source_target_pairs={{0,0},{2,2},{4,4},{6,6},{8,16},{10,18},{12,20},{14,22},{16,8},{18,... | collective-permute-start | bytes 294920 | tf_op jit(solution)/shard_map/ppermute | solution.py:500
  27.9 10.4 %collective-permute-start.10 = (bf16[224,128]{1,0:T(8,128)(2,1)S(1)}, bf16[224,128]{1,0:T(8,128)(2,1)S(1)}, u32[]{:S(2)}, u32[]{:S(2)}) collective-permute-start(bf16[224,128]{1,0:T(8,128)(2,1)S(1)} %get-tuple-element.47.refs_0_), channel_id=1, source_target_pairs={{0,8},{2,10},{4,12},{6,14},{8,0},{10,2},{12,4},{14,6},{16,24},{18,... | collective-permute-start | bytes 172040 | tf_op jit(solution)/shard_map/ppermute | solution.py:482
  30.9 9.6 %collective-permute-start.11 = (bf16[224,128]{1,0:T(8,128)(2,1)S(1)}, bf16[224,128]{1,0:T(8,128)(2,1)S(1)}, u32[]{:S(2)}, u32[]{:S(2)}) collective-permute-start(bf16[224,128]{1,0:T(8,128)(2,1)S(1)} %get-tuple-element.47.refs_0_), channel_id=1, source_target_pairs={{0,16},{2,18},{4,20},{6,22},{8,24},{10,26},{12,28},{14,30},{16,0},... | collective-permute-start | bytes 172040 | tf_op jit(solution)/shard_map/ppermute | solution.py:482
  31.1 9.4 %collective-permute-start.12 = (bf16[224,128]{1,0:T(8,128)(2,1)S(1)}, bf16[224,128]{1,0:T(8,128)(2,1)S(1)}, u32[]{:S(2)}, u32[]{:S(2)}) collective-permute-start(bf16[224,128]{1,0:T(8,128)(2,1)S(1)} %get-tuple-element.47.refs_0_), channel_id=1, source_target_pairs={{0,24},{2,26},{4,28},{6,30},{8,16},{10,18},{12,20},{14,22},{16,8},... | collective-permute-start | bytes 172040 | tf_op jit(solution)/shard_map/ppermute | solution.py:482
  36.1 5.8 %collective-permute-start.13 = (bf16[128,128]{1,0:T(8,128)(2,1)S(1)}, bf16[128,128]{1,0:T(8,128)(2,1)S(1)}, u32[]{:S(2)}, u32[]{:S(2)}) collective-permute-start(bf16[128,128]{1,0:T(8,128)(2,1)S(1)} %get-tuple-element.49.refs_0_), channel_id=1, source_target_pairs={{0,8},{2,10},{4,12},{6,14},{8,0},{10,2},{12,4},{14,6},{16,24},{18,... | collective-permute-start | bytes 98312 | tf_op jit(solution)/shard_map/ppermute | solution.py:482
  37.2 5.5 %collective-permute-start.14 = (bf16[128,128]{1,0:T(8,128)(2,1)S(1)}, bf16[128,128]{1,0:T(8,128)(2,1)S(1)}, u32[]{:S(2)}, u32[]{:S(2)}) collective-permute-start(bf16[128,128]{1,0:T(8,128)(2,1)S(1)} %get-tuple-element.49.refs_0_), channel_id=1, source_target_pairs={{0,16},{2,18},{4,20},{6,22},{8,24},{10,26},{12,28},{14,30},{16,0},... | collective-permute-start | bytes 98312 | tf_op jit(solution)/shard_map/ppermute | solution.py:482
  38.3 5.7 %collective-permute-start.15 = (bf16[128,128]{1,0:T(8,128)(2,1)S(1)}, bf16[128,128]{1,0:T(8,128)(2,1)S(1)}, u32[]{:S(2)}, u32[]{:S(2)}) collective-permute-start(bf16[128,128]{1,0:T(8,128)(2,1)S(1)} %get-tuple-element.49.refs_0_), channel_id=1, source_target_pairs={{0,24},{2,26},{4,28},{6,30},{8,16},{10,18},{12,20},{14,22},{16,8},... | collective-permute-start | bytes 98312 | tf_op jit(solution)/shard_map/ppermute | solution.py:482
